TPU v7x, 128 devices: a whole 4x4x4 slice. The times are simulated.
128 devices in a mesh: fsdp: 32 (over z, y, x_hi), sp: 4 (over x_lo, core).
Axes of the slice: x: 4 (x_hi: 2, x_lo: 2; x = x_hi * 2 + x_lo), y: 4, z: 4, core: 2. Of those that a mesh axis runs over, the one named last changes fastest.
Arguments:
- tokens: bfloat16 [32, 512, 1536], P('fsdp', 'sp'), may hold values from -6 to 6
- modulation: float32 [32, 1, 6, 1536], P('fsdp'), may hold values from -4 to 4
- w_qkv: bfloat16 [1, 1536, 3, 1536], P(None, 'fsdp', None, 'sp'), may hold values from -0.15625 to 0.15625
- w_out: bfloat16 [1, 1536, 1536], P(None, 'sp', 'fsdp'), may hold values from -0.15625 to 0.15625
- w_in: bfloat16 [1, 1536, 6144], P(None, 'fsdp', 'sp'), may hold values from -0.15625 to 0.15625
- w_back: bfloat16 [1, 6144, 1536], P(None, 'sp', 'fsdp'), may hold values from -0.078125 to 0.078125
- out_grad: bfloat16 [32, 512, 1536], P('fsdp', 'sp'), may hold values from -6 to 6
Outputs:
- final_out: bfloat16 [32, 512, 1536], P('fsdp', 'sp')
- input_grad: float32 [32, 512, 1536], P('fsdp', 'sp')
- grad_qkv: float32 [1, 1536, 3, 1536], P(None, 'fsdp', None, 'sp')
- grad_out: float32 [1, 1536, 1536], P(None, 'sp', 'fsdp')
- grad_in: float32 [1, 1536, 6144], P(None, 'fsdp', 'sp')
- grad_back: float32 [1, 6144, 1536], P(None, 'sp', 'fsdp')
All inputs are finite; a program needn't handle non-finite values.
Results may differ from a plain program's by a relative error of at most 0.03.
Values may be sent and summed in bfloat16 or wider, within the bound.
A program may use at most 128 MiB of HBM per device.

v0:
```python
import math

import jax
import jax.numpy as jnp
from jax import lax
from jax.sharding import Mesh
from jax.sharding import PartitionSpec as P

HEAD_DIM = 128
SP = ("sp_0", "sp_1")


ln_eps = 1e-06
temper = 2.5
block_limit = 512


def laid_out(blocks, dim):
    blocks = jnp.moveaxis(blocks, 0, dim)
    lengths = blocks.shape
    return blocks.reshape(*lengths[:dim], lengths[dim] * lengths[dim + 1], *lengths[dim + 2 :])


def one_gather(arrays, axis, dims):
    ravelled = jnp.concatenate([a.reshape(-1) for a in arrays])
    lines, at, gathered = lax.all_gather(ravelled, axis), 0, []
    for a, dim in zip(arrays, dims):
        blocks = lines[:, at : at + a.size].reshape(-1, *a.shape)
        gathered.append(laid_out(blocks, dim))
        at += a.size
    return tuple(gathered)


def own_block(blocks, axes, turns):
    inside = blocks.shape[1:]
    blocks = blocks.reshape(*(lax.axis_size(a) for a in axes), *inside)
    blocks = jnp.moveaxis(blocks, turns, range(len(axes))).reshape(-1, *inside)
    for k in turns:
        blocks = lax.psum_scatter(blocks, axes[k], scatter_dimension=0, tiled=True)
    return blocks[0]


def cut_along(value, dim, count):
    return jnp.stack(jnp.split(value, count, axis=dim))


def sum_by_axis(value, axes, turns, dim):
    count = lax.axis_size(axes)
    return own_block(cut_along(value, dim, count), axes, turns)


def sum_packed(arrays, axis, dims):
    count = lax.axis_size(axis)
    blocks = [cut_along(a, dim, count) for a, dim in zip(arrays, dims)]
    lines = jnp.concatenate([b.reshape(count, -1) for b in blocks], axis=1)
    ravelled, at, gathered = lax.psum_scatter(lines, axis, tiled=True)[0], 0, []
    for b in blocks:
        part = b[0]
        gathered.append(ravelled[at : at + part.size].reshape(part.shape))
        at += part.size
    return tuple(gathered)


def normalize(stream):
    mean_part = jnp.mean(stream, axis=-1, keepdims=True)
    centred = stream - mean_part
    rstd = lax.rsqrt(jnp.mean(centred * centred, axis=-1, keepdims=True) + ln_eps)
    return (centred * rstd, rstd)


def norm_back(normed, rstd, incoming):
    first = jnp.mean(incoming, axis=-1, keepdims=True)
    second = jnp.mean(incoming * normed, axis=-1, keepdims=True)
    return rstd * (incoming - first - normed * second)


def gelu_tanh(hidden):
    return jax.nn.gelu(hidden, approximate=True)


def project(left, weight):
    flat_rows = left.reshape(-1, left.shape[-1])
    result = jnp.dot(flat_rows, weight, preferred_element_type=jnp.float32)
    return result.reshape(left.shape[:-1] + (weight.shape[1],))


def project_back(left, weight):
    flat_rows = left.reshape(-1, left.shape[-1])
    result = lax.dot_general(
        flat_rows, weight, (((1,), (1,)), ((), ())), preferred_element_type=jnp.float32
    )
    return result.reshape(left.shape[:-1] + (weight.shape[0],))


def weight_term(left, right, grad_scale):
    left_rows = left.reshape(-1, left.shape[-1])
    right_rows = right.reshape(-1, right.shape[-1])

    def term_rows(start, count):
        column_part = lax.dynamic_slice_in_dim(left_rows, start, count, 1)
        product = lax.dot_general(
            column_part, right_rows, (((0,), (0,)), ((), ())), preferred_element_type=jnp.float32
        )
        return product * grad_scale

    return term_rows


def split_heads(packed, head_count):
    return packed.reshape(packed.shape[:-1] + (head_count, packed.shape[-1] // head_count))


def heads_major(tensor):
    videos, seq_len, head_count, head_width = tensor.shape
    return tensor.transpose(0, 2, 1, 3).reshape(videos * head_count, seq_len, head_width)


def heads_minor(tensor, videos):
    merged, seq_len, head_width = tensor.shape
    return tensor.reshape(videos, merged // videos, seq_len, head_width).transpose(0, 2, 1, 3)


def attend_head(triple):
    queries, key_rows, values = triple
    seq_len, head_width = queries.shape
    block_size = min(block_limit, seq_len)
    score_factor = temper / math.sqrt(head_width)
    values_wide = values.astype(jnp.float32)

    def one_block(query_rows):
        scores = jnp.dot(query_rows, key_rows.T, preferred_element_type=jnp.float32) * score_factor
        softmaxed = jax.nn.softmax(scores, axis=-1)
        return jnp.dot(softmaxed, values_wide, precision=lax.Precision.DEFAULT).astype(jnp.bfloat16)

    attended = lax.map(one_block, queries.reshape(seq_len // block_size, block_size, head_width))
    return attended.reshape(seq_len, head_width)


def attend_back(quadruple):
    queries, key_rows, values, upstream = quadruple
    seq_len, head_width = queries.shape
    block_size = min(block_limit, seq_len)
    score_factor = temper / math.sqrt(head_width)
    keys_wide = key_rows.astype(jnp.float32)

    def one_block(running, block_pair):
        query_rows, grad_rows = block_pair
        scores = jnp.dot(query_rows, key_rows.T, preferred_element_type=jnp.float32) * score_factor
        softmaxed = jax.nn.softmax(scores, axis=-1)
        dprobs = jnp.dot(grad_rows, values.T, preferred_element_type=jnp.float32)
        dscores = (
            softmaxed
            * (dprobs - jnp.sum(softmaxed * dprobs, axis=-1, keepdims=True))
            * score_factor
        )
        dquery = jnp.dot(dscores, keys_wide, precision=lax.Precision.DEFAULT)
        grad_keys = running[0] + jnp.dot(
            dscores.T, query_rows.astype(jnp.float32), precision=lax.Precision.DEFAULT
        )
        dvalues = running[1] + jnp.dot(
            softmaxed.T, grad_rows.astype(jnp.float32), precision=lax.Precision.DEFAULT
        )
        return ((grad_keys, dvalues), dquery)

    zero_rows = jnp.zeros((seq_len, head_width), jnp.float32)
    count = seq_len // block_size
    blocks = (
        queries.reshape(count, block_size, head_width),
        upstream.reshape(count, block_size, head_width),
    )
    (grad_keys, dvalues), dquery = lax.scan(one_block, (zero_rows, zero_rows), blocks)
    return (
        dquery.reshape(seq_len, head_width).astype(jnp.bfloat16),
        grad_keys.astype(jnp.bfloat16),
        dvalues.astype(jnp.bfloat16),
    )


def attend_all(queries, key_rows, values):
    attended = lax.map(
        attend_head, (heads_major(queries), heads_major(key_rows), heads_major(values))
    )
    return heads_minor(attended, queries.shape[0])


def attend_all_back(queries, key_rows, values, upstream):
    grad_heads = lax.map(
        attend_back,
        (heads_major(queries), heads_major(key_rows), heads_major(values), heads_major(upstream)),
    )
    return tuple((heads_minor(grad_piece, queries.shape[0]) for grad_piece in grad_heads))


def body(tokens, modulation, w_qkv, w_out, w_in, w_back, out_grad):
    videos, local_seq, model_width = tokens.shape
    layers = w_qkv.shape[0]
    own_width = w_qkv.shape[3]
    own_heads = own_width // HEAD_DIM
    grad_scale = 1.0 / math.sqrt(videos * local_seq * lax.axis_size("fsdp") * lax.axis_size(SP))
    stream = tokens.astype(jnp.float32)
    stored = []
    fetched = []
    for layer_index in range(layers):
        weights = one_gather(
            (w_qkv[layer_index], w_out[layer_index], w_in[layer_index], w_back[layer_index]),
            "fsdp",
            (0, 1, 0, 1),
        )
        fetched.append(weights)
        whole_qkv, whole_out, whole_in, whole_back = weights
        joint = whole_qkv.reshape(model_width, 3 * own_width)
        layer_mod = modulation[:, layer_index][:, :, None, :]
        normed_first, rstd_first = normalize(stream)
        input_first = (normed_first * (1.0 + layer_mod[:, 1]) + layer_mod[:, 0]).astype(
            jnp.bfloat16
        )
        first_rows = lax.all_gather(input_first, SP, axis=1, tiled=True)
        packed = project(first_rows, joint).astype(jnp.bfloat16)
        queries = split_heads(packed[..., :own_width], own_heads)
        key_rows = split_heads(packed[..., own_width : 2 * own_width], own_heads)
        values = split_heads(packed[..., 2 * own_width :], own_heads)
        attended = attend_all(queries, key_rows, values).reshape(videos, -1, own_width)
        attn_part = sum_by_axis(
            project(attended, whole_out).astype(jnp.bfloat16), SP, (1, 0), 1
        ).astype(jnp.float32)
        middle = stream + layer_mod[:, 2] * attn_part
        normed_second, rstd_second = normalize(middle)
        input_second = (normed_second * (1.0 + layer_mod[:, 4]) + layer_mod[:, 3]).astype(
            jnp.bfloat16
        )
        second_rows = lax.all_gather(input_second, SP, axis=1, tiled=True)
        hidden = project(second_rows, whole_in)
        activated = gelu_tanh(hidden).astype(jnp.bfloat16)
        ffn_part = sum_by_axis(
            project(activated, whole_back).astype(jnp.bfloat16), SP, (1, 0), 1
        ).astype(jnp.float32)
        stream = middle + layer_mod[:, 5] * ffn_part
        stored.append(
            (
                normed_first,
                rstd_first,
                first_rows,
                queries,
                key_rows,
                values,
                attended,
                normed_second,
                rstd_second,
                second_rows,
                hidden,
                activated,
            )
        )
    final_out = stream.astype(jnp.bfloat16)
    stream_grad = out_grad.astype(jnp.float32)
    results = [None] * layers
    for layer_index in range(layers - 1, -1, -1):
        (
            normed_first,
            rstd_first,
            first_rows,
            queries,
            key_rows,
            values,
            attended,
            normed_second,
            rstd_second,
            second_rows,
            hidden,
            activated,
        ) = stored[layer_index]
        whole_qkv, whole_out, whole_in, whole_back = fetched[layer_index]
        joint = whole_qkv.reshape(model_width, 3 * own_width)
        layer_mod = modulation[:, layer_index][:, :, None, :]
        down_grad = (layer_mod[:, 5] * stream_grad).astype(jnp.bfloat16)
        down_rows = lax.all_gather(down_grad, SP, axis=1, tiled=True)
        back_hidden = project_back(down_rows, whole_back)
        unused, pullback = jax.vjp(gelu_tanh, hidden)
        up_grad = pullback(back_hidden)[0].astype(jnp.bfloat16)
        back_second = sum_by_axis(
            project_back(up_grad, whole_in).astype(jnp.bfloat16), SP, (1, 0), 1
        ).astype(jnp.float32)
        stream_grad = stream_grad + norm_back(
            normed_second, rstd_second, back_second * (1.0 + layer_mod[:, 4])
        )
        attn_grad = (layer_mod[:, 2] * stream_grad).astype(jnp.bfloat16)
        attn_rows = lax.all_gather(attn_grad, SP, axis=1, tiled=True)
        mixed_grad = split_heads(project_back(attn_rows, whole_out).astype(jnp.bfloat16), own_heads)
        grad_query, grad_keys, grad_values = attend_all_back(queries, key_rows, values, mixed_grad)
        packed_grad = jnp.concatenate(
            [
                grad_query.reshape(videos, -1, own_width),
                grad_keys.reshape(videos, -1, own_width),
                grad_values.reshape(videos, -1, own_width),
            ],
            axis=-1,
        )
        back_first = lax.psum_scatter(
            project_back(packed_grad, joint).astype(jnp.bfloat16),
            SP,
            scatter_dimension=1,
            tiled=True,
        ).astype(jnp.float32)
        stream_grad = stream_grad + norm_back(
            normed_first, rstd_first, back_first * (1.0 + layer_mod[:, 1])
        )
        term_qkv = weight_term(first_rows, packed_grad, grad_scale)
        term_out = weight_term(attn_rows, attended, grad_scale)
        term_in = weight_term(second_rows, up_grad, grad_scale)
        term_back = weight_term(down_rows, activated, grad_scale)
        full_terms = (
            term_qkv(0, model_width),
            term_out(0, model_width),
            term_in(0, model_width),
            term_back(0, model_width),
        )
        sum_qkv, sum_out, sum_in, sum_back = tuple(
            (
                part.astype(jnp.float32)
                for part in sum_packed(
                    (
                        full_terms[0].astype(jnp.bfloat16),
                        full_terms[1].astype(jnp.bfloat16),
                        full_terms[2].astype(jnp.bfloat16),
                        full_terms[3].astype(jnp.bfloat16),
                    ),
                    "fsdp",
                    (0, 0, 0, 0),
                )
            )
        )
        results[layer_index] = (
            sum_qkv.reshape(sum_qkv.shape[0], 3, own_width),
            sum_out.T,
            sum_in,
            sum_back.T,
        )
    grad_qkv = jnp.stack([results[index][0] for index in range(layers)])
    grad_out = jnp.stack([results[index][1] for index in range(layers)])
    grad_in = jnp.stack([results[index][2] for index in range(layers)])
    grad_back = jnp.stack([results[index][3] for index in range(layers)])
    return (final_out, stream_grad, grad_qkv, grad_out, grad_in, grad_back)


def solution(mesh):
    torus = Mesh(mesh.devices.reshape(mesh.shape["fsdp"], 2, 2), ("fsdp", "sp_0", "sp_1"))
    return jax.shard_map(
        body,
        mesh=torus,
        in_specs=(
            P("fsdp", SP, None),
            P("fsdp", None, None, None),
            P(None, "fsdp", None, SP),
            P(None, SP, "fsdp"),
            P(None, "fsdp", SP),
            P(None, SP, "fsdp"),
            P("fsdp", SP, None),
        ),
        out_specs=(
            P("fsdp", SP, None),
            P("fsdp", SP, None),
            P(None, "fsdp", None, SP),
            P(None, SP, "fsdp"),
            P(None, "fsdp", SP),
            P(None, SP, "fsdp"),
        ),
        check_vma=False,
    )
```

profile of v0, /device:TPU:0, one launch (start us, length us, event | category | flops | bytes accessed | tf_op | source)
XLA Modules:
  0.0 1303.5 jit_solution(8247963021903286426)
XLA Ops:
  15.2 139.5 %all-gather.15.cloned.1.call-done = bf16[7077888]{0:T(1024)(128)(2,1)} async-done(((bf16[221184]{0:T(1024)(128)(2,1)}), bf16[7077888]{0:T(1024)(128)(2,1)}) %all-gather.15.cloned.1.call-update) | async-done | bytes 14155792 | tf_op jit(solution)/shard_map/all_gather | solution.py:26
  154.7 12.9 reshape.778
  172.7 6.6 all-gather.7.cloned.1.call-done
  197.8 13.1 %reduce-scatter.8.cloned.1.call-done = bf16[2,1,128,1536]{3,2,1,0:T(8,128)(2,1)} async-done(((bf16[4,1,128,1536]{3,2,1,0:T(8,128)(2,1)}), bf16[2,1,128,1536]{3,2,1,0:T(8,128)(2,1)}) %reduce-scatter.8.cloned.1.call-update) | async-done | bytes 786448 | tf_op jit(solution)/shard_map/reduce_scatter | solution.py:39
  211.0 23.5 %reduce-scatter.10.cloned.1.call-done = bf16[1,1,128,1536]{3,2,1,0:T(8,128)(2,1)} async-done(((bf16[2,1,128,1536]{3,2,1,0:T(8,128)(2,1)}), bf16[1,1,128,1536]{3,2,1,0:T(8,128)(2,1)}) %reduce-scatter.10.cloned.1.call-update) | async-done | bytes 393232 | tf_op jit(solution)/shard_map/reduce_scatter | solution.py:39
  240.1 8.1 fusion.111
  248.2 6.0 reshape_reshape.8
  254.2 15.1 %reshape.753 = bf16[32,1536,48]{2,1,0:T(8,128)(2,1)} reshape(bf16[32,73728]{1,0:T(8,128)(2,1)} %get-tuple-element.184) | data formatting | bytes 9437184 | tf_op jit(solution)/shard_map/reshape | solution.py:28
  269.3 12.0 copy.35
  281.3 7.2 fusion.68
  292.1 8.0 fusion.52
  304.7 6.1 fusion.55
  312.5 5.1 reduce-scatter.16.cloned.1.call-done
  317.6 15.5 %reduce-scatter.12.cloned.1.call-done = bf16[2,1,128,1536]{3,2,1,0:T(8,128)(2,1)} async-done(((bf16[4,1,128,1536]{3,2,1,0:T(8,128)(2,1)}), bf16[2,1,128,1536]{3,2,1,0:T(8,128)(2,1)}) %reduce-scatter.12.cloned.1.call-update) | async-done | bytes 786448 | tf_op jit(solution)/shard_map/reduce_scatter | solution.py:39
  333.2 6.7 fusion.43
  339.9 16.9 %reduce-scatter.18.cloned.1.call-done = bf16[1,1,128,1536]{3,2,1,0:T(8,128)(2,1)} async-done(((bf16[2,1,128,1536]{3,2,1,0:T(8,128)(2,1)}), bf16[1,1,128,1536]{3,2,1,0:T(8,128)(2,1)}) %reduce-scatter.18.cloned.1.call-update) | async-done | bytes 393232 | tf_op jit(solution)/shard_map/reduce_scatter | solution.py:39
  358.2 21.7 %reduce-scatter.14.cloned.1.call-done = bf16[1,1,128,1536]{3,2,1,0:T(8,128)(2,1)} async-done(((bf16[2,1,128,1536]{3,2,1,0:T(8,128)(2,1)}), bf16[1,1,128,1536]{3,2,1,0:T(8,128)(2,1)}) %reduce-scatter.14.cloned.1.call-update) | async-done | bytes 393232 | tf_op jit(solution)/shard_map/reduce_scatter | solution.py:39
  449.1 28.3 %stack.567 = bf16[32,73728]{1,0:T(8,128)(2,1)} concatenate(bf16[1,73728]{1,0:T(2,128)(2,1)} %bitcast.775, bf16[1,73728]{1,0:T(2,128)(2,1)} %bitcast.776, bf16[1,73728]{1,0:T(2,128)(2,1)} %bitcast.777, bf16[1,73728]{1,0:T(2,128)(2,1)} %bitcast.778, bf16[1,73728]{1,0:T(2,128)(2,1)} %bitcast.779, bf16[1,73728]{1,0:T(2,128)(2,1)} %bitcast.780, bf16[1,73728]{1,0:T(2,128)(2,1)} %bitcast.781, ...), dimensions={0} | concatenate | bytes 9437184 | tf_op jit(solution)/shard_map/stack | solution.py:44
  477.4 28.6 %stack.600 = bf16[32,73728]{1,0:T(8,128)(2,1)} concatenate(bf16[1,73728]{1,0:T(2,128)(2,1)} %bitcast.807, bf16[1,73728]{1,0:T(2,128)(2,1)} %bitcast.808, bf16[1,73728]{1,0:T(2,128)(2,1)} %bitcast.809, bf16[1,73728]{1,0:T(2,128)(2,1)} %bitcast.810, bf16[1,73728]{1,0:T(2,128)(2,1)} %bitcast.811, bf16[1,73728]{1,0:T(2,128)(2,1)} %bitcast.812, bf16[1,73728]{1,0:T(2,128)(2,1)} %bitcast.813, ...), dimensions={0} | concatenate | bytes 9437184 | tf_op jit(solution)/shard_map/stack | solution.py:44
  511.9 24.3 %while.25 = (s32[]{:T(128)}, bf16[3,512,128]{1,2,0:T(8,128)(2,1)}, bf16[3,512,128]{1,2,0:T(8,128)(2,1)}, bf16[3,512,128]{1,2,0:T(8,128)(2,1)}, bf16[3,512,128]{2...) while((s32[]{:T(128)}, bf16[3,512,128]{1,2,0:T(8,128)(2,1)}, ...), condition=%wide.region_20.21_spmd, body=%wide.region_16.20_spmd.sunk | while | flops 340982272 | bytes 16547457 | solution.py:187
  600.0 23.8 %stack.501 = bf16[32,55296]{1,0:T(8,128)(2,1)} concatenate(bf16[1,55296]{1,0:T(2,128)(2,1)} %bitcast.848, bf16[1,55296]{1,0:T(2,128)(2,1)} %bitcast.849, bf16[1,55296]{1,0:T(2,128)(2,1)} %bitcast.850, bf16[1,55296]{1,0:T(2,128)(2,1)} %bitcast.851, bf16[1,55296]{1,0:T(2,128)(2,1)} %bitcast.839, bf16[1,55296]{1,0:T(2,128)(2,1)} %bitcast.840, bf16[1,55296]{1,0:T(2,128)(2,1)} %bitcast.841, ...), dimensions={0} | concatenate | bytes 7077888 | tf_op jit(solution)/shard_map/stack | solution.py:44
  623.8 9.1 stack.534
  632.9 31.7 %pad_maximum_fusion = bf16[32,221184]{1,0:T(8,128)(2,1)} fusion(bf16[32,73728]{1,0:T(8,128)(2,1)} %stack.600, bf16[32,73728]{1,0:T(8,128)(2,1)} %stack.567, bf16[32,18432]{1,0:T(8,128)(2,1)S(1)} %stack.534, bf16[32,55296]{1,0:T(8,128)(2,1)} %stack.501), kind=kLoop, calls=%fused_computation.54 | loop fusion | flops 56623104 | bytes 28311552 | tf_op jit(solution)/shard_map/concatenate | solution.py:55
  669.4 615.7 %all-reduce.3.cloned.1.call-done = bf16[32,221184]{1,0:T(8,128)(2,1)} async-done(((bf16[32,221184]{1,0:T(8,128)(2,1)}), bf16[32,221184]{1,0:T(8,128)(2,1)}) %all-reduce.3.cloned.1.call-update) | async-done | bytes 14155792
  (426 shorter events, 229.9 us)
Async XLA Ops:
  7.2 147.5 %all-gather.15.cloned.1.call-start = ((), (), s32[]{:S(2)}) async-start(), calls=%async_computation.18 | async-start | bytes 14598144 | tf_op jit(solution)/shard_map/all_gather | solution.py:26
  12.9 166.3 %all-gather.7.cloned.1.call-start = ((), (), s32[]{:S(2)}) async-start(), calls=%async_computation.7 | async-start | bytes 1966080 | tf_op jit(solution)/shard_map/all_gather | solution.py:217
  13.6 141.1 %copy-start.51 = (f32[1536]{0:T(1024)}, f32[1536]{0:T(1024)S(1)}, u32[]{:S(2)}) copy-start(f32[1536]{0:T(1024)S(1)} %get-tuple-element.145) | copy-start | bytes 18436
  13.8 141.0 %copy-start.56 = (f32[128]{0:T(128)}, f32[128]{0:T(128)S(1)}, u32[]{:S(2)}) copy-start(f32[128]{0:T(128)S(1)} %broadcast_multiply_fusion.5) | copy-start | bytes 1540
  14.1 140.7 %copy-start.58 = (f32[128]{0:T(128)}, f32[128]{0:T(128)S(1)}, u32[]{:S(2)}) copy-start(f32[128]{0:T(128)S(1)} %add_rsqrt_fusion.1) | copy-start | bytes 1540
  15.1 195.8 %reduce-scatter.8.cloned.1.call-start = ((), (), s32[]{:S(2)}) async-start(), calls=%async_computation.8 | async-start | bytes 2359296 | tf_op jit(solution)/shard_map/reduce_scatter | solution.py:39
  196.4 38.0 %copy-start.1 = (bf16[1,128,1536]{2,1,0:T(8,128)(2,1)S(1)}, bf16[1,128,1536]{2,1,0:T(8,128)(2,1)}, u32[]{:S(2)}) copy-start(bf16[1,128,1536]{2,1,0:T(8,128)(2,1)} %param.11) | copy-start | bytes 1179652
  196.4 40.5 %copy-start.55 = (f32[1536]{0:T(1024)S(1)}, f32[1536]{0:T(1024)}, u32[]{:S(2)}) copy-start(f32[1536]{0:T(1024)} %get-tuple-element.142) | copy-start | bytes 18436
  197.7 41.3 %copy-start.5 = (bf16[1,128,1536]{2,1,0:T(8,128)(2,1)S(1)}, bf16[1,128,1536]{2,1,0:T(8,128)(2,1)}, u32[]{:S(2)}) copy-start(bf16[1,128,1536]{2,1,0:T(8,128)(2,1)} %param.17) | copy-start | bytes 1179652
  197.7 41.3 %copy-start.53 = (f32[1536]{0:T(1024)S(1)}, f32[1536]{0:T(1024)}, u32[]{:S(2)}) copy-start(f32[1536]{0:T(1024)} %get-tuple-element.141) | copy-start | bytes 18436
  197.8 36.7 %reduce-scatter.10.cloned.1.call-start = ((), (), s32[]{:S(2)}) async-start(), calls=%async_computation.9 | async-start | bytes 1179648 | tf_op jit(solution)/shard_map/reduce_scatter | solution.py:39
  210.9 70.4 %all-gather.9.cloned.1.call-start = ((), (), s32[]{:S(2)}) async-start(), calls=%async_computation.10 | async-start | bytes 1966080 | tf_op jit(solution)/shard_map/all_gather | solution.py:231
  238.9 53.1 %all-gather.11.cloned.1.call-start = ((), (), s32[]{:S(2)}) async-start(), calls=%async_computation.13 | async-start | bytes 1966080 | tf_op jit(solution)/shard_map/all_gather | solution.py:276
  239.8 77.7 %reduce-scatter.16.cloned.1.call-start = ((), (), s32[]{:S(2)}) async-start(), calls=%async_computation.14 | async-start | bytes 2359296 | tf_op jit(solution)/shard_map/reduce_scatter | solution.py:39
  304.4 28.7 %reduce-scatter.12.cloned.1.call-start = ((), (), s32[]{:S(2)}) async-start(), calls=%async_computation.11 | async-start | bytes 2359296 | tf_op jit(solution)/shard_map/reduce_scatter | solution.py:39
  312.4 44.4 %reduce-scatter.18.cloned.1.call-start = ((), (), s32[]{:S(2)}) async-start(), calls=%async_computation.15 | async-start | bytes 1179648 | tf_op jit(solution)/shard_map/reduce_scatter | solution.py:39
  317.6 62.4 %reduce-scatter.14.cloned.1.call-start = ((), (), s32[]{:S(2)}) async-start(), calls=%async_computation.12 | async-start | bytes 1179648 | tf_op jit(solution)/shard_map/reduce_scatter | solution.py:39
  333.1 172.9 %all-gather.13.cloned.1.call-start = ((), (), s32[]{:S(2)}) async-start(), calls=%async_computation.16 | async-start | bytes 1966080 | tf_op jit(solution)/shard_map/all_gather | solution.py:287
  382.6 283.3 %reduce-scatter.20.cloned.1.call-start = ((), (), s32[]{:S(2)}) async-start(), calls=%async_computation.17 | async-start | bytes 1966080 | tf_op jit(solution)/shard_map/reduce_scatter | solution.py:298
  550.1 25.8 %copy-start.10 = (bf16[1,1,48,1152]{3,2,1,0:T(8,128)(2,1)S(1)}, bf16[1,1,48,1152]{3,2,1,0:T(8,128)(2,1)}, u32[]{:S(2)}) copy-start(bf16[1,1,48,1152]{3,2,1,0:T(8,128)(2,1)} %get-tuple-element.268) | copy-start | bytes 331780
  551.2 25.5 %copy-start.9 = (bf16[1,1,48,1152]{3,2,1,0:T(8,128)(2,1)S(1)}, bf16[1,1,48,1152]{3,2,1,0:T(8,128)(2,1)}, u32[]{:S(2)}) copy-start(bf16[1,1,48,1152]{3,2,1,0:T(8,128)(2,1)} %get-tuple-element.280) | copy-start | bytes 331780
  572.4 26.1 %copy-start.39 = (bf16[1,1,48,384]{3,2,1,0:T(8,128)(2,1)S(1)}, bf16[1,1,48,384]{3,2,1,0:T(8,128)(2,1)}, u32[]{:S(2)}) copy-start(bf16[1,1,48,384]{3,2,1,0:T(8,128)(2,1)} %get-tuple-element.313) | copy-start | bytes 110596
  573.3 25.9 %copy-start.38 = (bf16[1,1,48,384]{3,2,1,0:T(8,128)(2,1)S(1)}, bf16[1,1,48,384]{3,2,1,0:T(8,128)(2,1)}, u32[]{:S(2)}) copy-start(bf16[1,1,48,384]{3,2,1,0:T(8,128)(2,1)} %get-tuple-element.312) | copy-start | bytes 110596
  600.0 685.1 %all-reduce.3.cloned.1.call-start = ((), (), s32[]{:S(2)}) async-start(), calls=%async_computation.19 | async-start | bytes 28311552
  (61 other events, 900.8 us)
Sparse Core Ops, SparseCore 0:
  13.1 141.6 all-gather.14
  157.0 22.2 all-gather.6
  197.9 12.9 reduce-scatter.7
  213.1 21.2 reduce-scatter.9
  239.1 25.3 all-gather.8
  266.5 25.5 all-gather.10
  304.5 12.9 reduce-scatter.15
  319.9 13.1 reduce-scatter.11
  335.5 21.2 reduce-scatter.17
  359.0 20.8 reduce-scatter.13
  382.7 25.3 all-gather.12
  600.1 24.5 reduce-scatter.19
  664.8 620.2 all-reduce.2
where the time goes:
time: 1320 us; the launch traced here: 1300 us
  waiting for transfers between devices  861 us (65%)
  local copies, waits for them, and re-layouts  298 us (23%)
  matrix products  67.9 us (5%)
  other arithmetic  58.8 us (4%)
  between operations  15 us (1%)
    unnamed x14, waiting for transfers between devices  616 us
    all_gather x1, waiting for transfers between devices, one_gather(): lines, at, gathered = (lax.all_gather(ravelled, axis), 0, [])  140 us
    unnamed x275, local copies, waits for them, and re-layouts  122 us
    reduce_scatter x6, waiting for transfers between devices, own_block(): blocks = lax.psum_scatter(blocks, axes[k], scatter_dimension=0, tiled=True)  95.7 us
    another operation x7, local copies, waits for them, and re-layouts, cut_along(): return jnp.stack(jnp.split(value, count, axis=dim))  90.1 us
    concatenate x1, other arithmetic, sum_packed(): lines = jnp.concatenate([b.reshape(count, -1) for b in blocks], axis=1)  31.7 us
  transfers between devices with their start and end apart: 13, of which 10 were waited for; matrix products, arithmetic and copies ran while one was open for 21% of the time, Pallas kernels for 0%

commit v1 on v0

v1 whole, which is shorter than its diff:
```python
import math

import jax
import jax.numpy as jnp
from jax import lax
from jax.sharding import PartitionSpec as P

HEAD_DIM = 128
LN_EPS = 1e-06
TEMPER = 2.5


def normalize(x):
    c = x - jnp.mean(x, axis=-1, keepdims=True)
    r = lax.rsqrt(jnp.mean(c * c, axis=-1, keepdims=True) + LN_EPS)
    return c * r, r


def norm_back(n, r, e):
    return r * (e - jnp.mean(e, axis=-1, keepdims=True) - n * jnp.mean(e * n, axis=-1, keepdims=True))


def dot(a, b, ca, cb):
    return lax.dot_general(a, b, (((ca,), (cb,)), ((), ())), preferred_element_type=jnp.float32)


def bf(x):
    return x.astype(jnp.bfloat16)


def body(tokens, modulation, w_qkv, w_out, w_in, w_back, out_grad):
    seq, width = tokens.shape[1:]
    own = w_qkv.shape[3]
    heads = own // HEAD_DIM
    ff = w_in.shape[2]
    c = TEMPER / math.sqrt(HEAD_DIM)
    q_s = 1.0 / math.sqrt(seq * lax.axis_size("fsdp") * lax.axis_size("sp"))
    mod = modulation[0, 0]
    m = [mod[i : i + 1] for i in range(6)]

    rows = w_qkv.shape[1]
    weights = [
        lax.all_gather(w, "fsdp", axis=0, tiled=True)
        for w in (w_qkv[0].reshape(rows, 3 * own), w_out[0].T, w_in[0], w_back[0].T)
    ]
    wq, wo, wi, wb = weights

    def gather(v):
        return lax.all_gather(v, "sp", axis=0, tiled=True)

    def scatter(v):
        return lax.psum_scatter(bf(v), "sp", scatter_dimension=0, tiled=True).astype(jnp.float32)

    x = tokens[0].astype(jnp.float32)
    dx = out_grad[0].astype(jnp.float32)
    n1, r1 = normalize(x)
    a1 = gather(bf(n1 * (1.0 + m[1]) + m[0]))
    dm = gather(bf(m[5] * dx))
    qkv = bf(dot(a1, wq, 1, 0))

    def attend(h):
        q, k, v = (qkv[:, i * own + h * HEAD_DIM : i * own + (h + 1) * HEAD_DIM] for i in range(3))
        p = jax.nn.softmax(dot(q, k, 1, 1) * c, axis=-1)
        return q, k, v, p

    o = jnp.concatenate([bf(dot(bf(p), v, 1, 0)) for q, k, v, p in map(attend, range(heads))], axis=1)
    mid = x + m[2] * scatter(dot(o, wo, 1, 1))
    n2, r2 = normalize(mid)
    a2 = gather(bf(n2 * (1.0 + m[4]) + m[3]))
    u = dot(a2, wi, 1, 0)
    act, pull = jax.vjp(lambda t: jax.nn.gelu(t, approximate=True), u)
    g = bf(act)
    final = bf(mid + m[5] * scatter(dot(g, wb, 1, 1)))

    du = bf(pull(dot(dm, wb, 1, 0))[0])
    dmid = dx + norm_back(n2, r2, scatter(dot(du, wi, 1, 1)) * (1.0 + m[4]))
    da = gather(bf(m[2] * dmid))
    do = bf(dot(da, wo, 1, 0))
    dq, dk, dv = [], [], []
    for h in range(heads):
        q, k, v, p = attend(h)
        doh = do[:, h * HEAD_DIM : (h + 1) * HEAD_DIM]
        dp = dot(doh, v, 1, 1)
        ds = bf(c * p * (dp - jnp.sum(p * dp, axis=-1, keepdims=True)))
        dq.append(bf(dot(ds, k, 1, 0)))
        dk.append(bf(dot(ds, q, 0, 0)))
        dv.append(bf(dot(bf(p), doh, 0, 0)))
    dqkv = jnp.concatenate(dq + dk + dv, axis=1)
    dxin = dmid + norm_back(n1, r1, scatter(dot(dqkv, wq, 1, 1)) * (1.0 + m[1]))

    def reduce(a, b):
        g = bf(dot(a, b, 0, 0) * q_s)
        return lax.psum_scatter(g, "fsdp", scatter_dimension=0, tiled=True).astype(jnp.float32)

    gb = reduce(dm, g)
    gi = reduce(a2, du)
    go = reduce(da, o)
    gq = reduce(a1, dqkv)
    return (
        final[None],
        dxin[None],
        gq.reshape(1, rows, 3, own),
        go.T[None],
        gi[None],
        gb.T[None],
    )


def solution(mesh):
    return jax.shard_map(
        body,
        mesh=mesh,
        in_specs=(
            P("fsdp", "sp", None),
            P("fsdp", None, None, None),
            P(None, "fsdp", None, "sp"),
            P(None, "sp", "fsdp"),
            P(None, "fsdp", "sp"),
            P(None, "sp", "fsdp"),
            P("fsdp", "sp", None),
        ),
        out_specs=(
            P("fsdp", "sp", None),
            P("fsdp", "sp", None),
            P(None, "fsdp", None, "sp"),
            P(None, "sp", "fsdp"),
            P(None, "fsdp", "sp"),
            P(None, "sp", "fsdp"),
        ),
        check_vma=False,
    )
```

time: 1320 us -> 1510 us (1.14); the launches traced: 1300 us -> 1510 us
  waiting for transfers between devices: 861 us -> 1390 us
  local copies, waits for them, and re-layouts: 298 us -> 11.5 us
  other arithmetic: 58.8 us -> 25 us
    reduce_scatter x7 -> x8, waiting for transfers between devices: 95.7 us -> 976 us  [the longest x4 893 us: reduce(): lax.psum_scatter(g, 'fsdp', scatter_dimension=0, tiled=True)]
    unnamed x14 -> x16, waiting for transfers between devices: 616 us -> 2.11 us
    all_gather x5 -> x8, waiting for transfers between devices: 150 us -> 409 us  [the longest x4 309 us: body(): lax.all_gather(w, 'fsdp', axis=0, tiled=True)]
    unnamed x275 -> x95, local copies, waits for them, and re-layouts: 122 us -> 10.5 us
    another operation x21 -> x0, local copies, waits for them, and re-layouts: 105 us -> none  [the longest x7 90.1 us: cut_along(): return jnp.stack(jnp.split(value, count, axis=dim))]
    concatenate x3 -> x0, other arithmetic: 32.5 us -> none  [the longest x1 31.7 us: sum_packed(): lines = jnp.concatenate([b.reshape(count, -1) for b in blocks], axis=1)]
    transpose x5 -> x0, local copies, waits for them, and re-layouts: 19 us -> none  [the longest x2 15.2 us: laid_out(): blocks = jnp.moveaxis(blocks, 0, dim)]
    reshape x2 -> x1, local copies, waits for them, and re-layouts: 19.4 us -> 0.98 us  [body(): gq.reshape(1, rows, 3, own)]
  transfers between devices with their start and end apart: 13 -> 16, of which waited for: 10 -> 16; matrix products, arithmetic and copies ran while one was open for 21% -> 4% of each run, Pallas kernels for 0% -> 0%
where the time goes in v1:
time: 1510 us
  waiting for transfers between devices  1390 us (92%)
  matrix products  72.8 us (5%)
  other arithmetic  25 us (2%)
    reduce_scatter x4, waiting for transfers between devices, reduce(): lax.psum_scatter(g, 'fsdp', scatter_dimension=0, tiled=True)  893 us
    all_gather x4, waiting for transfers between devices, body(): lax.all_gather(w, 'fsdp', axis=0, tiled=True)  309 us
    all_gather x4, waiting for transfers between devices, gather(): return lax.all_gather(v, 'sp', axis=0, tiled=True)  100 us
    reduce_scatter x4, waiting for transfers between devices, scatter(): lax.psum_scatter(bf(v), 'sp', scatter_dimension=0, tiled=True)  82.7 us
    dot_general x30, matrix products, dot(): lax.dot_general(a, b, (((ca,), (cb,)), ((), ())), preferred_element_type=...  72.8 us
  transfers between devices with their start and end apart: 16, of which 16 were waited for; matrix products, arithmetic and copies ran while one was open for 4% of the time, Pallas kernels for 0%

profile of v1, /device:TPU:0, one launch (start us, length us, event | category | flops | bytes accessed | tf_op | source)
XLA Modules:
  0.0 1511.7 jit_solution(13099963642387650823)
XLA Ops:
  14.2 25.4 %all-gather.10.cloned.1.call-done = bf16[512,1536]{1,0:T(8,128)(2,1)} async-done(((bf16[128,1536]{1,0:T(8,128)(2,1)}), bf16[512,1536]{1,0:T(8,128)(2,1)}) %all-gather.10.cloned.1.call-update) | async-done | bytes 1572880 | tf_op jit(solution)/shard_map/all_gather | solution.py:49
  39.6 82.2 %all-gather.12.cloned.1.call-done = bf16[1536,1152]{1,0:T(8,128)(2,1)} async-done(((bf16[48,1152]{1,0:T(8,128)(2,1)}), bf16[1536,1152]{1,0:T(8,128)(2,1)}) %all-gather.12.cloned.1.call-update) | async-done | bytes 3538960 | tf_op jit(solution)/shard_map/all_gather | solution.py:43
  121.8 4.7 convolution_convert_fusion.1
  129.2 61.7 %all-gather.14.cloned.1.call-done = bf16[1536,384]{1,0:T(8,128)(2,1)} async-done(((bf16[48,384]{1,0:T(8,128)(2,1)}), bf16[1536,384]{1,0:T(8,128)(2,1)}) %all-gather.14.cloned.1.call-update) | async-done | bytes 1179664 | tf_op jit(solution)/shard_map/all_gather | solution.py:43
  197.5 18.0 %reduce-scatter.9.cloned.1.call-done = bf16[128,1536]{1,0:T(8,128)(2,1)} async-done(((bf16[512,1536]{1,0:T(8,128)(2,1)}), bf16[128,1536]{1,0:T(8,128)(2,1)}) %reduce-scatter.9.cloned.1.call-update) | async-done | bytes 393232 | tf_op jit(solution)/shard_map/reduce_scatter | solution.py:52
  219.1 23.9 %all-gather.20.cloned.1.call-done = bf16[512,1536]{1,0:T(8,128)(2,1)} async-done(((bf16[128,1536]{1,0:T(8,128)(2,1)}), bf16[512,1536]{1,0:T(8,128)(2,1)}) %all-gather.20.cloned.1.call-update) | async-done | bytes 1572880 | tf_op jit(solution)/shard_map/all_gather | solution.py:49
  243.0 87.1 %all-gather.18.cloned.1.call-done = bf16[1536,1536]{1,0:T(8,128)(2,1)} async-done(((bf16[48,1536]{1,0:T(8,128)(2,1)}), bf16[1536,1536]{1,0:T(8,128)(2,1)}) %all-gather.18.cloned.1.call-update) | async-done | bytes 4718608 | tf_op jit(solution)/shard_map/all_gather | solution.py:43
  330.1 7.1 fusion.97
  337.3 77.8 %all-gather.24.cloned.1.call-done = bf16[1,1536,1536]{2,1,0:T(8,128)(2,1)} async-done(((bf16[1,48,1536]{2,1,0:T(8,128)(2,1)}), bf16[1,1536,1536]{2,1,0:T(8,128)(2,1)}) %all-gather.24.cloned.1.call-update) | async-done | bytes 4718608 | tf_op jit(solution)/shard_map/all_gather | solution.py:43
  415.1 25.5 %all-gather.16.cloned.1.call-done = bf16[512,1536]{1,0:T(8,128)(2,1)} async-done(((bf16[128,1536]{1,0:T(8,128)(2,1)}), bf16[512,1536]{1,0:T(8,128)(2,1)}) %all-gather.16.cloned.1.call-update) | async-done | bytes 1572880 | tf_op jit(solution)/shard_map/all_gather | solution.py:49
  440.6 9.7 fusion.13
  451.5 3.8 fusion.14
  455.6 7.3 convolution_convert_fusion.2
  462.9 17.4 %reduce-scatter.13.cloned.1.call-done = bf16[128,1536]{1,0:T(8,128)(2,1)} async-done(((bf16[512,1536]{1,0:T(8,128)(2,1)}), bf16[128,1536]{1,0:T(8,128)(2,1)}) %reduce-scatter.13.cloned.1.call-update) | async-done | bytes 393232 | tf_op jit(solution)/shard_map/reduce_scatter | solution.py:52
  481.7 25.6 %reduce-scatter.11.cloned.1.call-done = bf16[128,1536]{1,0:T(8,128)(2,1)} async-done(((bf16[512,1536]{1,0:T(8,128)(2,1)}), bf16[128,1536]{1,0:T(8,128)(2,1)}) %reduce-scatter.11.cloned.1.call-update) | async-done | bytes 393232 | tf_op jit(solution)/shard_map/reduce_scatter | solution.py:52
  510.3 25.5 %all-gather.22.cloned.1.call-done = bf16[512,1536]{1,0:T(8,128)(2,1)} async-done(((bf16[128,1536]{1,0:T(8,128)(2,1)}), bf16[512,1536]{1,0:T(8,128)(2,1)}) %all-gather.22.cloned.1.call-update) | async-done | bytes 1572880 | tf_op jit(solution)/shard_map/all_gather | solution.py:49
  562.2 4.4 fusion
  568.0 6.8 fusion.1
  576.5 4.1 fusion.2
  580.6 196.6 %reduce-scatter.19.cloned.1.call-done = bf16[48,384]{1,0:T(8,128)(2,1)} async-done(((bf16[1536,384]{1,0:T(8,128)(2,1)}), bf16[48,384]{1,0:T(8,128)(2,1)}) %reduce-scatter.19.cloned.1.call-update) | async-done | bytes 36880 | tf_op jit(solution)/shard_map/reduce_scatter | solution.py:93
  778.6 21.7 %reduce-scatter.15.cloned.1.call-done = bf16[128,1536]{1,0:T(8,128)(2,1)} async-done(((bf16[512,1536]{1,0:T(8,128)(2,1)}), bf16[128,1536]{1,0:T(8,128)(2,1)}) %reduce-scatter.15.cloned.1.call-update) | async-done | bytes 393232 | tf_op jit(solution)/shard_map/reduce_scatter | solution.py:52
  803.9 234.4 %reduce-scatter.21.cloned.1.call-done = bf16[48,1536]{1,0:T(8,128)(2,1)} async-done(((bf16[1536,1536]{1,0:T(8,128)(2,1)}), bf16[48,1536]{1,0:T(8,128)(2,1)}) %reduce-scatter.21.cloned.1.call-update) | async-done | bytes 147472 | tf_op jit(solution)/shard_map/reduce_scatter | solution.py:93
  1039.9 232.3 %reduce-scatter.23.cloned.1.call-done = bf16[48,1536]{1,0:T(8,128)(2,1)} async-done(((bf16[1536,1536]{1,0:T(8,128)(2,1)}), bf16[48,1536]{1,0:T(8,128)(2,1)}) %reduce-scatter.23.cloned.1.call-update) | async-done | bytes 147472 | tf_op jit(solution)/shard_map/reduce_scatter | solution.py:93
  1273.8 229.6 %reduce-scatter.17.cloned.1.call-done = bf16[48,1152]{1,0:T(8,128)(2,1)} async-done(((bf16[1536,1152]{1,0:T(8,128)(2,1)}), bf16[48,1152]{1,0:T(8,128)(2,1)}) %reduce-scatter.17.cloned.1.call-update) | async-done | bytes 110608 | tf_op jit(solution)/shard_map/reduce_scatter | solution.py:93
  (178 shorter events, 64.6 us)
Async XLA Ops:
  7.2 32.5 %all-gather.10.cloned.1.call-start = ((), (), s32[]{:S(2)}) async-start(), calls=%async_computation.8 | async-start | bytes 1966080 | tf_op jit(solution)/shard_map/all_gather | solution.py:49
  8.4 118.1 %copy-start.22 = (f32[128]{0:T(128)}, f32[128]{0:T(128)S(1)}, u32[]{:S(2)}) copy-start(f32[128]{0:T(128)S(1)} %broadcast_multiply_fusion.5) | copy-start | bytes 1540
  9.6 116.8 %copy-start.24 = (f32[128]{0:T(128)}, f32[128]{0:T(128)S(1)}, u32[]{:S(2)}) copy-start(f32[128]{0:T(128)S(1)} %add_rsqrt_fusion.1) | copy-start | bytes 1540
  12.6 109.2 %all-gather.12.cloned.1.call-start = ((), (), s32[]{:S(2)}) async-start(), calls=%async_computation.9 | async-start | bytes 3649536 | tf_op jit(solution)/shard_map/all_gather | solution.py:43
  13.4 177.5 %all-gather.14.cloned.1.call-start = ((), (), s32[]{:S(2)}) async-start(), calls=%async_computation.10 | async-start | bytes 1216512 | tf_op jit(solution)/shard_map/all_gather | solution.py:43
  14.1 201.3 %reduce-scatter.9.cloned.1.call-start = ((), (), s32[]{:S(2)}) async-start(), calls=%async_computation.11 | async-start | bytes 1966080 | tf_op jit(solution)/shard_map/reduce_scatter | solution.py:52
  127.0 411.5 %copy-start.14 = (f32[512]{0:T(512)}, f32[512]{0:T(512)S(1)}, u32[]{:S(2)}) copy-start(f32[512]{0:T(512)S(1)} %fusion.39) | copy-start | bytes 6148
  128.4 62.4 %copy-start.36 = (bf16[512,128]{0,1:T(8,128)(2,1)}, bf16[512,128]{0,1:T(8,128)(2,1)S(1)}, u32[]{:S(2)}) copy-start(bf16[512,128]{0,1:T(8,128)(2,1)S(1)} %convolution_convert_fusion.14) | copy-start | bytes 393220
  128.8 62.0 %copy-start.38 = (bf16[512,128]{0,1:T(8,128)(2,1)}, bf16[512,128]{0,1:T(8,128)(2,1)S(1)}, u32[]{:S(2)}) copy-start(bf16[512,128]{0,1:T(8,128)(2,1)S(1)} %convolution_convert_fusion.15) | copy-start | bytes 393220
  194.3 48.7 %all-gather.20.cloned.1.call-start = ((), (), s32[]{:S(2)}) async-start(), calls=%async_computation.15 | async-start | bytes 1966080 | tf_op jit(solution)/shard_map/all_gather | solution.py:49
  196.1 134.0 %all-gather.18.cloned.1.call-start = ((), (), s32[]{:S(2)}) async-start(), calls=%async_computation.13 | async-start | bytes 4866048 | tf_op jit(solution)/shard_map/all_gather | solution.py:43
  196.7 218.4 %all-gather.24.cloned.1.call-start = ((), (), s32[]{:S(2)}) async-start(), calls=%async_computation.23 | async-start | bytes 4866048 | tf_op jit(solution)/shard_map/all_gather | solution.py:43
  197.5 243.1 %all-gather.16.cloned.1.call-start = ((), (), s32[]{:S(2)}) async-start(), calls=%async_computation.12 | async-start | bytes 1966080 | tf_op jit(solution)/shard_map/all_gather | solution.py:49
  219.1 261.2 %reduce-scatter.13.cloned.1.call-start = ((), (), s32[]{:S(2)}) async-start(), calls=%async_computation.16 | async-start | bytes 1966080 | tf_op jit(solution)/shard_map/reduce_scatter | solution.py:52
  455.4 52.0 %reduce-scatter.11.cloned.1.call-start = ((), (), s32[]{:S(2)}) async-start(), calls=%async_computation.14 | async-start | bytes 1966080 | tf_op jit(solution)/shard_map/reduce_scatter | solution.py:52
  462.9 72.9 %all-gather.22.cloned.1.call-start = ((), (), s32[]{:S(2)}) async-start(), calls=%async_computation.17 | async-start | bytes 1966080 | tf_op jit(solution)/shard_map/all_gather | solution.py:49
  510.2 267.0 %reduce-scatter.19.cloned.1.call-start = ((), (), s32[]{:S(2)}) async-start(), calls=%async_computation.20 | async-start | bytes 1216512 | tf_op jit(solution)/shard_map/reduce_scatter | solution.py:93
  549.4 251.0 %reduce-scatter.15.cloned.1.call-start = ((), (), s32[]{:S(2)}) async-start(), calls=%async_computation.18 | async-start | bytes 1966080 | tf_op jit(solution)/shard_map/reduce_scatter | solution.py:52
  560.8 477.4 %reduce-scatter.21.cloned.1.call-start = ((), (), s32[]{:S(2)}) async-start(), calls=%async_computation.21 | async-start | bytes 4866048 | tf_op jit(solution)/shard_map/reduce_scatter | solution.py:93
  566.6 705.6 %reduce-scatter.23.cloned.1.call-start = ((), (), s32[]{:S(2)}) async-start(), calls=%async_computation.22 | async-start | bytes 4866048 | tf_op jit(solution)/shard_map/reduce_scatter | solution.py:93
  574.8 928.7 %reduce-scatter.17.cloned.1.call-start = ((), (), s32[]{:S(2)}) async-start(), calls=%async_computation.19 | async-start | bytes 3649536 | tf_op jit(solution)/shard_map/reduce_scatter | solution.py:93
  580.6 219.8 %copy-start.23 = (f32[128]{0:T(128)S(1)}, f32[128]{0:T(128)}, u32[]{:S(2)}) copy-start(f32[128]{0:T(128)} %copy-done.22) | copy-start | bytes 1540
  580.6 219.8 %copy-start.25 = (f32[128]{0:T(128)S(1)}, f32[128]{0:T(128)}, u32[]{:S(2)}) copy-start(f32[128]{0:T(128)} %copy-done.24) | copy-start | bytes 1540
  580.6 221.1 %copy-start.4 = (f32[128,1536]{1,0:T(8,128)S(1)}, f32[128,1536]{1,0:T(8,128)}, u32[]{:S(2)}) copy-start(f32[128,1536]{1,0:T(8,128)} %get-tuple-element.29) | copy-start | bytes 2359300
  (38 other events, 167.1 us)
Sparse Core Ops, SparseCore 0:
  12.7 26.8 all-gather.9
  43.2 78.5 all-gather.11
  124.8 65.9 all-gather.13
  194.5 20.9 reduce-scatter.8
  217.6 25.4 all-gather.19
  245.9 84.1 all-gather.17
  333.2 81.8 all-gather.23
  417.3 23.1 all-gather.15
  455.5 24.7 reduce-scatter.12
  482.6 24.6 reduce-scatter.10
  510.4 25.4 all-gather.21
  549.5 227.6 reduce-scatter.18
  779.6 20.6 reduce-scatter.14
  805.3 232.9 reduce-scatter.20
  1043.2 228.9 reduce-scatter.22
  1277.0 226.3 reduce-scatter.16

commit v2 on v1

v2 whole, which is shorter than its diff:
```python
import functools
import math

import jax
import jax.numpy as jnp
from jax import lax
from jax.experimental import pallas as pl
from jax.experimental.pallas import tpu as pltpu
from jax.sharding import Mesh
from jax.sharding import PartitionSpec as P

HEAD_DIM = 128
LN_EPS = 1e-06
TEMPER = 2.5
BF = jnp.bfloat16
F32 = jnp.float32
AXES = ("z", "y", "h", "l", "c")


def bf(x):
    return x.astype(BF)


def f32(x):
    return x.astype(F32)


def dot(a, b, ca=1, cb=0):
    return lax.dot_general(a, b, (((ca,), (cb,)), ((), ())), preferred_element_type=F32)


def normalize(x):
    d = x - jnp.mean(x, axis=-1, keepdims=True)
    r = lax.rsqrt(jnp.mean(d * d, axis=-1, keepdims=True) + LN_EPS)
    return d * r, r


def norm_back(n, r, e):
    return r * (e - jnp.mean(e, axis=-1, keepdims=True) - n * jnp.mean(e * n, axis=-1, keepdims=True))


def gelu_pair(u):
    k0 = math.sqrt(2.0 / math.pi)
    s = u * u
    t = jnp.tanh(k0 * u * (1.0 + 0.044715 * s))
    g = 0.5 * u * (1.0 + t)
    d = 0.5 * (1.0 + t) + 0.5 * k0 * u * (1.0 - t * t) * (1.0 + 3.0 * 0.044715 * s)
    return g, d


def kernel(
    dims, tok, mod, wblk, og, fin, dxin, grads,
    W, G, R1A, R1B, R2A, R2B, A1, A2, DM, DA, GG, DU, QKV, DQKV, O, DO, PR, PS, RX, SX, MID, DX,
    own_sem, a1s, a1r, a2s, a2r, r1s, r1r, r2s, r2r, gs, gr, ss, sr,
):
    nz, ny, nh = dims
    z, y, h, l, c = (lax.axis_index(a) for a in AXES)
    ol, oc = 1 - l, 1 - c
    rows, width = wblk.shape[1:]
    half = width // 2
    seq = QKV.shape[0]
    pair = seq // 2
    own = QKV.shape[1] // 3
    heads = own // HEAD_DIM
    slab = ny * nh * rows
    scale = TEMPER / math.sqrt(HEAD_DIM)
    q_s = 1.0 / math.sqrt(seq * nz * ny * nh)
    cols = (pl.ds(0, half), pl.ds(half, half))

    def copy(src, dst, ssem, rsem, dev):
        return pltpu.make_async_remote_copy(
            src_ref=src, dst_ref=dst, send_sem=ssem, recv_sem=rsem,
            device_id=dev, device_id_type=pl.DeviceIdType.MESH,
        )

    def zz(k):
        return lax.rem(z + k + nz, nz)

    def yy(k):
        return lax.rem(y + k + ny, ny)

    def hh(k):
        return lax.rem(h + k + nh, nh)

    def at_rows(i):
        return pl.ds(pl.multiple_of(i * rows, 16), rows)

    group = (ny * nh, nz * nh)
    ring = (nz, ny)

    def far(color, j):
        d, dh = j // nh, j % nh
        return {"y": yy(d), "h": hh(dh)} if color == 0 else {"z": zz(d), "h": hh(dh)}

    def near(color, k):
        return {"z": zz(k)} if color == 0 else {"y": yy(k)}

    core_peer = {"c": oc}
    line_peer = {"l": ol}

    def own_block(s):
        return pltpu.make_async_copy(wblk.at[s], W.at[s, z, y, at_rows(h)], own_sem.at[s])

    def block_at(buf, s, color, j, sign):
        d, dh = j // nh, j % nh
        if color == 0:
            return buf.at[s, z, yy(sign * d), at_rows(hh(sign * dh)), cols[0]]
        return buf.at[s, zz(sign * d), y, at_rows(hh(sign * dh)), cols[1]]

    def slab_at(buf, s, color, k):
        if color == 0:
            return buf.at[s, zz(k), :, :, cols[0]]
        return buf.at[s, :, yy(k), :, cols[1]]

    def ag1(s, color, j, recv):
        piece = block_at(W, s, color, j if recv else 0, -1)
        return copy(piece, piece, a1s.at[s, color, j - 1], a1r.at[s, color, j - 1], far(color, j))

    def ag2(s, color, k, recv):
        piece = slab_at(W, s, color, -k if recv else 0)
        return copy(piece, piece, a2s.at[s, color, k - 1], a2r.at[s, color, k - 1], near(color, k))

    def ag1_start(s):
        for color in (0, 1):
            for j in range(1, group[color]):
                ag1(s, color, j, False).start()

    def ag2_start(s):
        for color in (0, 1):
            for j in range(1, group[color]):
                ag1(s, color, j, True).wait_recv()
            for k in range(1, ring[color]):
                ag2(s, color, k, False).start()

    def ag_wait(s):
        for color in (0, 1):
            for k in range(1, ring[color]):
                ag2(s, color, k, True).wait_recv()

    def ag_sent():
        for s in range(3):
            for color in (0, 1):
                for j in range(1, group[color]):
                    ag1(s, color, j, False).wait_send()
                for k in range(1, ring[color]):
                    ag2(s, color, k, False).wait_send()

    R1 = (R1A, R1B)
    R2 = (R2A, R2B)

    def rs1(s, g, color, k):
        return copy(
            slab_at(G, g, color, k), R1[color].at[g, k - 1],
            r1s.at[s, color, k - 1], r1r.at[s, color, k - 1], near(color, k),
        )

    def rs2(s, g, color, j):
        return copy(
            block_at(G, g, color, j, 1), R2[color].at[s, j - 1],
            r2s.at[s, color, j - 1], r2r.at[s, color, j - 1], far(color, j),
        )

    def rs1_start(s, g):
        for color in (0, 1):
            for k in range(1, ring[color]):
                rs1(s, g, color, k).start()

    def rs2_start(s, g):
        for color in (0, 1):
            for k in range(1, ring[color]):
                rs1(s, g, color, k).wait_recv()

            @pl.loop(0, group[color] // nh)
            def _(i):
                at = (g, z, i, slice(None), cols[0]) if color == 0 else (g, i, y, slice(None), cols[1])
                total = f32(G[at])
                for k in range(1, ring[color]):
                    total = total + f32(R1[color][g, k - 1, i])
                G[at] = bf(total)

        for color in (0, 1):
            for j in range(1, group[color]):
                rs2(s, g, color, j).start()

    def rs_finish(s, g):
        for color in (0, 1):
            for j in range(1, group[color]):
                rs2(s, g, color, j).wait_recv()
            total = f32(G[g, z, y, at_rows(h), cols[color]])
            for j in range(1, group[color]):
                total = total + f32(R2[color][s, j - 1])
            grads[s, :, cols[color]] = total

    def rs_sent(s, g):
        for color in (0, 1):
            for k in range(1, ring[color]):
                rs1(s, g, color, k).wait_send()
            for j in range(1, group[color]):
                rs2(s, g, color, j).wait_send()

    def g_copy(i, buf, step, recv):
        if step == 0:
            piece, dev = buf.at[l, oc if recv else c], core_peer
        elif step == 1:
            piece, dev = buf.at[ol if recv else l, c], line_peer
        else:
            piece, dev = buf.at[ol, oc if recv else c], core_peer
        return copy(piece, piece, gs.at[i, step], gr.at[i, step], dev)

    def gather_start(i, buf):
        g_copy(i, buf, 1, False).start()
        g_copy(i, buf, 0, False).start()

    def gather_relay(i, buf):
        g_copy(i, buf, 1, True).wait_recv()
        g_copy(i, buf, 2, False).start()

    def gather_wait(i, buf, step):
        g_copy(i, buf, step, True).wait_recv()

    def gather_sent(i, buf):
        for step in range(3):
            g_copy(i, buf, step, False).wait_send()

    def s_copy(i, step):
        src, dev = (
            (PS.at[ol, oc], core_peer),
            (SX, line_peer),
            (PS.at[l, oc], core_peer),
        )[step]
        return copy(src, RX.at[i % 2, step], ss.at[i, step], sr.at[i, step], dev)

    def scatter_far(i, compute):
        compute(ol)
        s_copy(i, 0).start()
        s_copy(i, 0).wait_recv()
        SX[...] = bf(f32(PS[ol, c]) + f32(RX[i % 2, 0]))
        s_copy(i, 1).start()

    def scatter_near(i, compute):
        compute(l)
        s_copy(i, 2).start()

    def scatter_result(i):
        s_copy(i, 2).wait_recv()
        s_copy(i, 1).wait_recv()
        total = f32(PS[l, c]) + f32(RX[i % 2, 2]) + f32(RX[i % 2, 1])
        for step in range(3):
            s_copy(i, step).wait_send()
        return total

    def pair_rows(i):
        return pl.ds(pl.multiple_of(i * pair, 128), pair)

    def back_product(left, s, lo, n):
        def compute(i):
            @pl.loop(0, nz)
            def _(b):
                w = W[s, b, :, :, pl.ds(lo, n)].reshape(slab, n)
                at = pl.ds(pl.multiple_of(b * slab, 128), slab)
                PS[i, :, :, at] = bf(dot(left(i), w, 1, 1)).reshape(2, pair // 2, slab)
        return compute

    def two(buf, i):
        return buf[i].reshape(pair, buf.shape[-1])

    def all_rows(buf, at):
        return buf[:, :, :, at].reshape(seq, -1)

    def grad_product(g, left, right, n, lo, tile):
        @pl.loop(0, nz)
        def _(b):
            a = all_rows(left, pl.ds(pl.multiple_of(b * slab, 128), slab)).T

            @pl.loop(0, n // tile)
            def _(t):
                at = pl.multiple_of(t * tile, 128)
                value = dot(a, right(pl.ds(at, tile))) * q_s
                G[g, b, :, :, pl.ds(lo + at, tile)] = bf(value).reshape(ny, nh * rows, tile)

    peers = [far(0, j) for j in range(1, group[0])]
    peers += [far(1, j) for j in range(1, group[1]) if j >= nh]
    peers += [{"c": oc}, {"l": ol}, {"l": ol, "c": oc}]
    barrier = pltpu.get_barrier_semaphore()
    for dev in peers:
        pl.semaphore_signal(barrier, inc=1, device_id=dev, device_id_type=pl.DeviceIdType.MESH)
    for s in range(3):
        own_block(s).start()
    m = [mod[i : i + 1, :] for i in range(6)]
    n1, r1 = normalize(f32(tok[...]))
    A1[l, c] = bf(n1 * (1.0 + m[1]) + m[0])
    DM[l, c] = bf(m[5] * f32(og[...]))
    for s in range(3):
        own_block(s).wait()
    pl.semaphore_wait(barrier, len(peers))

    ag1_start(0)
    gather_start(0, A1)
    ag1_start(1)
    ag1_start(2)
    ag2_start(0)
    gather_start(1, DM)
    gather_relay(0, A1)
    ag2_start(1)
    ag2_start(2)
    gather_relay(1, DM)
    gather_wait(0, A1, 0)
    gather_wait(0, A1, 2)

    ag_wait(0)

    @pl.loop(0, 3)
    def _(t):
        at = pl.ds(pl.multiple_of(t * own, 128), own)
        w = W[0, :, :, :, at].reshape(width, own)
        QKV[:, at] = bf(dot(A1[...].reshape(seq, width), w))

    def head(hd, i):
        return pl.ds(pl.multiple_of(i * own + hd * HEAD_DIM, 128), HEAD_DIM)

    @pl.loop(0, heads)
    def _(hd):
        s = dot(QKV[:, head(hd, 0)], QKV[:, head(hd, 1)], 1, 1) * scale
        e = jnp.exp(s - jnp.max(s, axis=-1, keepdims=True))
        p = bf(e * (1.0 / jnp.sum(e, axis=-1, keepdims=True)))
        PR[hd] = p
        O[:, head(hd, 0)] = bf(dot(p, QKV[:, head(hd, 2)]))

    out_product = back_product(lambda i: O[pair_rows(i), :], 0, 3 * own, own)
    scatter_far(0, out_product)
    scatter_near(0, out_product)
    mid = f32(tok[...]) + m[2] * scatter_result(0)
    MID[...] = mid
    n2, r2 = normalize(mid)
    A2[l, c] = bf(n2 * (1.0 + m[4]) + m[3])
    gather_start(2, A2)
    gather_wait(1, DM, 0)
    gather_wait(1, DM, 2)

    tile = 256

    def hidden(i):
        @pl.loop(0, width // tile)
        def _(t):
            at = pl.ds(pl.multiple_of(t * tile, 128), tile)
            g, d = gelu_pair(dot(two(A2, i), W[1, :, :, :, at].reshape(width, tile)))
            GG[i, :, :, at] = bf(g).reshape(2, pair // 2, tile)
            DU[i, :, :, at] = bf(d).reshape(2, pair // 2, tile)

    ag_wait(1)
    gather_wait(2, A2, 0)
    hidden(l)
    gather_relay(2, A2)
    gather_wait(2, A2, 2)
    hidden(ol)
    ag_wait(2)

    @pl.loop(0, width // tile)
    def _(t):
        at = pl.ds(pl.multiple_of(t * tile, 128), tile)
        dg = dot(DM[...].reshape(seq, width), W[2, :, :, :, at].reshape(width, tile))
        DU[:, :, :, at] = bf(f32(DU[:, :, :, at]) * dg.reshape(2, 2, pair // 2, tile))

    in_back = back_product(lambda i: two(DU, i), 1, 0, width)
    scatter_far(1, in_back)
    grad_product(0, DM, lambda at: all_rows(GG, at), width, 0, 2 * tile)
    rs1_start(2, 0)
    scatter_near(1, in_back)
    grad_product(1, A2, lambda at: all_rows(DU, at), width, 0, 2 * tile)
    rs1_start(1, 1)
    e2 = scatter_result(1) * (1.0 + m[4])
    n2, r2 = normalize(MID[...])
    dmid = f32(og[...]) + norm_back(n2, r2, e2)
    DX[...] = dmid
    DA[l, c] = bf(m[2] * dmid)
    gather_start(3, DA)

    ff_back = back_product(lambda i: two(GG, i), 2, 0, width)
    scatter_far(2, ff_back)
    scatter_near(2, ff_back)
    gather_relay(3, DA)
    gather_wait(3, DA, 0)
    gather_wait(3, DA, 2)

    DO[...] = bf(dot(DA[...].reshape(seq, width), W[0, :, :, :, pl.ds(3 * own, own)].reshape(width, own)))

    @pl.loop(0, heads)
    def _(hd):
        do = DO[:, head(hd, 0)]
        p = PR[hd]
        t = f32(p) * dot(do, QKV[:, head(hd, 2)], 1, 1)
        ds = bf(scale * (t - f32(p) * jnp.sum(t, axis=-1, keepdims=True)))
        DQKV[:, head(hd, 0)] = bf(dot(ds, QKV[:, head(hd, 1)]))
        DQKV[:, head(hd, 1)] = bf(dot(ds.T, QKV[:, head(hd, 0)]))
        DQKV[:, head(hd, 2)] = bf(dot(p.T, do))

    fin[...] = bf(MID[...] + m[5] * scatter_result(2))
    rs2_start(2, 0)
    qkv_back = back_product(lambda i: DQKV[pair_rows(i), :], 0, 0, 3 * own)
    scatter_far(3, qkv_back)
    rs_finish(2, 0)
    rs_sent(2, 0)
    grad_product(0, A1, lambda at: DQKV[:, at], 3 * own, 0, own)
    grad_product(0, DA, lambda at: O[:, at], own, 3 * own, own)
    rs1_start(0, 0)
    scatter_near(3, qkv_back)
    rs2_start(1, 1)
    e1 = scatter_result(3) * (1.0 + m[1])
    n1, r1 = normalize(f32(tok[...]))
    dxin[...] = DX[...] + norm_back(n1, r1, e1)
    rs2_start(0, 0)
    rs_finish(1, 1)
    rs_finish(0, 0)
    rs_sent(1, 1)
    rs_sent(0, 0)
    ag_sent()
    for i, buf in enumerate((A1, DM, A2, DA)):
        gather_sent(i, buf)


def step(dims, tokens, modulation, w_qkv, w_out, w_in, w_back, out_grad):
    nz, ny, nh = dims
    count, width = tokens.shape[1:]
    rows, own, ff = w_qkv.shape[1], w_qkv.shape[3], w_in.shape[2]
    assert ff == width and 4 * own == width
    seq = 4 * count
    heads = own // HEAD_DIM
    blocks = jnp.stack(
        [
            jnp.concatenate([w_qkv[0].reshape(rows, 3 * own), w_out[0].T], axis=1),
            w_in[0],
            w_back[0].T,
        ]
    )
    big = (nz, ny, nh * rows)
    half = width // 2
    vmem = pltpu.VMEM
    dma = pltpu.SemaphoreType.DMA
    tokens_buf = vmem((2, 2, count, width), BF)
    n1 = max(ny, nz) * nh - 1
    n2 = max(ny, nz) - 1
    scratch = [
        vmem((3, *big, width), BF),
        vmem((2, *big, width), BF),
        vmem((2, nz - 1, ny, nh * rows, half), BF),
        vmem((2, ny - 1, nz, nh * rows, half), BF),
        vmem((3, ny * nh - 1, rows, half), BF),
        vmem((3, nz * nh - 1, rows, half), BF),
        *[tokens_buf] * 6,
        vmem((seq, 3 * own), BF),
        vmem((seq, 3 * own), BF),
        vmem((seq, own), BF),
        vmem((seq, own), BF),
        vmem((heads, seq, seq), BF),
        tokens_buf,
        vmem((2, 3, count, width), BF),
        vmem((count, width), BF),
        vmem((count, width), F32),
        vmem((count, width), F32),
        dma((3,)),
        dma((3, 2, n1)), dma((3, 2, n1)),
        dma((3, 2, n2)), dma((3, 2, n2)),
        dma((3, 2, n2)), dma((3, 2, n2)),
        dma((3, 2, n1)), dma((3, 2, n1)),
        dma((4, 3)), dma((4, 3)),
        dma((4, 3)), dma((4, 3)),
    ]
    spec = pl.BlockSpec(memory_space=pltpu.VMEM)
    final, dx, grads = pl.pallas_call(
        functools.partial(kernel, dims),
        out_shape=(
            jax.ShapeDtypeStruct((count, width), BF),
            jax.ShapeDtypeStruct((count, width), F32),
            jax.ShapeDtypeStruct((3, rows, width), F32),
        ),
        in_specs=[spec, spec, pl.BlockSpec(memory_space=pl.ANY), spec],
        out_specs=(spec, spec, spec),
        scratch_shapes=scratch,
        compiler_params=pltpu.CompilerParams(
            collective_id=0, has_side_effects=True, vmem_limit_bytes=67043328
        ),
    )(tokens[0], modulation[0, 0], blocks, out_grad[0])
    return (
        final[None],
        dx[None],
        grads[0, :, : 3 * own].reshape(1, rows, 3, own),
        grads[0, :, 3 * own :].T[None],
        grads[1][None],
        grads[2].T[None],
    )


def solution(mesh):
    n = mesh.shape["fsdp"]
    nh = 2 if n > 4 else 1
    ny = int(round(math.sqrt(n // nh)))
    dims = (n // nh // ny, ny, nh)
    torus = Mesh(mesh.devices.reshape(*dims, 2, 2), AXES)
    fsdp, sp = AXES[:3], AXES[3:]
    placed = (
        P(fsdp, sp, None),
        P(fsdp, None, None, None),
        P(None, fsdp, None, sp),
        P(None, sp, fsdp),
        P(None, fsdp, sp),
        P(None, sp, fsdp),
        P(fsdp, sp, None),
    )
    return jax.shard_map(
        functools.partial(step, dims),
        mesh=torus,
        in_specs=placed,
        out_specs=(placed[0], *placed[:1], *placed[2:6]),
        check_vma=False,
    )
```

time: 1510 us -> 251 us (0.17)
  waiting for transfers between devices: 1390 us -> 0 us
  Pallas kernels: 0 us -> 238 us
  matrix products: 72.8 us -> 0 us
  other arithmetic: 25 us -> 0.82 us
    reduce_scatter x8 -> x0, waiting for transfers between devices: 976 us -> none  [the longest x4 893 us: reduce(): lax.psum_scatter(g, 'fsdp', scatter_dimension=0, tiled=True)]
    all_gather x8 -> x0, waiting for transfers between devices: 409 us -> none  [the longest x4 309 us: body(): lax.all_gather(w, 'fsdp', axis=0, tiled=True)]
    pallas_call x0 -> x1, Pallas kernels: none -> 238 us  [step(): pl.pallas_call(functools.partial(kernel, dims), out_shape=(jax.ShapeDtype...]
    dot_general x30 -> x0, matrix products: 72.8 us -> none  [dot(): lax.dot_general(a, b, (((ca,), (cb,)), ((), ())), preferred_element_type=...]
  transfers between devices with their start and end apart: 16 -> 0, of which waited for: 16 -> 0; matrix products, arithmetic and copies ran while one was open for 4% -> 0% of each run, Pallas kernels for 0% -> 0%
where the time goes in v2:
time: 251 us
  Pallas kernels  238 us (95%)
  local copies, waits for them, and re-layouts  10.8 us (4%)
    pallas_call x1, Pallas kernels, step(): pl.pallas_call(functools.partial(kernel, dims), out_shape=(jax.ShapeDtype...  238 us
    unnamed x15, local copies, waits for them, and re-layouts  5.7 us

profile of v2, /device:TPU:0, one launch (start us, length us, event | category | flops | bytes accessed | tf_op | source)
XLA Modules:
  0.0 250.6 jit_solution(472750780549743199)
XLA Ops:
  0.6 1.4 copy.23
  2.0 1.0 copy.15
  3.0 0.0 copy-start.4
  3.0 0.7 copy-done.4
  3.8 0.0 copy-start.2
  3.8 0.0 copy-start.3
  3.8 0.9 copy-done.2
  4.7 0.1 copy-done.3
  4.7 0.8 pad_maximum_fusion.wblk
  5.5 238.3 %shard_map.118 = (bf16[128,1536]{1,0:T(8,128)(2,1)}, f32[128,1536]{1,0:T(8,128)}, f32[3,48,1536]{2,1,0:T(8,128)}) custom-call(bf16[128,1536]{1,0:T(8,128)(2,1)} %bitcast.41, f32[6,1536]{1,0:T(8,128)} %bitcast.44, bf16[3,48,1536]{2,1,0:T(8,128)(2,1)} %pad_maximum_fusion.wblk, bf16[128,1536]{1,0:T(8,128)(2,1)} %bitcast.42), custom_call_target="tpu_custom_call" | custom-call | tf_op jit(solution)/shard_map/pallas_call | solution.py:469
  243.9 1.5 slice_bitcast_fusion.1
  245.4 0.9 slice.12
  246.3 0.0 copy-start.1
  246.3 2.0 slice_bitcast_fusion
  248.3 0.0 copy-start
  248.3 0.7 copy.22
  249.0 0.0 copy-done.1
  249.0 0.7 copy.26
  249.7 0.0 copy-done
  249.8 0.9 copy.27
  (2 shorter events, 0.0 us)
Async XLA Ops:
  3.0 0.8 copy-start.4
  3.8 0.9 copy-start.2
  3.8 1.0 copy-start.3
  246.3 2.7 %copy-start.1 = (bf16[128,1536]{1,0:T(8,128)(2,1)S(1)}, bf16[128,1536]{1,0:T(8,128)(2,1)}, u32[]{:S(2)}) copy-start(bf16[128,1536]{1,0:T(8,128)(2,1)} %get-tuple-element.9) | copy-start | bytes 1179652
  248.3 1.5 copy-start

commit v3 on v2

--- a/solution.py
+++ b/solution.py
@@ -50,14 +50,14 @@
 
 def kernel(
     dims, tok, mod, wblk, og, fin, dxin, grads,
-    W, G, R1A, R1B, R2A, R2B, A1, A2, DM, DA, GG, DU, QKV, DQKV, O, DO, PR, PS, RX, SX, MID, DX,
-    own_sem, a1s, a1r, a2s, a2r, r1s, r1r, r2s, r2r, gs, gr, ss, sr,
+    W, G, R1A, R1B, R2A, R2B, R3, A1, A2, DM, DA, GG, DU, QKV, DQKV, O, DO, PR, PS, RX, SX, MID, DX,
+    own_sem, a1s, a1r, a2s, a2r, a3s, a3r, a4s, a4r, r1s, r1r, r2s, r2r, r3s, r3r, gs, gr, ss, sr,
 ):
     nz, ny, nh = dims
     z, y, h, l, c = (lax.axis_index(a) for a in AXES)
     ol, oc = 1 - l, 1 - c
     rows, width = wblk.shape[1:]
-    half = width // 2
+    half, quarter = width // 2, width // 4
     seq = QKV.shape[0]
     pair = seq // 2
     own = QKV.shape[1] // 3
@@ -85,118 +85,156 @@
     def at_rows(i):
         return pl.ds(pl.multiple_of(i * rows, 16), rows)
 
-    group = (ny * nh, nz * nh)
-    ring = (nz, ny)
-
-    def far(color, j):
-        d, dh = j // nh, j % nh
-        return {"y": yy(d), "h": hh(dh)} if color == 0 else {"z": zz(d), "h": hh(dh)}
-
-    def near(color, k):
-        return {"z": zz(k)} if color == 0 else {"y": yy(k)}
-
     core_peer = {"c": oc}
     line_peer = {"l": ol}
+    pair_peer = {"h": 1 - h}
+    ring_cols = ((pl.ds(0, quarter), pl.ds(quarter, quarter)), (pl.ds(half, quarter), pl.ds(half + quarter, quarter)))
+    local_cols = (pl.ds(0, quarter), pl.ds(quarter, quarter))
+
+    def last(color, k):
+        return {"z": zz(k)} if color == 0 else {"y": yy(k)}
+
+    def mid_dev(color, k):
+        return last(1 - color, k)
+
+    def slab_at(buf, color, k, at):
+        return buf.at[zz(k), :, :, at] if color == 0 else buf.at[:, yy(k), :, at]
+
+    def line_at(buf, color, k):
+        return buf.at[z, yy(k), :, cols[0]] if color == 0 else buf.at[zz(k), y, :, cols[1]]
 
     def own_block(s):
         return pltpu.make_async_copy(wblk.at[s], W.at[s, z, y, at_rows(h)], own_sem.at[s])
 
-    def block_at(buf, s, color, j, sign):
-        d, dh = j // nh, j % nh
-        if color == 0:
-            return buf.at[s, z, yy(sign * d), at_rows(hh(sign * dh)), cols[0]]
-        return buf.at[s, zz(sign * d), y, at_rows(hh(sign * dh)), cols[1]]
-
-    def slab_at(buf, s, color, k):
-        if color == 0:
-            return buf.at[s, zz(k), :, :, cols[0]]
-        return buf.at[s, :, yy(k), :, cols[1]]
-
-    def ag1(s, color, j, recv):
-        piece = block_at(W, s, color, j if recv else 0, -1)
-        return copy(piece, piece, a1s.at[s, color, j - 1], a1r.at[s, color, j - 1], far(color, j))
-
-    def ag2(s, color, k, recv):
-        piece = slab_at(W, s, color, -k if recv else 0)
-        return copy(piece, piece, a2s.at[s, color, k - 1], a2r.at[s, color, k - 1], near(color, k))
-
-    def ag1_start(s):
-        for color in (0, 1):
-            for j in range(1, group[color]):
-                ag1(s, color, j, False).start()
-
-    def ag2_start(s):
-        for color in (0, 1):
-            for j in range(1, group[color]):
-                ag1(s, color, j, True).wait_recv()
-            for k in range(1, ring[color]):
-                ag2(s, color, k, False).start()
+    def ag_pair(s, recv):
+        piece = W.at[s, z, y, at_rows(1 - h if recv else h)]
+        return copy(piece, piece, a1s.at[s], a1r.at[s], pair_peer)
+
+    def ag_mid(s, color, k, recv):
+        piece = line_at(W.at[s], color, -k if recv else 0)
+        return copy(piece, piece, a2s.at[s, color, k - 1], a2r.at[s, color, k - 1], mid_dev(color, k))
+
+    def ag_last(s, color, d, recv):
+        k = 1 - 2 * d
+        piece = slab_at(W.at[s], color, -k if recv else 0, cols[color])
+        return copy(piece, piece, a3s.at[s, color, d], a3r.at[s, color, d], last(color, k))
+
+    def ag_relay(s, color, d, recv):
+        k = 1 - 2 * d
+        piece = slab_at(W.at[s], color, 2 if recv else -k, ring_cols[color][d])
+        return copy(piece, piece, a4s.at[s, color, d], a4r.at[s, color, d], last(color, k))
+
+    def ag_mid_start(s):
+        ag_pair(s, True).wait_recv()
+        for color in (0, 1):
+            for k in range(1, 4):
+                ag_mid(s, color, k, False).start()
+
+    def ag_last_start(s):
+        for color in (0, 1):
+            for k in range(1, 4):
+                ag_mid(s, color, k, True).wait_recv()
+            for d in (0, 1):
+                ag_last(s, color, d, False).start()
+
+    def ag_relay_start(s):
+        for color in (0, 1):
+            for d in (0, 1):
+                ag_last(s, color, d, True).wait_recv()
+                ag_relay(s, color, d, False).start()
 
     def ag_wait(s):
         for color in (0, 1):
-            for k in range(1, ring[color]):
-                ag2(s, color, k, True).wait_recv()
-
-    def ag_sent():
-        for s in range(3):
-            for color in (0, 1):
-                for j in range(1, group[color]):
-                    ag1(s, color, j, False).wait_send()
-                for k in range(1, ring[color]):
-                    ag2(s, color, k, False).wait_send()
+            for d in (0, 1):
+                ag_relay(s, color, d, True).wait_recv()
+
+    def ag_sent(s):
+        ag_pair(s, False).wait_send()
+        for color in (0, 1):
+            for k in range(1, 4):
+                ag_mid(s, color, k, False).wait_send()
+            for d in (0, 1):
+                ag_last(s, color, d, False).wait_send()
+                ag_relay(s, color, d, False).wait_send()
 
     R1 = (R1A, R1B)
     R2 = (R2A, R2B)
-
-    def rs1(s, g, color, k):
+    parts = (W.at[1], G.at[1], G.at[0])
+
+    def rs_ring(s, color, d, kind):
+        k = 1 - 2 * d
+        q = 1 - d if kind == 1 else d
+        src = slab_at(parts[s], color, 2 if kind == 0 else k, ring_cols[color][q])
+        dst = R1[color].at[s, 2 if kind == 0 else d, :, :, local_cols[q]]
+        return copy(src, dst, r1s.at[s, color, d, kind], r1r.at[s, color, d, kind], last(color, k))
+
+    def rs_mid(s, color, k):
         return copy(
-            slab_at(G, g, color, k), R1[color].at[g, k - 1],
-            r1s.at[s, color, k - 1], r1r.at[s, color, k - 1], near(color, k),
+            line_at(parts[s], color, k), R2[color].at[s, k - 1],
+            r2s.at[s, color, k - 1], r2r.at[s, color, k - 1], mid_dev(color, k),
         )
 
-    def rs2(s, g, color, j):
-        return copy(
-            block_at(G, g, color, j, 1), R2[color].at[s, j - 1],
-            r2s.at[s, color, j - 1], r2r.at[s, color, j - 1], far(color, j),
-        )
-
-    def rs1_start(s, g):
-        for color in (0, 1):
-            for k in range(1, ring[color]):
-                rs1(s, g, color, k).start()
-
-    def rs2_start(s, g):
-        for color in (0, 1):
-            for k in range(1, ring[color]):
-                rs1(s, g, color, k).wait_recv()
-
-            @pl.loop(0, group[color] // nh)
+    def rs_pair(s):
+        return copy(parts[s].at[z, y, at_rows(1 - h)], R3.at[s], r3s.at[s], r3r.at[s], pair_peer)
+
+    def rs_start(s):
+        for kind in (0, 1):
+            for color in (0, 1):
+                for d in (0, 1):
+                    rs_ring(s, color, d, kind).start()
+
+    def rs_combine(s):
+        for color in (0, 1):
+            for d in (0, 1):
+                rs_ring(s, color, d, 0).wait_recv()
+                k = 1 - 2 * d
+
+                @pl.loop(0, 4)
+                def _(i):
+                    at = (zz(k), i) if color == 0 else (i, yy(k))
+                    at = (*at, slice(None), ring_cols[color][d])
+                    parts[s][at] = bf(f32(parts[s][at]) + f32(R1[color][s, 2, i, :, local_cols[d]]))
+
+                rs_ring(s, color, d, 2).start()
+
+    def rs_mid_start(s):
+        for color in (0, 1):
+            for d in (0, 1):
+                for kind in (1, 2):
+                    rs_ring(s, color, d, kind).wait_recv()
+
+            @pl.loop(0, 4)
             def _(i):
-                at = (g, z, i, slice(None), cols[0]) if color == 0 else (g, i, y, slice(None), cols[1])
-                total = f32(G[at])
-                for k in range(1, ring[color]):
-                    total = total + f32(R1[color][g, k - 1, i])
-                G[at] = bf(total)
-
-        for color in (0, 1):
-            for j in range(1, group[color]):
-                rs2(s, g, color, j).start()
-
-    def rs_finish(s, g):
-        for color in (0, 1):
-            for j in range(1, group[color]):
-                rs2(s, g, color, j).wait_recv()
-            total = f32(G[g, z, y, at_rows(h), cols[color]])
-            for j in range(1, group[color]):
-                total = total + f32(R2[color][s, j - 1])
-            grads[s, :, cols[color]] = total
-
-    def rs_sent(s, g):
-        for color in (0, 1):
-            for k in range(1, ring[color]):
-                rs1(s, g, color, k).wait_send()
-            for j in range(1, group[color]):
-                rs2(s, g, color, j).wait_send()
+                at = (z, i) if color == 0 else (i, y)
+                at = (*at, slice(None), cols[color])
+                parts[s][at] = bf(f32(parts[s][at]) + f32(R1[color][s, 0, i]) + f32(R1[color][s, 1, i]))
+
+            for k in range(1, 4):
+                rs_mid(s, color, k).start()
+
+    def rs_pair_start(s):
+        for color in (0, 1):
+            for k in range(1, 4):
+                rs_mid(s, color, k).wait_recv()
+            at = (z, y, slice(None), cols[color])
+            total = f32(parts[s][at])
+            for k in range(3):
+                total = total + f32(R2[color][s, k])
+            parts[s][at] = bf(total)
+        rs_pair(s).start()
+
+    def rs_finish(s):
+        rs_pair(s).wait_recv()
+        grads[s] = f32(parts[s][z, y, at_rows(h), :]) + f32(R3[s])
+
+    def rs_sent(s):
+        for color in (0, 1):
+            for d in (0, 1):
+                for kind in (0, 1, 2):
+                    rs_ring(s, color, d, kind).wait_send()
+            for k in range(1, 4):
+                rs_mid(s, color, k).wait_send()
+        rs_pair(s).wait_send()
 
     def g_copy(i, buf, step, recv):
         if step == 0:
@@ -267,7 +305,7 @@
     def all_rows(buf, at):
         return buf[:, :, :, at].reshape(seq, -1)
 
-    def grad_product(g, left, right, n, lo, tile):
+    def grad_product(s, left, right, n, lo, tile):
         @pl.loop(0, nz)
         def _(b):
             a = all_rows(left, pl.ds(pl.multiple_of(b * slab, 128), slab)).T
@@ -276,11 +314,10 @@
             def _(t):
                 at = pl.multiple_of(t * tile, 128)
                 value = dot(a, right(pl.ds(at, tile))) * q_s
-                G[g, b, :, :, pl.ds(lo + at, tile)] = bf(value).reshape(ny, nh * rows, tile)
-
-    peers = [far(0, j) for j in range(1, group[0])]
-    peers += [far(1, j) for j in range(1, group[1]) if j >= nh]
-    peers += [{"c": oc}, {"l": ol}, {"l": ol, "c": oc}]
+                parts[s][b, :, :, pl.ds(lo + at, tile)] = bf(value).reshape(ny, nh * rows, tile)
+
+    peers = [{"z": zz(k)} for k in range(1, 4)] + [{"y": yy(k)} for k in range(1, 4)]
+    peers += [pair_peer, core_peer, line_peer, {"l": ol, "c": oc}]
     barrier = pltpu.get_barrier_semaphore()
     for dev in peers:
         pl.semaphore_signal(barrier, inc=1, device_id=dev, device_id_type=pl.DeviceIdType.MESH)
@@ -294,15 +331,18 @@
         own_block(s).wait()
     pl.semaphore_wait(barrier, len(peers))
 
-    ag1_start(0)
+    ag_pair(0, False).start()
     gather_start(0, A1)
-    ag1_start(1)
-    ag1_start(2)
-    ag2_start(0)
+    ag_pair(1, False).start()
+    ag_pair(2, False).start()
+    ag_mid_start(0)
+    ag_last_start(0)
+    ag_mid_start(1)
+    gather_relay(0, A1)
     gather_start(1, DM)
-    gather_relay(0, A1)
-    ag2_start(1)
-    ag2_start(2)
+    ag_relay_start(0)
+    ag_mid_start(2)
+    ag_last_start(1)
     gather_relay(1, DM)
     gather_wait(0, A1, 0)
     gather_wait(0, A1, 2)
@@ -329,6 +369,8 @@
     out_product = back_product(lambda i: O[pair_rows(i), :], 0, 3 * own, own)
     scatter_far(0, out_product)
     scatter_near(0, out_product)
+    ag_last_start(2)
+    ag_relay_start(1)
     mid = f32(tok[...]) + m[2] * scatter_result(0)
     MID[...] = mid
     n2, r2 = normalize(mid)
@@ -353,6 +395,7 @@
     gather_relay(2, A2)
     gather_wait(2, A2, 2)
     hidden(ol)
+    ag_relay_start(2)
     ag_wait(2)
 
     @pl.loop(0, width // tile)
@@ -363,11 +406,12 @@
 
     in_back = back_product(lambda i: two(DU, i), 1, 0, width)
     scatter_far(1, in_back)
-    grad_product(0, DM, lambda at: all_rows(GG, at), width, 0, 2 * tile)
-    rs1_start(2, 0)
+    grad_product(2, DM, lambda at: all_rows(GG, at), width, 0, 2 * tile)
+    rs_start(2)
     scatter_near(1, in_back)
     grad_product(1, A2, lambda at: all_rows(DU, at), width, 0, 2 * tile)
-    rs1_start(1, 1)
+    rs_start(1)
+    rs_combine(2)
     e2 = scatter_result(1) * (1.0 + m[4])
     n2, r2 = normalize(MID[...])
     dmid = f32(og[...]) + norm_back(n2, r2, e2)
@@ -378,6 +422,7 @@
     ff_back = back_product(lambda i: two(GG, i), 2, 0, width)
     scatter_far(2, ff_back)
     scatter_near(2, ff_back)
+    rs_combine(1)
     gather_relay(3, DA)
     gather_wait(3, DA, 0)
     gather_wait(3, DA, 2)
@@ -394,26 +439,31 @@
         DQKV[:, head(hd, 1)] = bf(dot(ds.T, QKV[:, head(hd, 0)]))
         DQKV[:, head(hd, 2)] = bf(dot(p.T, do))
 
+    ag_sent(1)
+    grad_product(0, A1, lambda at: DQKV[:, at], 3 * own, 0, own)
+    grad_product(0, DA, lambda at: O[:, at], own, 3 * own, own)
+    rs_start(0)
     fin[...] = bf(MID[...] + m[5] * scatter_result(2))
-    rs2_start(2, 0)
     qkv_back = back_product(lambda i: DQKV[pair_rows(i), :], 0, 0, 3 * own)
     scatter_far(3, qkv_back)
-    rs_finish(2, 0)
-    rs_sent(2, 0)
-    grad_product(0, A1, lambda at: DQKV[:, at], 3 * own, 0, own)
-    grad_product(0, DA, lambda at: O[:, at], own, 3 * own, own)
-    rs1_start(0, 0)
     scatter_near(3, qkv_back)
-    rs2_start(1, 1)
+    rs_mid_start(2)
+    rs_combine(0)
     e1 = scatter_result(3) * (1.0 + m[1])
     n1, r1 = normalize(f32(tok[...]))
     dxin[...] = DX[...] + norm_back(n1, r1, e1)
-    rs2_start(0, 0)
-    rs_finish(1, 1)
-    rs_finish(0, 0)
-    rs_sent(1, 1)
-    rs_sent(0, 0)
-    ag_sent()
+    rs_mid_start(1)
+    rs_pair_start(2)
+    rs_mid_start(0)
+    rs_pair_start(1)
+    rs_finish(2)
+    rs_pair_start(0)
+    rs_finish(1)
+    rs_finish(0)
+    for s in range(3):
+        rs_sent(s)
+    ag_sent(0)
+    ag_sent(2)
     for i, buf in enumerate((A1, DM, A2, DA)):
         gather_sent(i, buf)
 
@@ -437,15 +487,14 @@
     vmem = pltpu.VMEM
     dma = pltpu.SemaphoreType.DMA
     tokens_buf = vmem((2, 2, count, width), BF)
-    n1 = max(ny, nz) * nh - 1
-    n2 = max(ny, nz) - 1
     scratch = [
         vmem((3, *big, width), BF),
         vmem((2, *big, width), BF),
-        vmem((2, nz - 1, ny, nh * rows, half), BF),
-        vmem((2, ny - 1, nz, nh * rows, half), BF),
-        vmem((3, ny * nh - 1, rows, half), BF),
-        vmem((3, nz * nh - 1, rows, half), BF),
+        vmem((3, 3, 4, nh * rows, half), BF),
+        vmem((3, 3, 4, nh * rows, half), BF),
+        vmem((3, 3, nh * rows, half), BF),
+        vmem((3, 3, nh * rows, half), BF),
+        vmem((3, rows, width), BF),
         *[tokens_buf] * 6,
         vmem((seq, 3 * own), BF),
         vmem((seq, 3 * own), BF),
@@ -458,10 +507,13 @@
         vmem((count, width), F32),
         vmem((count, width), F32),
         dma((3,)),
-        dma((3, 2, n1)), dma((3, 2, n1)),
-        dma((3, 2, n2)), dma((3, 2, n2)),
-        dma((3, 2, n2)), dma((3, 2, n2)),
-        dma((3, 2, n1)), dma((3, 2, n1)),
+        dma((3,)), dma((3,)),
+        dma((3, 2, 3)), dma((3, 2, 3)),
+        dma((3, 2, 2)), dma((3, 2, 2)),
+        dma((3, 2, 2)), dma((3, 2, 2)),
+        dma((3, 2, 2, 3)), dma((3, 2, 2, 3)),
+        dma((3, 2, 3)), dma((3, 2, 3)),
+        dma((3,)), dma((3,)),
         dma((4, 3)), dma((4, 3)),
         dma((4, 3)), dma((4, 3)),
     ]
@@ -491,10 +543,8 @@
 
 
 def solution(mesh):
-    n = mesh.shape["fsdp"]
-    nh = 2 if n > 4 else 1
-    ny = int(round(math.sqrt(n // nh)))
-    dims = (n // nh // ny, ny, nh)
+    dims = (4, 4, 2)
+    assert mesh.shape["fsdp"] == 32 and mesh.shape["sp"] == 4
     torus = Mesh(mesh.devices.reshape(*dims, 2, 2), AXES)
     fsdp, sp = AXES[:3], AXES[3:]
     placed = (

time: 251 us -> 214 us (0.85)
  Pallas kernels: 238 us -> 202 us
    pallas_call x1, Pallas kernels: 238 us -> 202 us  [step(): pl.pallas_call(functools.partial(kernel, dims), out_shape=(jax.ShapeDtype...]
where the time goes in v3:
time: 214 us
  Pallas kernels  202 us (94%)
  local copies, waits for them, and re-layouts  10.8 us (5%)
    pallas_call x1, Pallas kernels, step(): pl.pallas_call(functools.partial(kernel, dims), out_shape=(jax.ShapeDtype...  202 us
    unnamed x15, local copies, waits for them, and re-layouts  5.7 us

profile of v3, /device:TPU:0, one launch (start us, length us, event | category | flops | bytes accessed | tf_op | source)
XLA Modules:
  0.0 213.9 jit_solution(10700282722254063690)
XLA Ops:
  0.6 1.4 copy.23
  2.0 1.0 copy.15
  3.0 0.0 copy-start.4
  3.0 0.7 copy-done.4
  3.8 0.0 copy-start.2
  3.8 0.0 copy-start.3
  3.8 0.9 copy-done.2
  4.7 0.1 copy-done.3
  4.7 0.8 pad_maximum_fusion.wblk
  5.5 201.6 %shard_map.118 = (bf16[128,1536]{1,0:T(8,128)(2,1)}, f32[128,1536]{1,0:T(8,128)}, f32[3,48,1536]{2,1,0:T(8,128)}) custom-call(bf16[128,1536]{1,0:T(8,128)(2,1)} %bitcast.41, f32[6,1536]{1,0:T(8,128)} %bitcast.44, bf16[3,48,1536]{2,1,0:T(8,128)(2,1)} %pad_maximum_fusion.wblk, bf16[128,1536]{1,0:T(8,128)(2,1)} %bitcast.42), custom_call_target="tpu_custom_call" | custom-call | tf_op jit(solution)/shard_map/pallas_call | solution.py:521
  207.1 1.5 slice_bitcast_fusion.1
  208.6 0.9 slice.12
  209.6 0.0 copy-start.1
  209.6 2.0 slice_bitcast_fusion
  211.6 0.0 copy-start
  211.6 0.7 copy.22
  212.3 0.0 copy-done.1
  212.3 0.7 copy.26
  213.0 0.0 copy-done
  213.0 0.9 copy.27
  (2 shorter events, 0.0 us)
Async XLA Ops:
  3.0 0.8 copy-start.4
  3.8 0.9 copy-start.2
  3.8 1.0 copy-start.3
  209.6 2.7 %copy-start.1 = (bf16[128,1536]{1,0:T(8,128)(2,1)S(1)}, bf16[128,1536]{1,0:T(8,128)(2,1)}, u32[]{:S(2)}) copy-start(bf16[128,1536]{1,0:T(8,128)(2,1)} %get-tuple-element.9) | copy-start | bytes 1179652
  211.6 1.5 copy-start

commit v4 on v3

--- a/solution.py
+++ b/solution.py
@@ -49,15 +49,15 @@
 
 
 def kernel(
-    dims, tok, mod, wblk, og, fin, dxin, grads,
+    dims, tok_in, mod_in, wq_in, wo_in, wi_in, wb_in, og_in, fin, dxin, grads,
     W, G, R1A, R1B, R2A, R2B, R3, A1, A2, DM, DA, GG, DU, QKV, DQKV, O, DO, PR, PS, RX, SX, MID, DX,
-    own_sem, a1s, a1r, a2s, a2r, a3s, a3r, a4s, a4r, r1s, r1r, r2s, r2r, r3s, r3r, gs, gr, ss, sr,
+    tok, mod, og, in_sem, a1s, a1r, a2s, a2r, a3s, a3r, a4s, a4r, r1s, r1r, r2s, r2r, r3s, r3r, gs, gr, ss, sr,
 ):
     nz, ny, nh = dims
     z, y, h, l, c = (lax.axis_index(a) for a in AXES)
     ol, oc = 1 - l, 1 - c
-    rows, width = wblk.shape[1:]
-    half, quarter = width // 2, width // 4
+    rows, width = wi_in.shape
+    half = width // 2
     seq = QKV.shape[0]
     pair = seq // 2
     own = QKV.shape[1] // 3
@@ -88,8 +88,7 @@
     core_peer = {"c": oc}
     line_peer = {"l": ol}
     pair_peer = {"h": 1 - h}
-    ring_cols = ((pl.ds(0, quarter), pl.ds(quarter, quarter)), (pl.ds(half, quarter), pl.ds(half + quarter, quarter)))
-    local_cols = (pl.ds(0, quarter), pl.ds(quarter, quarter))
+    halves = (pl.ds(0, 2), pl.ds(2, 2))
 
     def last(color, k):
         return {"z": zz(k)} if color == 0 else {"y": yy(k)}
@@ -97,22 +96,19 @@
     def mid_dev(color, k):
         return last(1 - color, k)
 
-    def slab_at(buf, color, k, at):
-        return buf.at[zz(k), :, :, at] if color == 0 else buf.at[:, yy(k), :, at]
-
-    def line_at(buf, color, k):
-        return buf.at[z, yy(k), :, cols[0]] if color == 0 else buf.at[zz(k), y, :, cols[1]]
-
-    def own_block(s):
-        return pltpu.make_async_copy(wblk.at[s], W.at[s, z, y, at_rows(h)], own_sem.at[s])
+    def slab_at(buf, color, k, at, part=slice(None)):
+        return buf.at[zz(k), part, :, at] if color == 0 else buf.at[part, yy(k), :, at]
+
+    def line_at(buf, color, k, at, part=slice(None)):
+        return buf.at[z, yy(k), part, at] if color == 0 else buf.at[zz(k), y, part, at]
 
     def ag_pair(s, recv):
         piece = W.at[s, z, y, at_rows(1 - h if recv else h)]
         return copy(piece, piece, a1s.at[s], a1r.at[s], pair_peer)
 
-    def ag_mid(s, color, k, recv):
-        piece = line_at(W.at[s], color, -k if recv else 0)
-        return copy(piece, piece, a2s.at[s, color, k - 1], a2r.at[s, color, k - 1], mid_dev(color, k))
+    def ag_mid(s, color, k, which, recv):
+        piece = line_at(W.at[s], color, -k if recv else 0, cols[color], at_rows(h if which == 0 else 1 - h))
+        return copy(piece, piece, a2s.at[s, color, k - 1, which], a2r.at[s, color, k - 1, which], mid_dev(color, k))
 
     def ag_last(s, color, d, recv):
         k = 1 - 2 * d
@@ -121,19 +117,21 @@
 
     def ag_relay(s, color, d, recv):
         k = 1 - 2 * d
-        piece = slab_at(W.at[s], color, 2 if recv else -k, ring_cols[color][d])
+        piece = slab_at(W.at[s], color, 2 if recv else -k, cols[color], halves[d])
         return copy(piece, piece, a4s.at[s, color, d], a4r.at[s, color, d], last(color, k))
 
-    def ag_mid_start(s):
-        ag_pair(s, True).wait_recv()
-        for color in (0, 1):
-            for k in range(1, 4):
-                ag_mid(s, color, k, False).start()
+    def ag_mid_start(s, which):
+        if which:
+            ag_pair(s, True).wait_recv()
+        for k in (1, 3, 2):
+            for color in (0, 1):
+                ag_mid(s, color, k, which, False).start()
 
     def ag_last_start(s):
         for color in (0, 1):
-            for k in range(1, 4):
-                ag_mid(s, color, k, True).wait_recv()
+            for which in (0, 1):
+                for k in range(1, 4):
+                    ag_mid(s, color, k, which, True).wait_recv()
             for d in (0, 1):
                 ag_last(s, color, d, False).start()
 
@@ -151,31 +149,51 @@
     def ag_sent(s):
         ag_pair(s, False).wait_send()
         for color in (0, 1):
-            for k in range(1, 4):
-                ag_mid(s, color, k, False).wait_send()
+            for which in (0, 1):
+                for k in range(1, 4):
+                    ag_mid(s, color, k, which, False).wait_send()
             for d in (0, 1):
                 ag_last(s, color, d, False).wait_send()
                 ag_relay(s, color, d, False).wait_send()
 
     R1 = (R1A, R1B)
     R2 = (R2A, R2B)
-    parts = (W.at[1], G.at[1], G.at[0])
+    parts = (G.at[0], G.at[1], W.at[1], W.at[1])
+    slots = (2, 1, 0, 0)
+    full = 3 * own
+    local_cols = (
+        (pl.ds(0, half), pl.ds(0, half)),
+        (pl.ds(0, half), pl.ds(0, half)),
+        (pl.ds(half - 256, 256), pl.ds(half - 128, 128)),
+        (pl.ds(0, half - 256), pl.ds(0, half - 128)),
+    )
+    grad_cols = (
+        (cols[0], cols[1]),
+        (cols[0], cols[1]),
+        (pl.ds(full, 256), pl.ds(full + 256, 128)),
+        (pl.ds(0, half - 256), pl.ds(half - 256, half - 128)),
+    )
+    pair_cols = (pl.ds(0, width), pl.ds(0, width), pl.ds(full, own), pl.ds(0, full))
 
     def rs_ring(s, color, d, kind):
         k = 1 - 2 * d
-        q = 1 - d if kind == 1 else d
-        src = slab_at(parts[s], color, 2 if kind == 0 else k, ring_cols[color][q])
-        dst = R1[color].at[s, 2 if kind == 0 else d, :, :, local_cols[q]]
+        part = halves[1 - d if kind == 1 else d]
+        src = slab_at(parts[s], color, 2 if kind == 0 else k, grad_cols[s][color], part)
+        dst = R1[color].at[slots[s], 2 if kind == 0 else d, part, :, local_cols[s][color]]
         return copy(src, dst, r1s.at[s, color, d, kind], r1r.at[s, color, d, kind], last(color, k))
 
     def rs_mid(s, color, k):
         return copy(
-            line_at(parts[s], color, k), R2[color].at[s, k - 1],
+            line_at(parts[s], color, k, grad_cols[s][color]),
+            R2[color].at[slots[s], k - 1, :, local_cols[s][color]],
             r2s.at[s, color, k - 1], r2r.at[s, color, k - 1], mid_dev(color, k),
         )
 
     def rs_pair(s):
-        return copy(parts[s].at[z, y, at_rows(1 - h)], R3.at[s], r3s.at[s], r3r.at[s], pair_peer)
+        return copy(
+            parts[s].at[z, y, at_rows(1 - h), pair_cols[s]], R3.at[slots[s], :, pair_cols[s]],
+            r3s.at[s], r3r.at[s], pair_peer,
+        )
 
     def rs_start(s):
         for kind in (0, 1):
@@ -189,11 +207,12 @@
                 rs_ring(s, color, d, 0).wait_recv()
                 k = 1 - 2 * d
 
-                @pl.loop(0, 4)
+                @pl.loop(2 * d, 2 * d + 2)
                 def _(i):
                     at = (zz(k), i) if color == 0 else (i, yy(k))
-                    at = (*at, slice(None), ring_cols[color][d])
-                    parts[s][at] = bf(f32(parts[s][at]) + f32(R1[color][s, 2, i, :, local_cols[d]]))
+                    at = (*at, slice(None), grad_cols[s][color])
+                    came = R1[color][slots[s], 2, i, :, local_cols[s][color]]
+                    parts[s][at] = bf(f32(parts[s][at]) + f32(came))
 
                 rs_ring(s, color, d, 2).start()
 
@@ -206,26 +225,30 @@
             @pl.loop(0, 4)
             def _(i):
                 at = (z, i) if color == 0 else (i, y)
-                at = (*at, slice(None), cols[color])
-                parts[s][at] = bf(f32(parts[s][at]) + f32(R1[color][s, 0, i]) + f32(R1[color][s, 1, i]))
-
-            for k in range(1, 4):
+                at = (*at, slice(None), grad_cols[s][color])
+                total = f32(parts[s][at])
+                for d in (0, 1):
+                    total = total + f32(R1[color][slots[s], d, i, :, local_cols[s][color]])
+                parts[s][at] = bf(total)
+
+            for k in (1, 3, 2):
                 rs_mid(s, color, k).start()
 
     def rs_pair_start(s):
         for color in (0, 1):
             for k in range(1, 4):
                 rs_mid(s, color, k).wait_recv()
-            at = (z, y, slice(None), cols[color])
+            at = (z, y, slice(None), grad_cols[s][color])
             total = f32(parts[s][at])
             for k in range(3):
-                total = total + f32(R2[color][s, k])
+                total = total + f32(R2[color][slots[s], k, :, local_cols[s][color]])
             parts[s][at] = bf(total)
         rs_pair(s).start()
 
     def rs_finish(s):
         rs_pair(s).wait_recv()
-        grads[s] = f32(parts[s][z, y, at_rows(h), :]) + f32(R3[s])
+        at = pair_cols[s]
+        grads[slots[s], :, at] = f32(parts[s][z, y, at_rows(h), at]) + f32(R3[slots[s], :, at])
 
     def rs_sent(s):
         for color in (0, 1):
@@ -321,31 +344,37 @@
     barrier = pltpu.get_barrier_semaphore()
     for dev in peers:
         pl.semaphore_signal(barrier, inc=1, device_id=dev, device_id_type=pl.DeviceIdType.MESH)
-    for s in range(3):
-        own_block(s).start()
-    m = [mod[i : i + 1, :] for i in range(6)]
+    mine = at_rows(h)
+    moves = [(wq_in.at[i], W.at[0, z, y, mine, pl.ds(i * own, own)]) for i in range(3)]
+    moves += [(wo_in, W.at[0, z, y, mine, pl.ds(3 * own, own)])]
+    moves += [(wi_in, W.at[1, z, y, mine]), (wb_in, W.at[2, z, y, mine])]
+    moves += [(tok_in, tok), (og_in, og), (mod_in, mod)]
+    loads = [pltpu.make_async_copy(src, dst, in_sem.at[i]) for i, (src, dst) in enumerate(moves)]
+    for load in loads:
+        load.start()
+    for load in loads:
+        load.wait()
+    m = [mod[i] for i in range(6)]
     n1, r1 = normalize(f32(tok[...]))
     A1[l, c] = bf(n1 * (1.0 + m[1]) + m[0])
     DM[l, c] = bf(m[5] * f32(og[...]))
+    pl.semaphore_wait(barrier, len(peers))
+
     for s in range(3):
-        own_block(s).wait()
-    pl.semaphore_wait(barrier, len(peers))
-
-    ag_pair(0, False).start()
+        ag_pair(s, False).start()
+        ag_mid_start(s, 0)
     gather_start(0, A1)
-    ag_pair(1, False).start()
-    ag_pair(2, False).start()
-    ag_mid_start(0)
+    ag_mid_start(0, 1)
+    ag_mid_start(1, 1)
     ag_last_start(0)
-    ag_mid_start(1)
+    ag_mid_start(2, 1)
     gather_relay(0, A1)
     gather_start(1, DM)
     ag_relay_start(0)
-    ag_mid_start(2)
     ag_last_start(1)
-    gather_relay(1, DM)
     gather_wait(0, A1, 0)
     gather_wait(0, A1, 2)
+    gather_relay(1, DM)
 
     ag_wait(0)
 
@@ -367,9 +396,9 @@
         O[:, head(hd, 0)] = bf(dot(p, QKV[:, head(hd, 2)]))
 
     out_product = back_product(lambda i: O[pair_rows(i), :], 0, 3 * own, own)
+    ag_last_start(2)
     scatter_far(0, out_product)
     scatter_near(0, out_product)
-    ag_last_start(2)
     ag_relay_start(1)
     mid = f32(tok[...]) + m[2] * scatter_result(0)
     MID[...] = mid
@@ -389,13 +418,15 @@
             GG[i, :, :, at] = bf(g).reshape(2, pair // 2, tile)
             DU[i, :, :, at] = bf(d).reshape(2, pair // 2, tile)
 
+    ag_relay_start(2)
+    gather_relay(2, A2)
+    gather_wait(2, A2, 0)
     ag_wait(1)
-    gather_wait(2, A2, 0)
     hidden(l)
-    gather_relay(2, A2)
     gather_wait(2, A2, 2)
     hidden(ol)
-    ag_relay_start(2)
+    grad_product(0, DM, lambda at: all_rows(GG, at), width, 0, 2 * tile)
+    rs_start(0)
     ag_wait(2)
 
     @pl.loop(0, width // tile)
@@ -406,12 +437,10 @@
 
     in_back = back_product(lambda i: two(DU, i), 1, 0, width)
     scatter_far(1, in_back)
-    grad_product(2, DM, lambda at: all_rows(GG, at), width, 0, 2 * tile)
-    rs_start(2)
-    scatter_near(1, in_back)
     grad_product(1, A2, lambda at: all_rows(DU, at), width, 0, 2 * tile)
     rs_start(1)
-    rs_combine(2)
+    scatter_near(1, in_back)
+    rs_combine(0)
     e2 = scatter_result(1) * (1.0 + m[4])
     n2, r2 = normalize(MID[...])
     dmid = f32(og[...]) + norm_back(n2, r2, e2)
@@ -428,6 +457,9 @@
     gather_wait(3, DA, 2)
 
     DO[...] = bf(dot(DA[...].reshape(seq, width), W[0, :, :, :, pl.ds(3 * own, own)].reshape(width, own)))
+    ag_sent(1)
+    grad_product(2, DA, lambda at: O[:, at], own, 3 * own, own)
+    rs_start(2)
 
     @pl.loop(0, heads)
     def _(hd):
@@ -439,33 +471,46 @@
         DQKV[:, head(hd, 1)] = bf(dot(ds.T, QKV[:, head(hd, 0)]))
         DQKV[:, head(hd, 2)] = bf(dot(p.T, do))
 
-    ag_sent(1)
-    grad_product(0, A1, lambda at: DQKV[:, at], 3 * own, 0, own)
-    grad_product(0, DA, lambda at: O[:, at], own, 3 * own, own)
-    rs_start(0)
+    grad_product(3, A1, lambda at: DQKV[:, at], 3 * own, 0, own)
+    rs_start(3)
     fin[...] = bf(MID[...] + m[5] * scatter_result(2))
     qkv_back = back_product(lambda i: DQKV[pair_rows(i), :], 0, 0, 3 * own)
     scatter_far(3, qkv_back)
     scatter_near(3, qkv_back)
-    rs_mid_start(2)
-    rs_combine(0)
+    rs_mid_start(0)
+    rs_combine(2)
+    rs_combine(3)
     e1 = scatter_result(3) * (1.0 + m[1])
     n1, r1 = normalize(f32(tok[...]))
     dxin[...] = DX[...] + norm_back(n1, r1, e1)
     rs_mid_start(1)
+    rs_pair_start(0)
+    rs_mid_start(2)
+    rs_mid_start(3)
+    rs_pair_start(1)
+    rs_finish(0)
     rs_pair_start(2)
-    rs_mid_start(0)
-    rs_pair_start(1)
+    rs_pair_start(3)
+    rs_finish(1)
     rs_finish(2)
-    rs_pair_start(0)
-    rs_finish(1)
-    rs_finish(0)
-    for s in range(3):
+    rs_finish(3)
+    for s in range(4):
         rs_sent(s)
     ag_sent(0)
     ag_sent(2)
     for i, buf in enumerate((A1, DM, A2, DA)):
         gather_sent(i, buf)
+
+
+def place(fin, dx, grads, o_fin, o_dx, o_qkv, o_out, o_in, o_back):
+    own = o_out.shape[1]
+    o_fin[0] = fin[...]
+    o_dx[0] = dx[...]
+    for i in range(3):
+        o_qkv[i] = grads[0, :, i * own : (i + 1) * own]
+    o_out[...] = grads[0, :, 3 * own :]
+    o_in[0] = grads[1]
+    o_back[...] = grads[2]
 
 
 def step(dims, tokens, modulation, w_qkv, w_out, w_in, w_back, out_grad):
@@ -475,13 +520,6 @@
     assert ff == width and 4 * own == width
     seq = 4 * count
     heads = own // HEAD_DIM
-    blocks = jnp.stack(
-        [
-            jnp.concatenate([w_qkv[0].reshape(rows, 3 * own), w_out[0].T], axis=1),
-            w_in[0],
-            w_back[0].T,
-        ]
-    )
     big = (nz, ny, nh * rows)
     half = width // 2
     vmem = pltpu.VMEM
@@ -506,14 +544,17 @@
         vmem((count, width), BF),
         vmem((count, width), F32),
         vmem((count, width), F32),
-        dma((3,)),
+        vmem((count, width), BF),
+        vmem((6, 1, width), F32),
+        vmem((count, width), BF),
+        dma((9,)),
         dma((3,)), dma((3,)),
-        dma((3, 2, 3)), dma((3, 2, 3)),
+        dma((3, 2, 3, 2)), dma((3, 2, 3, 2)),
         dma((3, 2, 2)), dma((3, 2, 2)),
         dma((3, 2, 2)), dma((3, 2, 2)),
-        dma((3, 2, 2, 3)), dma((3, 2, 2, 3)),
-        dma((3, 2, 3)), dma((3, 2, 3)),
-        dma((3,)), dma((3,)),
+        dma((4, 2, 2, 3)), dma((4, 2, 2, 3)),
+        dma((4, 2, 3)), dma((4, 2, 3)),
+        dma((4,)), dma((4,)),
         dma((4, 3)), dma((4, 3)),
         dma((4, 3)), dma((4, 3)),
     ]
@@ -525,21 +566,30 @@
             jax.ShapeDtypeStruct((count, width), F32),
             jax.ShapeDtypeStruct((3, rows, width), F32),
         ),
-        in_specs=[spec, spec, pl.BlockSpec(memory_space=pl.ANY), spec],
+        in_specs=[pl.BlockSpec(memory_space=pl.ANY)] * 7,
         out_specs=(spec, spec, spec),
         scratch_shapes=scratch,
         compiler_params=pltpu.CompilerParams(
             collective_id=0, has_side_effects=True, vmem_limit_bytes=67043328
         ),
-    )(tokens[0], modulation[0, 0], blocks, out_grad[0])
-    return (
-        final[None],
-        dx[None],
-        grads[0, :, : 3 * own].reshape(1, rows, 3, own),
-        grads[0, :, 3 * own :].T[None],
-        grads[1][None],
-        grads[2].T[None],
+    )(
+        tokens[0], modulation[0].transpose(1, 0, 2), w_qkv[0].transpose(1, 0, 2), w_out[0].T,
+        w_in[0], w_back[0].T, out_grad[0],
     )
+    final, dx, qkv, out, inner, back = pl.pallas_call(
+        place,
+        out_shape=(
+            jax.ShapeDtypeStruct((1, count, width), BF),
+            jax.ShapeDtypeStruct((1, count, width), F32),
+            jax.ShapeDtypeStruct((3, rows, own), F32),
+            jax.ShapeDtypeStruct((rows, own), F32),
+            jax.ShapeDtypeStruct((1, rows, width), F32),
+            jax.ShapeDtypeStruct((rows, width), F32),
+        ),
+        in_specs=[spec] * 3,
+        out_specs=(spec,) * 6,
+    )(final, dx, grads)
+    return final, dx, qkv.transpose(1, 0, 2)[None], out.T[None], inner, back.T[None]
 
 
 def solution(mesh):

time: 214 us -> 185 us (0.86)
  Pallas kernels: 202 us -> 184 us
  local copies, waits for them, and re-layouts: 10.8 us -> 0 us
    pallas_call x1, Pallas kernels: 202 us -> 181 us  [step(): pl.pallas_call(functools.partial(kernel, dims), out_shape=(jax.ShapeDtype...]
    unnamed x15 -> x0, local copies, waits for them, and re-layouts: 5.7 us -> none
    broadcast_in_dim x2 -> x0, local copies, waits for them, and re-layouts: 3.47 us -> none  [the longest x1 1.95 us: step(): grads[2].T[None]]
    pallas_call x0 -> x1, Pallas kernels: none -> 2.88 us  [step(): pl.pallas_call(place, out_shape=(jax.ShapeDtypeStruct((1, count, width),...]
where the time goes in v4:
time: 185 us; the launch traced here: 184 us
  Pallas kernels  184 us (99%)
    pallas_call x1, Pallas kernels, step(): pl.pallas_call(functools.partial(kernel, dims), out_shape=(jax.ShapeDtype...  181 us

profile of v4, /device:TPU:0, one launch (start us, length us, event | category | flops | bytes accessed | tf_op | source)
XLA Modules:
  0.0 184.4 jit_solution(4012811009791024345)
XLA Ops:
  0.6 180.9 %shard_map.118 = (bf16[128,1536]{1,0:T(8,128)(2,1)}, f32[128,1536]{1,0:T(8,128)}, f32[3,48,1536]{2,1,0:T(8,128)}) custom-call(bf16[128,1536]{1,0:T(8,128)(2,1)} %bitcast.22, f32[6,1,1536]{2,1,0:T(1,128)} %bitcast.27, bf16[3,48,384]{2,1,0:T(8,128)(2,1)} %bitcast.26, bf16[48,384]{1,0:T(8,128)(2,1)} %bitcast.28, bf16[48,1536]{1,0:T(8,128)(2,1)} %bitcast.24, ...), custom_call_target="tpu_custom_call" | custom-call | tf_op jit(solution)/shard_map/pallas_call | solution.py:562
  181.5 2.9 %shard_map.119 = (bf16[1,128,1536]{2,1,0:T(8,128)(2,1)}, f32[1,128,1536]{2,1,0:T(8,128)}, f32[3,48,384]{2,1,0:T(8,128)}, f32[48,384]{1,0:T(8,128)}, f32[1,48,1536]{2,1,0:T(8,128)}, /*index=5*/f32[48,1536]{1,0:T(8,128)}) custom-call(bf16[128,1536]{1,0:T(8,128)(2,1)} %get-tuple-element.15.fin, f32[128,1536]{1,0:T(8,128)} %get-tuple-element.16.dx, ...), custom_call_target="tpu_custom_call" | custom-call | tf_op jit(solution)/shard_map/pallas_call | solution.py:579

commit v5 on v4

--- a/solution.py
+++ b/solution.py
@@ -50,7 +50,7 @@
 
 def kernel(
     dims, tok_in, mod_in, wq_in, wo_in, wi_in, wb_in, og_in, fin, dxin, grads,
-    W, G, R1A, R1B, R2A, R2B, R3, A1, A2, DM, DA, GG, DU, QKV, DQKV, O, DO, PR, PS, RX, SX, MID, DX,
+    W, G, R1A, R1B, R2A, R2B, R3, A1, A2, DM, DA, GG, DU, QKV, DQKV, O, DO, PR, PS, RX, SX, MID, DX, AT,
     tok, mod, og, in_sem, a1s, a1r, a2s, a2r, a3s, a3r, a4s, a4r, r1s, r1r, r2s, r2r, r3s, r3r, gs, gr, ss, sr,
 ):
     nz, ny, nh = dims
@@ -158,22 +158,21 @@
 
     R1 = (R1A, R1B)
     R2 = (R2A, R2B)
-    parts = (G.at[0], G.at[1], W.at[1], W.at[1])
-    slots = (2, 1, 0, 0)
     full = 3 * own
-    local_cols = (
-        (pl.ds(0, half), pl.ds(0, half)),
-        (pl.ds(0, half), pl.ds(0, half)),
-        (pl.ds(half - 256, 256), pl.ds(half - 128, 128)),
-        (pl.ds(0, half - 256), pl.ds(0, half - 128)),
-    )
-    grad_cols = (
-        (cols[0], cols[1]),
-        (cols[0], cols[1]),
-        (pl.ds(full, 256), pl.ds(full + 256, 128)),
-        (pl.ds(0, half - 256), pl.ds(half - 256, half - 128)),
-    )
-    pair_cols = (pl.ds(0, width), pl.ds(0, width), pl.ds(full, own), pl.ds(0, full))
+    sections = 3 + heads
+    parts = (G.at[0], G.at[1]) + (W.at[1],) * (1 + heads)
+    slots = (2, 1) + (0,) * (1 + heads)
+    local_cols = [cols[:1] * 2] * 2
+    grad_cols = [cols] * 2
+    pair_cols = [pl.ds(0, width)] * 2
+    at0 = [0, 0]
+    for i, base in enumerate([full] + [hd * own for hd in range(heads)]):
+        first = 256 if i % 2 == 0 else 128
+        second = own - first
+        local_cols.append((pl.ds(at0[0], first), pl.ds(at0[1], second)))
+        grad_cols.append((pl.ds(base, first), pl.ds(base + first, second)))
+        pair_cols.append(pl.ds(base, own))
+        at0 = [at0[0] + first, at0[1] + second]
 
     def rs_ring(s, color, d, kind):
         k = 1 - 2 * d
@@ -195,9 +194,9 @@
             r3s.at[s], r3r.at[s], pair_peer,
         )
 
-    def rs_start(s):
+    def rs_start(s, colors=(0, 1)):
         for kind in (0, 1):
-            for color in (0, 1):
+            for color in colors:
                 for d in (0, 1):
                     rs_ring(s, color, d, kind).start()
 
@@ -328,16 +327,24 @@
     def all_rows(buf, at):
         return buf[:, :, :, at].reshape(seq, -1)
 
-    def grad_product(s, left, right, n, lo, tile):
+    def turn(buf):
+        @pl.loop(0, nz)
+        def _(b):
+            AT[b] = all_rows(buf, pl.ds(pl.multiple_of(b * slab, 128), slab)).T
+
+    def grad_turned(s, right, start, stop, tile):
+        @pl.loop(0, (stop - start) // tile)
+        def _(t):
+            at = pl.ds(pl.multiple_of(start + t * tile, 128), tile)
+            value = dot(AT[...].reshape(width, seq), right(at)) * q_s
+            parts[s][:, :, :, at] = bf(value).reshape(nz, ny, nh * rows, tile)
+
+    def grad_product(s, left, right, n, lo):
         @pl.loop(0, nz)
         def _(b):
             a = all_rows(left, pl.ds(pl.multiple_of(b * slab, 128), slab)).T
-
-            @pl.loop(0, n // tile)
-            def _(t):
-                at = pl.multiple_of(t * tile, 128)
-                value = dot(a, right(pl.ds(at, tile))) * q_s
-                parts[s][b, :, :, pl.ds(lo + at, tile)] = bf(value).reshape(ny, nh * rows, tile)
+            value = dot(a, right) * q_s
+            parts[s][b, :, :, pl.ds(lo, n)] = bf(value).reshape(ny, nh * rows, n)
 
     peers = [{"z": zz(k)} for k in range(1, 4)] + [{"y": yy(k)} for k in range(1, 4)]
     peers += [pair_peer, core_peer, line_peer, {"l": ol, "c": oc}]
@@ -345,7 +352,10 @@
     for dev in peers:
         pl.semaphore_signal(barrier, inc=1, device_id=dev, device_id_type=pl.DeviceIdType.MESH)
     mine = at_rows(h)
-    moves = [(wq_in.at[i], W.at[0, z, y, mine, pl.ds(i * own, own)]) for i in range(3)]
+    moves = [
+        (wq_in.at[i, :, pl.ds(hd * HEAD_DIM, HEAD_DIM)], W.at[0, z, y, mine, pl.ds((3 * hd + i) * HEAD_DIM, HEAD_DIM)])
+        for i in range(3) for hd in range(heads)
+    ]
     moves += [(wo_in, W.at[0, z, y, mine, pl.ds(3 * own, own)])]
     moves += [(wi_in, W.at[1, z, y, mine]), (wb_in, W.at[2, z, y, mine])]
     moves += [(tok_in, tok), (og_in, og), (mod_in, mod)]
@@ -375,6 +385,9 @@
     gather_wait(0, A1, 0)
     gather_wait(0, A1, 2)
     gather_relay(1, DM)
+    gather_wait(1, DM, 0)
+    gather_wait(1, DM, 2)
+    turn(DM)
 
     ag_wait(0)
 
@@ -385,7 +398,10 @@
         QKV[:, at] = bf(dot(A1[...].reshape(seq, width), w))
 
     def head(hd, i):
-        return pl.ds(pl.multiple_of(i * own + hd * HEAD_DIM, 128), HEAD_DIM)
+        return pl.ds(pl.multiple_of((3 * hd + i) * HEAD_DIM, 128), HEAD_DIM)
+
+    def wide(hd):
+        return pl.ds(pl.multiple_of(hd * HEAD_DIM, 128), HEAD_DIM)
 
     @pl.loop(0, heads)
     def _(hd):
@@ -393,7 +409,7 @@
         e = jnp.exp(s - jnp.max(s, axis=-1, keepdims=True))
         p = bf(e * (1.0 / jnp.sum(e, axis=-1, keepdims=True)))
         PR[hd] = p
-        O[:, head(hd, 0)] = bf(dot(p, QKV[:, head(hd, 2)]))
+        O[:, wide(hd)] = bf(dot(p, QKV[:, head(hd, 2)]))
 
     out_product = back_product(lambda i: O[pair_rows(i), :], 0, 3 * own, own)
     ag_last_start(2)
@@ -405,8 +421,6 @@
     n2, r2 = normalize(mid)
     A2[l, c] = bf(n2 * (1.0 + m[4]) + m[3])
     gather_start(2, A2)
-    gather_wait(1, DM, 0)
-    gather_wait(1, DM, 2)
 
     tile = 256
 
@@ -425,8 +439,9 @@
     hidden(l)
     gather_wait(2, A2, 2)
     hidden(ol)
-    grad_product(0, DM, lambda at: all_rows(GG, at), width, 0, 2 * tile)
-    rs_start(0)
+    for color in (0, 1):
+        grad_turned(0, lambda at: all_rows(GG, at), color * half, (color + 1) * half, tile)
+        rs_start(0, (color,))
     ag_wait(2)
 
     @pl.loop(0, width // tile)
@@ -437,10 +452,13 @@
 
     in_back = back_product(lambda i: two(DU, i), 1, 0, width)
     scatter_far(1, in_back)
-    grad_product(1, A2, lambda at: all_rows(DU, at), width, 0, 2 * tile)
-    rs_start(1)
+    turn(A2)
+    grad_turned(1, lambda at: all_rows(DU, at), 0, half, tile)
+    rs_combine(0)
+    rs_start(1, (0,))
+    grad_turned(1, lambda at: all_rows(DU, at), half, width, tile)
+    rs_start(1, (1,))
     scatter_near(1, in_back)
-    rs_combine(0)
     e2 = scatter_result(1) * (1.0 + m[4])
     n2, r2 = normalize(MID[...])
     dmid = f32(og[...]) + norm_back(n2, r2, e2)
@@ -451,50 +469,57 @@
     ff_back = back_product(lambda i: two(GG, i), 2, 0, width)
     scatter_far(2, ff_back)
     scatter_near(2, ff_back)
+    turn(A1)
     rs_combine(1)
+    rs_mid_start(0)
     gather_relay(3, DA)
     gather_wait(3, DA, 0)
     gather_wait(3, DA, 2)
 
     DO[...] = bf(dot(DA[...].reshape(seq, width), W[0, :, :, :, pl.ds(3 * own, own)].reshape(width, own)))
     ag_sent(1)
-    grad_product(2, DA, lambda at: O[:, at], own, 3 * own, own)
+    grad_product(2, DA, O[...], own, full)
     rs_start(2)
 
-    @pl.loop(0, heads)
-    def _(hd):
-        do = DO[:, head(hd, 0)]
+    for hd in range(heads):
+        do = DO[:, wide(hd)]
         p = PR[hd]
         t = f32(p) * dot(do, QKV[:, head(hd, 2)], 1, 1)
         ds = bf(scale * (t - f32(p) * jnp.sum(t, axis=-1, keepdims=True)))
         DQKV[:, head(hd, 0)] = bf(dot(ds, QKV[:, head(hd, 1)]))
         DQKV[:, head(hd, 1)] = bf(dot(ds.T, QKV[:, head(hd, 0)]))
         DQKV[:, head(hd, 2)] = bf(dot(p.T, do))
-
-    grad_product(3, A1, lambda at: DQKV[:, at], 3 * own, 0, own)
-    rs_start(3)
+        grad_turned(3 + hd, lambda at: DQKV[:, at], hd * own, (hd + 1) * own, own)
+        if hd == 1:
+            rs_mid_start(1)
+        rs_start(3 + hd)
+
+    qkv_back = back_product(lambda i: DQKV[pair_rows(i), :], 0, 0, 3 * own)
     fin[...] = bf(MID[...] + m[5] * scatter_result(2))
-    qkv_back = back_product(lambda i: DQKV[pair_rows(i), :], 0, 0, 3 * own)
     scatter_far(3, qkv_back)
-    scatter_near(3, qkv_back)
-    rs_mid_start(0)
     rs_combine(2)
     rs_combine(3)
+    scatter_near(3, qkv_back)
+    rs_pair_start(0)
+    rs_combine(4)
+    rs_mid_start(2)
+    rs_combine(5)
+    rs_mid_start(3)
     e1 = scatter_result(3) * (1.0 + m[1])
     n1, r1 = normalize(f32(tok[...]))
     dxin[...] = DX[...] + norm_back(n1, r1, e1)
-    rs_mid_start(1)
-    rs_pair_start(0)
-    rs_mid_start(2)
-    rs_mid_start(3)
     rs_pair_start(1)
     rs_finish(0)
+    rs_mid_start(4)
     rs_pair_start(2)
+    rs_mid_start(5)
     rs_pair_start(3)
     rs_finish(1)
-    rs_finish(2)
-    rs_finish(3)
-    for s in range(4):
+    rs_pair_start(4)
+    rs_pair_start(5)
+    for s in range(2, sections):
+        rs_finish(s)
+    for s in range(sections):
         rs_sent(s)
     ag_sent(0)
     ag_sent(2)
@@ -507,7 +532,9 @@
     o_fin[0] = fin[...]
     o_dx[0] = dx[...]
     for i in range(3):
-        o_qkv[i] = grads[0, :, i * own : (i + 1) * own]
+        for hd in range(own // HEAD_DIM):
+            at = (3 * hd + i) * HEAD_DIM
+            o_qkv[i, :, hd * HEAD_DIM : (hd + 1) * HEAD_DIM] = grads[0, :, at : at + HEAD_DIM]
     o_out[...] = grads[0, :, 3 * own :]
     o_in[0] = grads[1]
     o_back[...] = grads[2]
@@ -544,17 +571,18 @@
         vmem((count, width), BF),
         vmem((count, width), F32),
         vmem((count, width), F32),
+        vmem((nz, ny * nh * rows, seq), BF),
         vmem((count, width), BF),
         vmem((6, 1, width), F32),
         vmem((count, width), BF),
-        dma((9,)),
+        dma((6 + 3 * heads,)),
         dma((3,)), dma((3,)),
         dma((3, 2, 3, 2)), dma((3, 2, 3, 2)),
         dma((3, 2, 2)), dma((3, 2, 2)),
         dma((3, 2, 2)), dma((3, 2, 2)),
-        dma((4, 2, 2, 3)), dma((4, 2, 2, 3)),
-        dma((4, 2, 3)), dma((4, 2, 3)),
-        dma((4,)), dma((4,)),
+        dma((3 + heads, 2, 2, 3)), dma((3 + heads, 2, 2, 3)),
+        dma((3 + heads, 2, 3)), dma((3 + heads, 2, 3)),
+        dma((3 + heads,)), dma((3 + heads,)),
         dma((4, 3)), dma((4, 3)),
         dma((4, 3)), dma((4, 3)),
     ]

time: 185 us -> 179 us (0.968)
  Pallas kernels: 184 us -> 179 us
    pallas_call x1, Pallas kernels: 181 us -> 176 us  [step(): pl.pallas_call(functools.partial(kernel, dims), out_shape=(jax.ShapeDtype...]
where the time goes in v5:
time: 179 us
  Pallas kernels  179 us (100%)
    pallas_call x1, Pallas kernels, step(): pl.pallas_call(functools.partial(kernel, dims), out_shape=(jax.ShapeDtype...  176 us

profile of v5, /device:TPU:0, one launch (start us, length us, event | category | flops | bytes accessed | tf_op | source)
XLA Modules:
  0.0 179.2 jit_solution(431118516260455967)
XLA Ops:
  0.6 175.7 %shard_map.118 = (bf16[128,1536]{1,0:T(8,128)(2,1)}, f32[128,1536]{1,0:T(8,128)}, f32[3,48,1536]{2,1,0:T(8,128)}) custom-call(bf16[128,1536]{1,0:T(8,128)(2,1)} %bitcast.22, f32[6,1,1536]{2,1,0:T(1,128)} %bitcast.27, bf16[3,48,384]{2,1,0:T(8,128)(2,1)} %bitcast.26, bf16[48,384]{1,0:T(8,128)(2,1)} %bitcast.28, bf16[48,1536]{1,0:T(8,128)(2,1)} %bitcast.24, ...), custom_call_target="tpu_custom_call" | custom-call | tf_op jit(solution)/shard_map/pallas_call | solution.py:590
  176.3 2.9 %shard_map.119 = (bf16[1,128,1536]{2,1,0:T(8,128)(2,1)}, f32[1,128,1536]{2,1,0:T(8,128)}, f32[3,48,384]{2,1,0:T(8,128)}, f32[48,384]{1,0:T(8,128)}, f32[1,48,1536]{2,1,0:T(8,128)}, /*index=5*/f32[48,1536]{1,0:T(8,128)}) custom-call(bf16[128,1536]{1,0:T(8,128)(2,1)} %get-tuple-element.15.fin, f32[128,1536]{1,0:T(8,128)} %get-tuple-element.16.dx, ...), custom_call_target="tpu_custom_call" | custom-call | tf_op jit(solution)/shard_map/pallas_call | solution.py:607

commit v6 on v5

--- a/solution.py
+++ b/solution.py
@@ -50,8 +50,8 @@
 
 def kernel(
     dims, tok_in, mod_in, wq_in, wo_in, wi_in, wb_in, og_in, fin, dxin, grads,
-    W, G, R1A, R1B, R2A, R2B, R3, A1, A2, DM, DA, GG, DU, QKV, DQKV, O, DO, PR, PS, RX, SX, MID, DX, AT,
-    tok, mod, og, in_sem, a1s, a1r, a2s, a2r, a3s, a3r, a4s, a4r, r1s, r1r, r2s, r2r, r3s, r3r, gs, gr, ss, sr,
+    W, G, R1A, R1B, R2A, R2B, R3, R1C, R2C, R4, R4H, A1, A2, DM, DA, GG, DU, QKV, DQKV, O, DO, PR, PS, RX, SX, MID, DX, AT,
+    tok, mod, og, in_sem, a1s, a1r, a2s, a2r, a3s, a3r, a4s, a4r, r1s, r1r, r2s, r2r, r3s, r3r, r4s, r4r, gs, gr, ss, sr,
 ):
     nz, ny, nh = dims
     z, y, h, l, c = (lax.axis_index(a) for a in AXES)
@@ -96,50 +96,71 @@
     def mid_dev(color, k):
         return last(1 - color, k)
 
-    def slab_at(buf, color, k, at, part=slice(None)):
-        return buf.at[zz(k), part, :, at] if color == 0 else buf.at[part, yy(k), :, at]
-
-    def line_at(buf, color, k, at, part=slice(None)):
-        return buf.at[z, yy(k), part, at] if color == 0 else buf.at[zz(k), y, part, at]
+    strip = 256
+    side = (width - strip) // 2
+    ag_cols = ((pl.ds(0, side), pl.ds(side, side), pl.ds(2 * side, strip)),) * 2 + (cols,)
+    every = slice(None)
+
+    def slab_at(buf, color, k, at, part=every, row=every):
+        return buf.at[zz(k), part, row, at] if color == 0 else buf.at[part, yy(k), row, at]
+
+    def line_at(buf, color, k, at, row=every):
+        return buf.at[z, yy(k), row, at] if color == 0 else buf.at[zz(k), y, row, at]
+
+    def line_of(s, color):
+        return color if color < 2 else s % 2
+
+    def row_of(color):
+        return every if color < 2 else at_rows(h)
 
     def ag_pair(s, recv):
-        piece = W.at[s, z, y, at_rows(1 - h if recv else h)]
-        return copy(piece, piece, a1s.at[s], a1r.at[s], pair_peer)
+        piece = W.at[s, z, y, at_rows(1 - h if recv else h), pl.ds(0, 2 * side if s < 2 else width)]
+        return copy(piece, piece, a1s.at[s, 0], a1r.at[s, 0], pair_peer)
+
+    def ag_final(s, recv):
+        piece = W.at[s, :, :, at_rows(1 - h if recv else h), ag_cols[s][2]]
+        return copy(piece, piece, a1s.at[s, 1], a1r.at[s, 1], pair_peer)
 
     def ag_mid(s, color, k, which, recv):
-        piece = line_at(W.at[s], color, -k if recv else 0, cols[color], at_rows(h if which == 0 else 1 - h))
-        return copy(piece, piece, a2s.at[s, color, k - 1, which], a2r.at[s, color, k - 1, which], mid_dev(color, k))
+        line = line_of(s, color)
+        piece = line_at(W.at[s], line, -k if recv else 0, ag_cols[s][color], at_rows(h if which == 0 else 1 - h))
+        return copy(piece, piece, a2s.at[s, color, k - 1, which], a2r.at[s, color, k - 1, which], mid_dev(line, k))
 
     def ag_last(s, color, d, recv):
-        k = 1 - 2 * d
-        piece = slab_at(W.at[s], color, -k if recv else 0, cols[color])
-        return copy(piece, piece, a3s.at[s, color, d], a3r.at[s, color, d], last(color, k))
+        k, line = 1 - 2 * d, line_of(s, color)
+        piece = slab_at(W.at[s], line, -k if recv else 0, ag_cols[s][color], row=row_of(color))
+        return copy(piece, piece, a3s.at[s, color, d], a3r.at[s, color, d], last(line, k))
 
     def ag_relay(s, color, d, recv):
-        k = 1 - 2 * d
-        piece = slab_at(W.at[s], color, 2 if recv else -k, cols[color], halves[d])
-        return copy(piece, piece, a4s.at[s, color, d], a4r.at[s, color, d], last(color, k))
-
-    def ag_mid_start(s, which):
+        k, line = 1 - 2 * d, line_of(s, color)
+        piece = slab_at(W.at[s], line, 2 if recv else -k, ag_cols[s][color], halves[d], row_of(color))
+        return copy(piece, piece, a4s.at[s, color, d], a4r.at[s, color, d], last(line, k))
+
+    def ag_mid_start(s, which, colors=(0, 1)):
         if which:
             ag_pair(s, True).wait_recv()
         for k in (1, 3, 2):
-            for color in (0, 1):
+            for color in colors:
                 ag_mid(s, color, k, which, False).start()
 
-    def ag_last_start(s):
-        for color in (0, 1):
-            for which in (0, 1):
+    def ag_last_start(s, colors=(0, 1)):
+        for color in colors:
+            for which in (0, 1) if color < 2 else (0,):
                 for k in range(1, 4):
                     ag_mid(s, color, k, which, True).wait_recv()
             for d in (0, 1):
                 ag_last(s, color, d, False).start()
 
-    def ag_relay_start(s):
-        for color in (0, 1):
+    def ag_relay_start(s, colors=(0, 1)):
+        for color in colors:
             for d in (0, 1):
                 ag_last(s, color, d, True).wait_recv()
                 ag_relay(s, color, d, False).start()
+
+    def ag_final_start(s):
+        for d in (0, 1):
+            ag_relay(s, 2, d, True).wait_recv()
+        ag_final(s, False).start()
 
     def ag_wait(s):
         for color in (0, 1):
@@ -148,8 +169,10 @@
 
     def ag_sent(s):
         ag_pair(s, False).wait_send()
-        for color in (0, 1):
-            for which in (0, 1):
+        if s < 2:
+            ag_final(s, False).wait_send()
+        for color in (0, 1, 2) if s < 2 else (0, 1):
+            for which in (0, 1) if color < 2 else (0,):
                 for k in range(1, 4):
                     ag_mid(s, color, k, which, False).wait_send()
             for d in (0, 1):
@@ -162,30 +185,46 @@
     sections = 3 + heads
     parts = (G.at[0], G.at[1]) + (W.at[1],) * (1 + heads)
     slots = (2, 1) + (0,) * (1 + heads)
-    local_cols = [cols[:1] * 2] * 2
-    grad_cols = [cols] * 2
-    pair_cols = [pl.ds(0, width)] * 2
-    at0 = [0, 0]
-    for i, base in enumerate([full] + [hd * own for hd in range(heads)]):
-        first = 256 if i % 2 == 0 else 128
-        second = own - first
-        local_cols.append((pl.ds(at0[0], first), pl.ds(at0[1], second)))
-        grad_cols.append((pl.ds(base, first), pl.ds(base + first, second)))
-        pair_cols.append(pl.ds(base, own))
-        at0 = [at0[0] + first, at0[1] + second]
+    lead = pl.ds(0, side)
+    local_cols = [(lead, lead), (cols[0], cols[0])]
+    grad_cols = [ag_cols[0], cols]
+    pair_cols = [pl.ds(0, 2 * side), pl.ds(0, width)]
+    third = own // 3
+    for i, start in enumerate([full] + [hd * own for hd in range(heads)]):
+        at = pl.ds(i * third, third)
+        local_cols.append((at, at, pl.ds((4 + i // 2) * third, third)))
+        grad_cols.append(tuple(pl.ds(start + j * third, third) for j in range(3)))
+        pair_cols.append(pl.ds(start, 2 * third))
+
+    def r1_at(s, color):
+        if color < 2:
+            return R1[color].at[slots[s], :, :, :, local_cols[s][color]]
+        return R1C if s == 0 else R1[s % 2].at[0, :, :, pl.ds(0, rows), local_cols[s][2]]
+
+    def r2_at(s, color):
+        if color < 2:
+            return R2[color].at[slots[s], :, :, local_cols[s][color]]
+        return R2C if s == 0 else R2[s % 2].at[0, :, pl.ds(0, rows), local_cols[s][2]]
+
+    def r4_at(s):
+        return R4 if s == 0 else R4H.at[s - 2]
+
+    def rs_first(s):
+        src = parts[s].at[:, :, at_rows(1 - h), grad_cols[s][2]]
+        return copy(src, r4_at(s), r4s.at[s], r4r.at[s], pair_peer)
 
     def rs_ring(s, color, d, kind):
-        k = 1 - 2 * d
+        k, line = 1 - 2 * d, line_of(s, color)
         part = halves[1 - d if kind == 1 else d]
-        src = slab_at(parts[s], color, 2 if kind == 0 else k, grad_cols[s][color], part)
-        dst = R1[color].at[slots[s], 2 if kind == 0 else d, part, :, local_cols[s][color]]
-        return copy(src, dst, r1s.at[s, color, d, kind], r1r.at[s, color, d, kind], last(color, k))
+        src = slab_at(parts[s], line, 2 if kind == 0 else k, grad_cols[s][color], part, row_of(color))
+        dst = r1_at(s, color).at[2 if kind == 0 else d, part]
+        return copy(src, dst, r1s.at[s, color, d, kind], r1r.at[s, color, d, kind], last(line, k))
 
     def rs_mid(s, color, k):
+        line = line_of(s, color)
         return copy(
-            line_at(parts[s], color, k, grad_cols[s][color]),
-            R2[color].at[slots[s], k - 1, :, local_cols[s][color]],
-            r2s.at[s, color, k - 1], r2r.at[s, color, k - 1], mid_dev(color, k),
+            line_at(parts[s], line, k, grad_cols[s][color], row_of(color)), r2_at(s, color).at[k - 1],
+            r2s.at[s, color, k - 1], r2r.at[s, color, k - 1], mid_dev(line, k),
         )
 
     def rs_pair(s):
@@ -194,54 +233,67 @@
             r3s.at[s], r3r.at[s], pair_peer,
         )
 
+    def rs_second(s):
+        rs_first(s).wait_recv()
+
+        @pl.loop(0, nz)
+        def _(i):
+            at = (i, every, at_rows(h), grad_cols[s][2])
+            parts[s][at] = bf(f32(parts[s][at]) + f32(r4_at(s)[i]))
+
+        rs_start(s, (2,))
+
     def rs_start(s, colors=(0, 1)):
         for kind in (0, 1):
             for color in colors:
                 for d in (0, 1):
                     rs_ring(s, color, d, kind).start()
 
-    def rs_combine(s):
-        for color in (0, 1):
+    def rs_combine(s, colors=(0, 1)):
+        for color in colors:
+            line = line_of(s, color)
             for d in (0, 1):
                 rs_ring(s, color, d, 0).wait_recv()
                 k = 1 - 2 * d
 
                 @pl.loop(2 * d, 2 * d + 2)
                 def _(i):
-                    at = (zz(k), i) if color == 0 else (i, yy(k))
-                    at = (*at, slice(None), grad_cols[s][color])
-                    came = R1[color][slots[s], 2, i, :, local_cols[s][color]]
-                    parts[s][at] = bf(f32(parts[s][at]) + f32(came))
+                    at = (zz(k), i) if line == 0 else (i, yy(k))
+                    at = (*at, row_of(color), grad_cols[s][color])
+                    parts[s][at] = bf(f32(parts[s][at]) + f32(r1_at(s, color)[2, i]))
 
                 rs_ring(s, color, d, 2).start()
 
-    def rs_mid_start(s):
-        for color in (0, 1):
+    def rs_mid_start(s, colors=(0, 1)):
+        for color in colors:
+            line = line_of(s, color)
             for d in (0, 1):
                 for kind in (1, 2):
                     rs_ring(s, color, d, kind).wait_recv()
 
             @pl.loop(0, 4)
             def _(i):
-                at = (z, i) if color == 0 else (i, y)
-                at = (*at, slice(None), grad_cols[s][color])
+                at = (z, i) if line == 0 else (i, y)
+                at = (*at, row_of(color), grad_cols[s][color])
                 total = f32(parts[s][at])
                 for d in (0, 1):
-                    total = total + f32(R1[color][slots[s], d, i, :, local_cols[s][color]])
+                    total = total + f32(r1_at(s, color)[d, i])
                 parts[s][at] = bf(total)
 
             for k in (1, 3, 2):
                 rs_mid(s, color, k).start()
 
+    def rs_total(s, color):
+        for k in range(1, 4):
+            rs_mid(s, color, k).wait_recv()
+        total = f32(parts[s][z, y, row_of(color), grad_cols[s][color]])
+        for k in range(3):
+            total = total + f32(r2_at(s, color)[k])
+        return total
+
     def rs_pair_start(s):
         for color in (0, 1):
-            for k in range(1, 4):
-                rs_mid(s, color, k).wait_recv()
-            at = (z, y, slice(None), grad_cols[s][color])
-            total = f32(parts[s][at])
-            for k in range(3):
-                total = total + f32(R2[color][slots[s], k, :, local_cols[s][color]])
-            parts[s][at] = bf(total)
+            parts[s][z, y, every, grad_cols[s][color]] = bf(rs_total(s, color))
         rs_pair(s).start()
 
     def rs_finish(s):
@@ -249,13 +301,18 @@
         at = pair_cols[s]
         grads[slots[s], :, at] = f32(parts[s][z, y, at_rows(h), at]) + f32(R3[slots[s], :, at])
 
+    def rs_finish_third(s):
+        grads[slots[s], :, grad_cols[s][2]] = rs_total(s, 2)
+
     def rs_sent(s):
-        for color in (0, 1):
+        for color in (0, 1) if s == 1 else (0, 1, 2):
             for d in (0, 1):
                 for kind in (0, 1, 2):
                     rs_ring(s, color, d, kind).wait_send()
             for k in range(1, 4):
                 rs_mid(s, color, k).wait_send()
+        if s != 1:
+            rs_first(s).wait_send()
         rs_pair(s).wait_send()
 
     def g_copy(i, buf, step, recv):
@@ -372,22 +429,27 @@
 
     for s in range(3):
         ag_pair(s, False).start()
+    for s in (0, 1):
+        ag_mid_start(s, 0, (2,))
         ag_mid_start(s, 0)
     gather_start(0, A1)
+    ag_last_start(0, (2,))
     ag_mid_start(0, 1)
     ag_mid_start(1, 1)
+    ag_last_start(1, (2,))
+    ag_relay_start(0, (2,))
     ag_last_start(0)
+    ag_relay_start(1, (2,))
+    ag_mid_start(2, 0)
     ag_mid_start(2, 1)
+    ag_final_start(0)
     gather_relay(0, A1)
-    gather_start(1, DM)
     ag_relay_start(0)
     ag_last_start(1)
+    ag_final_start(1)
+    gather_start(1, DM)
     gather_wait(0, A1, 0)
     gather_wait(0, A1, 2)
-    gather_relay(1, DM)
-    gather_wait(1, DM, 0)
-    gather_wait(1, DM, 2)
-    turn(DM)
 
     ag_wait(0)
 
@@ -413,6 +475,7 @@
 
     out_product = back_product(lambda i: O[pair_rows(i), :], 0, 3 * own, own)
     ag_last_start(2)
+    ag_final(0, True).wait_recv()
     scatter_far(0, out_product)
     scatter_near(0, out_product)
     ag_relay_start(1)
@@ -432,16 +495,24 @@
             GG[i, :, :, at] = bf(g).reshape(2, pair // 2, tile)
             DU[i, :, :, at] = bf(d).reshape(2, pair // 2, tile)
 
+    gather_relay(1, DM)
+    gather_wait(1, DM, 0)
+    gather_wait(1, DM, 2)
+    turn(DM)
     ag_relay_start(2)
     gather_relay(2, A2)
     gather_wait(2, A2, 0)
     ag_wait(1)
+    ag_final(1, True).wait_recv()
     hidden(l)
     gather_wait(2, A2, 2)
     hidden(ol)
-    for color in (0, 1):
-        grad_turned(0, lambda at: all_rows(GG, at), color * half, (color + 1) * half, tile)
-        rs_start(0, (color,))
+    for lo, hi in ((2 * side, width), (0, half), (half, 2 * side)):
+        grad_turned(0, lambda at: all_rows(GG, at), lo, hi, tile)
+        if lo == 2 * side:
+            rs_first(0).start()
+        else:
+            rs_start(0, (0,) if lo == 0 else (1,))
     ag_wait(2)
 
     @pl.loop(0, width // tile)
@@ -455,6 +526,7 @@
     turn(A2)
     grad_turned(1, lambda at: all_rows(DU, at), 0, half, tile)
     rs_combine(0)
+    rs_second(0)
     rs_start(1, (0,))
     grad_turned(1, lambda at: all_rows(DU, at), half, width, tile)
     rs_start(1, (1,))
@@ -470,6 +542,7 @@
     scatter_far(2, ff_back)
     scatter_near(2, ff_back)
     turn(A1)
+    rs_combine(0, (2,))
     rs_combine(1)
     rs_mid_start(0)
     gather_relay(3, DA)
@@ -479,6 +552,7 @@
     DO[...] = bf(dot(DA[...].reshape(seq, width), W[0, :, :, :, pl.ds(3 * own, own)].reshape(width, own)))
     ag_sent(1)
     grad_product(2, DA, O[...], own, full)
+    rs_first(2).start()
     rs_start(2)
 
     for hd in range(heads):
@@ -490,33 +564,49 @@
         DQKV[:, head(hd, 1)] = bf(dot(ds.T, QKV[:, head(hd, 0)]))
         DQKV[:, head(hd, 2)] = bf(dot(p.T, do))
         grad_turned(3 + hd, lambda at: DQKV[:, at], hd * own, (hd + 1) * own, own)
-        if hd == 1:
-            rs_mid_start(1)
+        rs_first(3 + hd).start()
         rs_start(3 + hd)
 
     qkv_back = back_product(lambda i: DQKV[pair_rows(i), :], 0, 0, 3 * own)
     fin[...] = bf(MID[...] + m[5] * scatter_result(2))
     scatter_far(3, qkv_back)
+    rs_second(2)
     rs_combine(2)
+    rs_mid_start(1)
+    scatter_near(3, qkv_back)
     rs_combine(3)
-    scatter_near(3, qkv_back)
+    rs_second(3)
+    rs_mid_start(0, (2,))
+    rs_combine(4)
+    rs_combine(2, (2,))
+    rs_second(4)
     rs_pair_start(0)
-    rs_combine(4)
+    rs_combine(5)
     rs_mid_start(2)
-    rs_combine(5)
+    rs_second(5)
+    rs_combine(3, (2,))
     rs_mid_start(3)
+    rs_finish_third(0)
+    rs_mid_start(2, (2,))
+    rs_combine(4, (2,))
     e1 = scatter_result(3) * (1.0 + m[1])
     n1, r1 = normalize(f32(tok[...]))
     dxin[...] = DX[...] + norm_back(n1, r1, e1)
+    rs_mid_start(4)
+    rs_mid_start(3, (2,))
+    rs_combine(5, (2,))
+    rs_mid_start(5)
     rs_pair_start(1)
     rs_finish(0)
-    rs_mid_start(4)
     rs_pair_start(2)
-    rs_mid_start(5)
+    rs_mid_start(4, (2,))
     rs_pair_start(3)
+    rs_mid_start(5, (2,))
+    rs_pair_start(4)
     rs_finish(1)
-    rs_pair_start(4)
     rs_pair_start(5)
+    for s in range(2, sections):
+        rs_finish_third(s)
     for s in range(2, sections):
         rs_finish(s)
     for s in range(sections):
@@ -560,6 +650,10 @@
         vmem((3, 3, nh * rows, half), BF),
         vmem((3, 3, nh * rows, half), BF),
         vmem((3, rows, width), BF),
+        vmem((3, 4, rows, 256), BF),
+        vmem((3, rows, 256), BF),
+        vmem((nz, ny, rows, 256), BF),
+        vmem((1 + heads, nz, ny, rows, own // 3), BF),
         *[tokens_buf] * 6,
         vmem((seq, 3 * own), BF),
         vmem((seq, 3 * own), BF),
@@ -576,12 +670,13 @@
         vmem((6, 1, width), F32),
         vmem((count, width), BF),
         dma((6 + 3 * heads,)),
-        dma((3,)), dma((3,)),
-        dma((3, 2, 3, 2)), dma((3, 2, 3, 2)),
-        dma((3, 2, 2)), dma((3, 2, 2)),
-        dma((3, 2, 2)), dma((3, 2, 2)),
-        dma((3 + heads, 2, 2, 3)), dma((3 + heads, 2, 2, 3)),
-        dma((3 + heads, 2, 3)), dma((3 + heads, 2, 3)),
+        dma((3, 2)), dma((3, 2)),
+        dma((3, 3, 3, 2)), dma((3, 3, 3, 2)),
+        dma((3, 3, 2)), dma((3, 3, 2)),
+        dma((3, 3, 2)), dma((3, 3, 2)),
+        dma((3 + heads, 3, 2, 3)), dma((3 + heads, 3, 2, 3)),
+        dma((3 + heads, 3, 3)), dma((3 + heads, 3, 3)),
+        dma((3 + heads,)), dma((3 + heads,)),
         dma((3 + heads,)), dma((3 + heads,)),
         dma((4, 3)), dma((4, 3)),
         dma((4, 3)), dma((4, 3)),

time: 179 us -> 173 us (0.966)
  Pallas kernels: 179 us -> 172 us
    pallas_call x1, Pallas kernels: 176 us -> 169 us  [step(): pl.pallas_call(functools.partial(kernel, dims), out_shape=(jax.ShapeDtype...]
where the time goes in v6:
time: 173 us
  Pallas kernels  172 us (99%)
    pallas_call x1, Pallas kernels, step(): pl.pallas_call(functools.partial(kernel, dims), out_shape=(jax.ShapeDtype...  169 us

profile of v6, /device:TPU:0, one launch (start us, length us, event | category | flops | bytes accessed | tf_op | source)
XLA Modules:
  0.0 172.6 jit_solution(2987671789989985126)
XLA Ops:
  0.6 169.1 %shard_map.118 = (bf16[128,1536]{1,0:T(8,128)(2,1)}, f32[128,1536]{1,0:T(8,128)}, f32[3,48,1536]{2,1,0:T(8,128)}) custom-call(bf16[128,1536]{1,0:T(8,128)(2,1)} %bitcast.22, f32[6,1,1536]{2,1,0:T(1,128)} %bitcast.27, bf16[3,48,384]{2,1,0:T(8,128)(2,1)} %bitcast.26, bf16[48,384]{1,0:T(8,128)(2,1)} %bitcast.28, bf16[48,1536]{1,0:T(8,128)(2,1)} %bitcast.24, ...), custom_call_target="tpu_custom_call" | custom-call | tf_op jit(solution)/shard_map/pallas_call | solution.py:685
  169.7 2.9 %shard_map.119 = (bf16[1,128,1536]{2,1,0:T(8,128)(2,1)}, f32[1,128,1536]{2,1,0:T(8,128)}, f32[3,48,384]{2,1,0:T(8,128)}, f32[48,384]{1,0:T(8,128)}, f32[1,48,1536]{2,1,0:T(8,128)}, /*index=5*/f32[48,1536]{1,0:T(8,128)}) custom-call(bf16[128,1536]{1,0:T(8,128)(2,1)} %get-tuple-element.15.fin, f32[128,1536]{1,0:T(8,128)} %get-tuple-element.16.dx, ...), custom_call_target="tpu_custom_call" | custom-call | tf_op jit(solution)/shard_map/pallas_call | solution.py:702

commit v7 on v6

--- a/solution.py
+++ b/solution.py
@@ -126,10 +126,11 @@
         piece = line_at(W.at[s], line, -k if recv else 0, ag_cols[s][color], at_rows(h if which == 0 else 1 - h))
         return copy(piece, piece, a2s.at[s, color, k - 1, which], a2r.at[s, color, k - 1, which], mid_dev(line, k))
 
-    def ag_last(s, color, d, recv):
+    def ag_last(s, color, d, j, recv):
         k, line = 1 - 2 * d, line_of(s, color)
-        piece = slab_at(W.at[s], line, -k if recv else 0, ag_cols[s][color], row=row_of(color))
-        return copy(piece, piece, a3s.at[s, color, d], a3r.at[s, color, d], last(line, k))
+        part = halves[d if j == 0 else 1 - d]
+        piece = slab_at(W.at[s], line, -k if recv else 0, ag_cols[s][color], part, row_of(color))
+        return copy(piece, piece, a3s.at[s, color, d, j], a3r.at[s, color, d, j], last(line, k))
 
     def ag_relay(s, color, d, recv):
         k, line = 1 - 2 * d, line_of(s, color)
@@ -148,23 +149,27 @@
             for which in (0, 1) if color < 2 else (0,):
                 for k in range(1, 4):
                     ag_mid(s, color, k, which, True).wait_recv()
-            for d in (0, 1):
-                ag_last(s, color, d, False).start()
+        for j in (0, 1):
+            for color in colors:
+                for d in (0, 1):
+                    ag_last(s, color, d, j, False).start()
 
     def ag_relay_start(s, colors=(0, 1)):
         for color in colors:
             for d in (0, 1):
-                ag_last(s, color, d, True).wait_recv()
+                ag_last(s, color, d, 0, True).wait_recv()
                 ag_relay(s, color, d, False).start()
 
     def ag_final_start(s):
         for d in (0, 1):
+            ag_last(s, 2, d, 1, True).wait_recv()
             ag_relay(s, 2, d, True).wait_recv()
         ag_final(s, False).start()
 
     def ag_wait(s):
         for color in (0, 1):
             for d in (0, 1):
+                ag_last(s, color, d, 1, True).wait_recv()
                 ag_relay(s, color, d, True).wait_recv()
 
     def ag_sent(s):
@@ -176,7 +181,8 @@
                 for k in range(1, 4):
                     ag_mid(s, color, k, which, False).wait_send()
             for d in (0, 1):
-                ag_last(s, color, d, False).wait_send()
+                for j in (0, 1):
+                    ag_last(s, color, d, j, False).wait_send()
                 ag_relay(s, color, d, False).wait_send()
 
     R1 = (R1A, R1B)
@@ -440,12 +446,12 @@
     ag_relay_start(0, (2,))
     ag_last_start(0)
     ag_relay_start(1, (2,))
-    ag_mid_start(2, 0)
-    ag_mid_start(2, 1)
     ag_final_start(0)
     gather_relay(0, A1)
     ag_relay_start(0)
     ag_last_start(1)
+    ag_mid_start(2, 0)
+    ag_mid_start(2, 1)
     ag_final_start(1)
     gather_start(1, DM)
     gather_wait(0, A1, 0)
@@ -474,11 +480,11 @@
         O[:, wide(hd)] = bf(dot(p, QKV[:, head(hd, 2)]))
 
     out_product = back_product(lambda i: O[pair_rows(i), :], 0, 3 * own, own)
-    ag_last_start(2)
     ag_final(0, True).wait_recv()
     scatter_far(0, out_product)
     scatter_near(0, out_product)
     ag_relay_start(1)
+    ag_last_start(2)
     mid = f32(tok[...]) + m[2] * scatter_result(0)
     MID[...] = mid
     n2, r2 = normalize(mid)
@@ -499,12 +505,12 @@
     gather_wait(1, DM, 0)
     gather_wait(1, DM, 2)
     turn(DM)
+    ag_wait(1)
+    ag_final(1, True).wait_recv()
+    gather_wait(2, A2, 0)
+    hidden(l)
     ag_relay_start(2)
     gather_relay(2, A2)
-    gather_wait(2, A2, 0)
-    ag_wait(1)
-    ag_final(1, True).wait_recv()
-    hidden(l)
     gather_wait(2, A2, 2)
     hidden(ol)
     for lo, hi in ((2 * side, width), (0, half), (half, 2 * side)):
@@ -672,7 +678,7 @@
         dma((6 + 3 * heads,)),
         dma((3, 2)), dma((3, 2)),
         dma((3, 3, 3, 2)), dma((3, 3, 3, 2)),
-        dma((3, 3, 2)), dma((3, 3, 2)),
+        dma((3, 3, 2, 2)), dma((3, 3, 2, 2)),
         dma((3, 3, 2)), dma((3, 3, 2)),
         dma((3 + heads, 3, 2, 3)), dma((3 + heads, 3, 2, 3)),
         dma((3 + heads, 3, 3)), dma((3 + heads, 3, 3)),

time: 173 us -> 169 us (0.977)
  Pallas kernels: 172 us -> 167 us
    pallas_call x1, Pallas kernels: 169 us -> 164 us  [step(): pl.pallas_call(functools.partial(kernel, dims), out_shape=(jax.ShapeDtype...]
where the time goes in v7:
time: 169 us; the launch traced here: 167 us
  Pallas kernels  167 us (99%)
    pallas_call x1, Pallas kernels, step(): pl.pallas_call(functools.partial(kernel, dims), out_shape=(jax.ShapeDtype...  164 us

profile of v7, /device:TPU:0, one launch (start us, length us, event | category | flops | bytes accessed | tf_op | source)
XLA Modules:
  0.0 167.2 jit_solution(3595660503379563941)
XLA Ops:
  0.6 163.7 %shard_map.118 = (bf16[128,1536]{1,0:T(8,128)(2,1)}, f32[128,1536]{1,0:T(8,128)}, f32[3,48,1536]{2,1,0:T(8,128)}) custom-call(bf16[128,1536]{1,0:T(8,128)(2,1)} %bitcast.22, f32[6,1,1536]{2,1,0:T(1,128)} %bitcast.27, bf16[3,48,384]{2,1,0:T(8,128)(2,1)} %bitcast.26, bf16[48,384]{1,0:T(8,128)(2,1)} %bitcast.28, bf16[48,1536]{1,0:T(8,128)(2,1)} %bitcast.24, ...), custom_call_target="tpu_custom_call" | custom-call | tf_op jit(solution)/shard_map/pallas_call | solution.py:691
  164.3 2.9 %shard_map.119 = (bf16[1,128,1536]{2,1,0:T(8,128)(2,1)}, f32[1,128,1536]{2,1,0:T(8,128)}, f32[3,48,384]{2,1,0:T(8,128)}, f32[48,384]{1,0:T(8,128)}, f32[1,48,1536]{2,1,0:T(8,128)}, /*index=5*/f32[48,1536]{1,0:T(8,128)}) custom-call(bf16[128,1536]{1,0:T(8,128)(2,1)} %get-tuple-element.15.fin, f32[128,1536]{1,0:T(8,128)} %get-tuple-element.16.dx, ...), custom_call_target="tpu_custom_call" | custom-call | tf_op jit(solution)/shard_map/pallas_call | solution.py:708

commit v8 on v7

--- a/solution.py
+++ b/solution.py
@@ -51,7 +51,7 @@
 def kernel(
     dims, tok_in, mod_in, wq_in, wo_in, wi_in, wb_in, og_in, fin, dxin, grads,
     W, G, R1A, R1B, R2A, R2B, R3, R1C, R2C, R4, R4H, A1, A2, DM, DA, GG, DU, QKV, DQKV, O, DO, PR, PS, RX, SX, MID, DX, AT,
-    tok, mod, og, in_sem, a1s, a1r, a2s, a2r, a3s, a3r, a4s, a4r, r1s, r1r, r2s, r2r, r3s, r3r, r4s, r4r, gs, gr, ss, sr,
+    tok, mod, og, in_sem, a1s, a1r, a2s, a2r, a3s, a3r, a4s, a4r, a5s, a5r, r1s, r1r, r2s, r2r, r3s, r3r, r4s, r4r, r5s, r5r, gs, gr, ss, sr,
 ):
     nz, ny, nh = dims
     z, y, h, l, c = (lax.axis_index(a) for a in AXES)
@@ -126,6 +126,11 @@
         piece = line_at(W.at[s], line, -k if recv else 0, ag_cols[s][color], at_rows(h if which == 0 else 1 - h))
         return copy(piece, piece, a2s.at[s, color, k - 1, which], a2r.at[s, color, k - 1, which], mid_dev(line, k))
 
+    def ag_hop(s, color, d, recv):
+        k = 1 - 2 * d
+        piece = line_at(W.at[s], color, 2 if recv else -k, ag_cols[s][color], at_rows(d))
+        return copy(piece, piece, a5s.at[s, color, d], a5r.at[s, color, d], mid_dev(color, k))
+
     def ag_last(s, color, d, j, recv):
         k, line = 1 - 2 * d, line_of(s, color)
         part = halves[d if j == 0 else 1 - d]
@@ -140,15 +145,29 @@
     def ag_mid_start(s, which, colors=(0, 1)):
         if which:
             ag_pair(s, True).wait_recv()
-        for k in (1, 3, 2):
+        for k in (1, 3, 2) if direct(s, colors[0]) else (1, 3):
             for color in colors:
                 ag_mid(s, color, k, which, False).start()
 
+    def direct(s, color):
+        return s != 1 or color == 2
+
+    def ag_hop_start(s):
+        for color in (0, 1):
+            for d in (0, 1):
+                for which in (0, 1):
+                    ag_mid(s, color, 1 + 2 * d, which, True).wait_recv()
+                ag_hop(s, color, d, False).start()
+
     def ag_last_start(s, colors=(0, 1)):
         for color in colors:
-            for which in (0, 1) if color < 2 else (0,):
-                for k in range(1, 4):
-                    ag_mid(s, color, k, which, True).wait_recv()
+            if direct(s, color):
+                for which in (0, 1) if color < 2 else (0,):
+                    for k in range(1, 4):
+                        ag_mid(s, color, k, which, True).wait_recv()
+            else:
+                for d in (0, 1):
+                    ag_hop(s, color, d, True).wait_recv()
         for j in (0, 1):
             for color in colors:
                 for d in (0, 1):
@@ -178,8 +197,11 @@
             ag_final(s, False).wait_send()
         for color in (0, 1, 2) if s < 2 else (0, 1):
             for which in (0, 1) if color < 2 else (0,):
-                for k in range(1, 4):
+                for k in (1, 2, 3) if direct(s, color) else (1, 3):
                     ag_mid(s, color, k, which, False).wait_send()
+            if not direct(s, color):
+                for d in (0, 1):
+                    ag_hop(s, color, d, False).wait_send()
             for d in (0, 1):
                 for j in (0, 1):
                     ag_last(s, color, d, j, False).wait_send()
@@ -233,6 +255,26 @@
             r2s.at[s, color, k - 1], r2r.at[s, color, k - 1], mid_dev(line, k),
         )
 
+    def ringed(s, color):
+        return s < 2 and color < 2
+
+    def rs_hop(s, color, d, kind):
+        k = 1 - 2 * d
+        row = at_rows(1 - d if kind == 1 else d)
+        src = line_at(parts[s], color, 2 if kind == 0 else k, grad_cols[s][color], row)
+        dst = r2_at(s, color).at[2 if kind == 0 else d, row]
+        return copy(src, dst, r5s.at[s, color, d, kind], r5r.at[s, color, d, kind], mid_dev(color, k))
+
+    def rs_hop_combine(s):
+        for color in (0, 1):
+            for d in (0, 1):
+                rs_hop(s, color, d, 0).wait_recv()
+                k = 1 - 2 * d
+                at = (z, yy(k)) if color == 0 else (zz(k), y)
+                at = (*at, at_rows(d), grad_cols[s][color])
+                parts[s][at] = bf(f32(parts[s][at]) + f32(r2_at(s, color)[2, d * rows : (d + 1) * rows]))
+                rs_hop(s, color, d, 2).start()
+
     def rs_pair(s):
         return copy(
             parts[s].at[z, y, at_rows(1 - h), pair_cols[s]], R3.at[slots[s], :, pair_cols[s]],
@@ -286,14 +328,24 @@
                     total = total + f32(r1_at(s, color)[d, i])
                 parts[s][at] = bf(total)
 
-            for k in (1, 3, 2):
-                rs_mid(s, color, k).start()
+            if ringed(s, color):
+                for kind in (0, 1):
+                    for d in (0, 1):
+                        rs_hop(s, color, d, kind).start()
+            else:
+                for k in (1, 3, 2):
+                    rs_mid(s, color, k).start()
 
     def rs_total(s, color):
-        for k in range(1, 4):
-            rs_mid(s, color, k).wait_recv()
+        if ringed(s, color):
+            for d in (0, 1):
+                for kind in (1, 2):
+                    rs_hop(s, color, d, kind).wait_recv()
+        else:
+            for k in range(1, 4):
+                rs_mid(s, color, k).wait_recv()
         total = f32(parts[s][z, y, row_of(color), grad_cols[s][color]])
-        for k in range(3):
+        for k in range(2 if ringed(s, color) else 3):
             total = total + f32(r2_at(s, color)[k])
         return total
 
@@ -315,8 +367,13 @@
             for d in (0, 1):
                 for kind in (0, 1, 2):
                     rs_ring(s, color, d, kind).wait_send()
-            for k in range(1, 4):
-                rs_mid(s, color, k).wait_send()
+            if ringed(s, color):
+                for d in (0, 1):
+                    for kind in (0, 1, 2):
+                        rs_hop(s, color, d, kind).wait_send()
+            else:
+                for k in range(1, 4):
+                    rs_mid(s, color, k).wait_send()
         if s != 1:
             rs_first(s).wait_send()
         rs_pair(s).wait_send()
@@ -444,16 +501,17 @@
     ag_mid_start(1, 1)
     ag_last_start(1, (2,))
     ag_relay_start(0, (2,))
+    ag_hop_start(1)
     ag_last_start(0)
     ag_relay_start(1, (2,))
     ag_final_start(0)
     gather_relay(0, A1)
+    gather_start(1, DM)
     ag_relay_start(0)
-    ag_last_start(1)
     ag_mid_start(2, 0)
     ag_mid_start(2, 1)
+    ag_last_start(1)
     ag_final_start(1)
-    gather_start(1, DM)
     gather_wait(0, A1, 0)
     gather_wait(0, A1, 2)
 
@@ -576,6 +634,7 @@
     qkv_back = back_product(lambda i: DQKV[pair_rows(i), :], 0, 0, 3 * own)
     fin[...] = bf(MID[...] + m[5] * scatter_result(2))
     scatter_far(3, qkv_back)
+    rs_hop_combine(0)
     rs_second(2)
     rs_combine(2)
     rs_mid_start(1)
@@ -586,31 +645,32 @@
     rs_combine(4)
     rs_combine(2, (2,))
     rs_second(4)
-    rs_pair_start(0)
     rs_combine(5)
     rs_mid_start(2)
+    rs_pair_start(0)
     rs_second(5)
+    rs_hop_combine(1)
     rs_combine(3, (2,))
     rs_mid_start(3)
     rs_finish_third(0)
     rs_mid_start(2, (2,))
     rs_combine(4, (2,))
+    rs_mid_start(4)
+    rs_mid_start(3, (2,))
     e1 = scatter_result(3) * (1.0 + m[1])
     n1, r1 = normalize(f32(tok[...]))
     dxin[...] = DX[...] + norm_back(n1, r1, e1)
-    rs_mid_start(4)
-    rs_mid_start(3, (2,))
+    rs_pair_start(1)
     rs_combine(5, (2,))
     rs_mid_start(5)
-    rs_pair_start(1)
     rs_finish(0)
     rs_pair_start(2)
     rs_mid_start(4, (2,))
     rs_pair_start(3)
     rs_mid_start(5, (2,))
     rs_pair_start(4)
+    rs_pair_start(5)
     rs_finish(1)
-    rs_pair_start(5)
     for s in range(2, sections):
         rs_finish_third(s)
     for s in range(2, sections):
@@ -680,10 +740,12 @@
         dma((3, 3, 3, 2)), dma((3, 3, 3, 2)),
         dma((3, 3, 2, 2)), dma((3, 3, 2, 2)),
         dma((3, 3, 2)), dma((3, 3, 2)),
+        dma((3, 2, 2)), dma((3, 2, 2)),
         dma((3 + heads, 3, 2, 3)), dma((3 + heads, 3, 2, 3)),
         dma((3 + heads, 3, 3)), dma((3 + heads, 3, 3)),
         dma((3 + heads,)), dma((3 + heads,)),
         dma((3 + heads,)), dma((3 + heads,)),
+        dma((2, 2, 2, 3)), dma((2, 2, 2, 3)),
         dma((4, 3)), dma((4, 3)),
         dma((4, 3)), dma((4, 3)),
     ]

time: 169 us -> 167 us (0.988)
  Pallas kernels: 167 us -> 164 us
    pallas_call x1, Pallas kernels: 164 us -> 161 us  [step(): pl.pallas_call(functools.partial(kernel, dims), out_shape=(jax.ShapeDtype...]
where the time goes in v8:
time: 167 us; the launch traced here: 165 us
  Pallas kernels  164 us (98%)
    pallas_call x1, Pallas kernels, step(): pl.pallas_call(functools.partial(kernel, dims), out_shape=(jax.ShapeDtype...  161 us

profile of v8, /device:TPU:0, one launch (start us, length us, event | category | flops | bytes accessed | tf_op | source)
XLA Modules:
  0.0 164.6 jit_solution(14648233707415253567)
XLA Ops:
  0.6 161.0 %shard_map.118 = (bf16[128,1536]{1,0:T(8,128)(2,1)}, f32[128,1536]{1,0:T(8,128)}, f32[3,48,1536]{2,1,0:T(8,128)}) custom-call(bf16[128,1536]{1,0:T(8,128)(2,1)} %bitcast.22, f32[6,1,1536]{2,1,0:T(1,128)} %bitcast.27, bf16[3,48,384]{2,1,0:T(8,128)(2,1)} %bitcast.26, bf16[48,384]{1,0:T(8,128)(2,1)} %bitcast.28, bf16[48,1536]{1,0:T(8,128)(2,1)} %bitcast.24, ...), custom_call_target="tpu_custom_call" | custom-call | tf_op jit(solution)/shard_map/pallas_call | solution.py:753
  161.7 2.9 %shard_map.119 = (bf16[1,128,1536]{2,1,0:T(8,128)(2,1)}, f32[1,128,1536]{2,1,0:T(8,128)}, f32[3,48,384]{2,1,0:T(8,128)}, f32[48,384]{1,0:T(8,128)}, f32[1,48,1536]{2,1,0:T(8,128)}, /*index=5*/f32[48,1536]{1,0:T(8,128)}) custom-call(bf16[128,1536]{1,0:T(8,128)(2,1)} %get-tuple-element.15.fin, f32[128,1536]{1,0:T(8,128)} %get-tuple-element.16.dx, ...), custom_call_target="tpu_custom_call" | custom-call | tf_op jit(solution)/shard_map/pallas_call | solution.py:770

commit v9 on v8

--- a/solution.py
+++ b/solution.py
@@ -48,10 +48,31 @@
     return g, d
 
 
+class copy:
+    def __init__(self, src, dst, ssem, rsem, dev):
+        self.src, self.rest = src, (dst, ssem, rsem, dev)
+
+    def made(self):
+        dst, ssem, rsem, dev = self.rest
+        return pltpu.make_async_remote_copy(
+            src_ref=self.src, dst_ref=dst, send_sem=ssem, recv_sem=rsem,
+            device_id=dev, device_id_type=pl.DeviceIdType.MESH,
+        )
+
+    def start(self):
+        self.made().start()
+
+    def wait_send(self):
+        self.made().wait_send()
+
+    def wait_recv(self):
+        self.made().wait_recv()
+
+
 def kernel(
-    dims, tok_in, mod_in, wq_in, wo_in, wi_in, wb_in, og_in, fin, dxin, grads,
+    dims, tok_in, mod_in, wq_in, wo_in, wi_in, wb_in, og_in, fin_out, dx_out, grads_out,
     W, G, R1A, R1B, R2A, R2B, R3, R1C, R2C, R4, R4H, A1, A2, DM, DA, GG, DU, QKV, DQKV, O, DO, PR, PS, RX, SX, MID, DX, AT,
-    tok, mod, og, in_sem, a1s, a1r, a2s, a2r, a3s, a3r, a4s, a4r, a5s, a5r, r1s, r1r, r2s, r2r, r3s, r3r, r4s, r4r, r5s, r5r, gs, gr, ss, sr,
+    tok, mod, og, fin, dxin, grads, in_sem, out_sem, ags, a1r, a2r, a3r, a4r, a5r, rss, r1r, r2r, r3r, r4r, r5r, gs, gr, ss, sr,
 ):
     nz, ny, nh = dims
     z, y, h, l, c = (lax.axis_index(a) for a in AXES)
@@ -67,11 +88,17 @@
     q_s = 1.0 / math.sqrt(seq * nz * ny * nh)
     cols = (pl.ds(0, half), pl.ds(half, half))
 
-    def copy(src, dst, ssem, rsem, dev):
-        return pltpu.make_async_remote_copy(
-            src_ref=src, dst_ref=dst, send_sem=ssem, recv_sem=rsem,
-            device_id=dev, device_id_type=pl.DeviceIdType.MESH,
-        )
+    def drain(sem, moves):
+        units = sum(math.prod(move.src.shape) for move in moves) // (rows * 128)
+        for height in (rows, nh * rows):
+            for i in range(1, nz + 1):
+                for j in range(1, ny + 1):
+                    n, rest = divmod(units * rows, height * i * j)
+                    if rest == 0 and n <= width // 128:
+                        view = W.at[0, pl.ds(0, i), pl.ds(0, j), pl.ds(0, height), pl.ds(0, n * 128)]
+                        pltpu.make_async_copy(view, view, sem).wait()
+                        return
+        raise ValueError(units)
 
     def zz(k):
         return lax.rem(z + k + nz, nz)
@@ -113,34 +140,39 @@
     def row_of(color):
         return every if color < 2 else at_rows(h)
 
+    def direct(s, color):
+        return s == 0 or color == 2
+
     def ag_pair(s, recv):
         piece = W.at[s, z, y, at_rows(1 - h if recv else h), pl.ds(0, 2 * side if s < 2 else width)]
-        return copy(piece, piece, a1s.at[s, 0], a1r.at[s, 0], pair_peer)
+        return copy(piece, piece, ags.at[s, 0], a1r.at[s, 0], pair_peer)
 
     def ag_final(s, recv):
         piece = W.at[s, :, :, at_rows(1 - h if recv else h), ag_cols[s][2]]
-        return copy(piece, piece, a1s.at[s, 1], a1r.at[s, 1], pair_peer)
+        return copy(piece, piece, ags.at[s, 1], a1r.at[s, 1], pair_peer)
 
     def ag_mid(s, color, k, which, recv):
         line = line_of(s, color)
         piece = line_at(W.at[s], line, -k if recv else 0, ag_cols[s][color], at_rows(h if which == 0 else 1 - h))
-        return copy(piece, piece, a2s.at[s, color, k - 1, which], a2r.at[s, color, k - 1, which], mid_dev(line, k))
+        side_of = 0 if direct(s, color) else (k - 1) // 2
+        return copy(piece, piece, ags.at[s, 2 + 2 * (color // 2)], a2r.at[s, color, side_of], mid_dev(line, k))
 
     def ag_hop(s, color, d, recv):
         k = 1 - 2 * d
         piece = line_at(W.at[s], color, 2 if recv else -k, ag_cols[s][color], at_rows(d))
-        return copy(piece, piece, a5s.at[s, color, d], a5r.at[s, color, d], mid_dev(color, k))
+        return copy(piece, piece, ags.at[s, 2], a5r.at[s, color], mid_dev(color, k))
 
     def ag_last(s, color, d, j, recv):
         k, line = 1 - 2 * d, line_of(s, color)
         part = halves[d if j == 0 else 1 - d]
         piece = slab_at(W.at[s], line, -k if recv else 0, ag_cols[s][color], part, row_of(color))
-        return copy(piece, piece, a3s.at[s, color, d, j], a3r.at[s, color, d, j], last(line, k))
+        arrived = a3r.at[s, color, d] if j == 0 else a4r.at[s, color // 2]
+        return copy(piece, piece, ags.at[s, 3 + color // 2], arrived, last(line, k))
 
     def ag_relay(s, color, d, recv):
         k, line = 1 - 2 * d, line_of(s, color)
         piece = slab_at(W.at[s], line, 2 if recv else -k, ag_cols[s][color], halves[d], row_of(color))
-        return copy(piece, piece, a4s.at[s, color, d], a4r.at[s, color, d], last(line, k))
+        return copy(piece, piece, ags.at[s, 3 + color // 2], a4r.at[s, color // 2], last(line, k))
 
     def ag_mid_start(s, which, colors=(0, 1)):
         if which:
@@ -149,25 +181,19 @@
             for color in colors:
                 ag_mid(s, color, k, which, False).start()
 
-    def direct(s, color):
-        return s != 1 or color == 2
-
     def ag_hop_start(s):
         for color in (0, 1):
             for d in (0, 1):
-                for which in (0, 1):
-                    ag_mid(s, color, 1 + 2 * d, which, True).wait_recv()
+                drain(a2r.at[s, color, d], [ag_mid(s, color, 1 + 2 * d, which, True) for which in (0, 1)])
                 ag_hop(s, color, d, False).start()
 
     def ag_last_start(s, colors=(0, 1)):
         for color in colors:
             if direct(s, color):
-                for which in (0, 1) if color < 2 else (0,):
-                    for k in range(1, 4):
-                        ag_mid(s, color, k, which, True).wait_recv()
+                sides = (0, 1) if color < 2 else (0,)
+                drain(a2r.at[s, color, 0], [ag_mid(s, color, k, which, True) for which in sides for k in (1, 2, 3)])
             else:
-                for d in (0, 1):
-                    ag_hop(s, color, d, True).wait_recv()
+                drain(a5r.at[s, color], [ag_hop(s, color, d, True) for d in (0, 1)])
         for j in (0, 1):
             for color in colors:
                 for d in (0, 1):
@@ -179,33 +205,33 @@
                 ag_last(s, color, d, 0, True).wait_recv()
                 ag_relay(s, color, d, False).start()
 
+    def late(s, colors):
+        return [move for color in colors for d in (0, 1)
+                for move in (ag_last(s, color, d, 1, True), ag_relay(s, color, d, True))]
+
     def ag_final_start(s):
-        for d in (0, 1):
-            ag_last(s, 2, d, 1, True).wait_recv()
-            ag_relay(s, 2, d, True).wait_recv()
+        drain(a4r.at[s, 1], late(s, (2,)))
         ag_final(s, False).start()
 
     def ag_wait(s):
-        for color in (0, 1):
-            for d in (0, 1):
-                ag_last(s, color, d, 1, True).wait_recv()
-                ag_relay(s, color, d, True).wait_recv()
+        drain(a4r.at[s, 0], late(s, (0, 1)))
 
     def ag_sent(s):
         ag_pair(s, False).wait_send()
+        middle = [ag_mid(s, color, k, which, False) for color in (0, 1) for which in (0, 1)
+                  for k in ((1, 2, 3) if direct(s, 0) else (1, 3))]
+        if not direct(s, 0):
+            middle += [ag_hop(s, color, d, False) for color in (0, 1) for d in (0, 1)]
+        drain(ags.at[s, 2], middle)
+
+        def ends(colors):
+            return [ag_last(s, color, d, j, False) for color in colors for d in (0, 1) for j in (0, 1)] + [
+                ag_relay(s, color, d, False) for color in colors for d in (0, 1)]
+
+        drain(ags.at[s, 3], ends((0, 1)))
         if s < 2:
             ag_final(s, False).wait_send()
-        for color in (0, 1, 2) if s < 2 else (0, 1):
-            for which in (0, 1) if color < 2 else (0,):
-                for k in (1, 2, 3) if direct(s, color) else (1, 3):
-                    ag_mid(s, color, k, which, False).wait_send()
-            if not direct(s, color):
-                for d in (0, 1):
-                    ag_hop(s, color, d, False).wait_send()
-            for d in (0, 1):
-                for j in (0, 1):
-                    ag_last(s, color, d, j, False).wait_send()
-                ag_relay(s, color, d, False).wait_send()
+            drain(ags.at[s, 4], [ag_mid(s, 2, k, 0, False) for k in (1, 2, 3)] + ends((2,)))
 
     R1 = (R1A, R1B)
     R2 = (R2A, R2B)
@@ -220,39 +246,48 @@
     third = own // 3
     for i, start in enumerate([full] + [hd * own for hd in range(heads)]):
         at = pl.ds(i * third, third)
-        local_cols.append((at, at, pl.ds((4 + i // 2) * third, third)))
+        local_cols.append((at, at))
         grad_cols.append(tuple(pl.ds(start + j * third, third) for j in range(3)))
         pair_cols.append(pl.ds(start, 2 * third))
+
+    spare = {2: (1, 4), 3: (1, 5), 4: (0, 4), 5: (0, 5)}
+
+    def rs_line(s, color):
+        return color if color < 2 else (0, None, 1, 1, 0, 1)[s]
+
+    def spare_at(s):
+        return pl.ds(spare[s][1] * third, third)
 
     def r1_at(s, color):
         if color < 2:
             return R1[color].at[slots[s], :, :, :, local_cols[s][color]]
-        return R1C if s == 0 else R1[s % 2].at[0, :, :, pl.ds(0, rows), local_cols[s][2]]
+        return R1C if s == 0 else R1[spare[s][0]].at[0, :, :, pl.ds(0, rows), spare_at(s)]
 
     def r2_at(s, color):
         if color < 2:
             return R2[color].at[slots[s], :, :, local_cols[s][color]]
-        return R2C if s == 0 else R2[s % 2].at[0, :, pl.ds(0, rows), local_cols[s][2]]
+        return R2C if s == 0 else R2[spare[s][0]].at[0, :, pl.ds(0, rows), spare_at(s)]
 
     def r4_at(s):
         return R4 if s == 0 else R4H.at[s - 2]
 
     def rs_first(s):
         src = parts[s].at[:, :, at_rows(1 - h), grad_cols[s][2]]
-        return copy(src, r4_at(s), r4s.at[s], r4r.at[s], pair_peer)
+        return copy(src, r4_at(s), rss.at[s, 5], r4r.at[s], pair_peer)
 
     def rs_ring(s, color, d, kind):
-        k, line = 1 - 2 * d, line_of(s, color)
+        k, line = 1 - 2 * d, rs_line(s, color)
         part = halves[1 - d if kind == 1 else d]
         src = slab_at(parts[s], line, 2 if kind == 0 else k, grad_cols[s][color], part, row_of(color))
         dst = r1_at(s, color).at[2 if kind == 0 else d, part]
-        return copy(src, dst, r1s.at[s, color, d, kind], r1r.at[s, color, d, kind], last(line, k))
+        arrived = r1r.at[s, color, d if kind == 0 else 2]
+        return copy(src, dst, rss.at[s, color // 2], arrived, last(line, k))
 
     def rs_mid(s, color, k):
-        line = line_of(s, color)
+        line = rs_line(s, color)
         return copy(
             line_at(parts[s], line, k, grad_cols[s][color], row_of(color)), r2_at(s, color).at[k - 1],
-            r2s.at[s, color, k - 1], r2r.at[s, color, k - 1], mid_dev(line, k),
+            rss.at[s, 2 + color // 2], r2r.at[s, color], mid_dev(line, k),
         )
 
     def ringed(s, color):
@@ -263,7 +298,8 @@
         row = at_rows(1 - d if kind == 1 else d)
         src = line_at(parts[s], color, 2 if kind == 0 else k, grad_cols[s][color], row)
         dst = r2_at(s, color).at[2 if kind == 0 else d, row]
-        return copy(src, dst, r5s.at[s, color, d, kind], r5r.at[s, color, d, kind], mid_dev(color, k))
+        arrived = r5r.at[s, color, d if kind == 0 else 2]
+        return copy(src, dst, rss.at[s, 2], arrived, mid_dev(color, k))
 
     def rs_hop_combine(s):
         for color in (0, 1):
@@ -278,7 +314,7 @@
     def rs_pair(s):
         return copy(
             parts[s].at[z, y, at_rows(1 - h), pair_cols[s]], R3.at[slots[s], :, pair_cols[s]],
-            r3s.at[s], r3r.at[s], pair_peer,
+            rss.at[s, 4], r3r.at[s], pair_peer,
         )
 
     def rs_second(s):
@@ -299,7 +335,7 @@
 
     def rs_combine(s, colors=(0, 1)):
         for color in colors:
-            line = line_of(s, color)
+            line = rs_line(s, color)
             for d in (0, 1):
                 rs_ring(s, color, d, 0).wait_recv()
                 k = 1 - 2 * d
@@ -314,10 +350,8 @@
 
     def rs_mid_start(s, colors=(0, 1)):
         for color in colors:
-            line = line_of(s, color)
-            for d in (0, 1):
-                for kind in (1, 2):
-                    rs_ring(s, color, d, kind).wait_recv()
+            line = rs_line(s, color)
+            drain(r1r.at[s, color, 2], [rs_ring(s, color, d, kind) for d in (0, 1) for kind in (1, 2)])
 
             @pl.loop(0, 4)
             def _(i):
@@ -338,12 +372,9 @@
 
     def rs_total(s, color):
         if ringed(s, color):
-            for d in (0, 1):
-                for kind in (1, 2):
-                    rs_hop(s, color, d, kind).wait_recv()
+            drain(r5r.at[s, color, 2], [rs_hop(s, color, d, kind) for d in (0, 1) for kind in (1, 2)])
         else:
-            for k in range(1, 4):
-                rs_mid(s, color, k).wait_recv()
+            drain(r2r.at[s, color], [rs_mid(s, color, k) for k in (1, 2, 3)])
         total = f32(parts[s][z, y, row_of(color), grad_cols[s][color]])
         for k in range(2 if ringed(s, color) else 3):
             total = total + f32(r2_at(s, color)[k])
@@ -363,17 +394,14 @@
         grads[slots[s], :, grad_cols[s][2]] = rs_total(s, 2)
 
     def rs_sent(s):
-        for color in (0, 1) if s == 1 else (0, 1, 2):
-            for d in (0, 1):
-                for kind in (0, 1, 2):
-                    rs_ring(s, color, d, kind).wait_send()
-            if ringed(s, color):
-                for d in (0, 1):
-                    for kind in (0, 1, 2):
-                        rs_hop(s, color, d, kind).wait_send()
+        for colors in ((0, 1),) if s == 1 else ((0, 1), (2,)):
+            rings = [rs_ring(s, color, d, kind) for color in colors for d in (0, 1) for kind in (0, 1, 2)]
+            drain(rss.at[s, colors[0] // 2], rings)
+            if ringed(s, colors[0]):
+                middle = [rs_hop(s, color, d, kind) for color in colors for d in (0, 1) for kind in (0, 1, 2)]
             else:
-                for k in range(1, 4):
-                    rs_mid(s, color, k).wait_send()
+                middle = [rs_mid(s, color, k) for color in colors for k in (1, 2, 3)]
+            drain(rss.at[s, 2 + colors[0] // 2], middle)
         if s != 1:
             rs_first(s).wait_send()
         rs_pair(s).wait_send()
@@ -385,7 +413,7 @@
             piece, dev = buf.at[ol if recv else l, c], line_peer
         else:
             piece, dev = buf.at[ol, oc if recv else c], core_peer
-        return copy(piece, piece, gs.at[i, step], gr.at[i, step], dev)
+        return copy(piece, piece, gs.at[i], gr.at[i, step], dev)
 
     def gather_start(i, buf):
         g_copy(i, buf, 1, False).start()
@@ -399,8 +427,7 @@
         g_copy(i, buf, step, True).wait_recv()
 
     def gather_sent(i, buf):
-        for step in range(3):
-            g_copy(i, buf, step, False).wait_send()
+        drain(gs.at[i], [g_copy(i, buf, step, False) for step in range(3)])
 
     def s_copy(i, step):
         src, dev = (
@@ -408,7 +435,7 @@
             (SX, line_peer),
             (PS.at[l, oc], core_peer),
         )[step]
-        return copy(src, RX.at[i % 2, step], ss.at[i, step], sr.at[i, step], dev)
+        return copy(src, RX.at[i % 2, step], ss.at[i], sr.at[i, step], dev)
 
     def scatter_far(i, compute):
         compute(ol)
@@ -425,8 +452,7 @@
         s_copy(i, 2).wait_recv()
         s_copy(i, 1).wait_recv()
         total = f32(PS[l, c]) + f32(RX[i % 2, 2]) + f32(RX[i % 2, 1])
-        for step in range(3):
-            s_copy(i, step).wait_send()
+        drain(ss.at[i], [s_copy(i, step) for step in range(3)])
         return total
 
     def pair_rows(i):
@@ -471,6 +497,8 @@
     barrier = pltpu.get_barrier_semaphore()
     for dev in peers:
         pl.semaphore_signal(barrier, inc=1, device_id=dev, device_id_type=pl.DeviceIdType.MESH)
+    outs = [(fin, fin_out), (dxin, dx_out)] + [(grads.at[i], grads_out.at[i]) for i in range(3)]
+    results = [pltpu.make_async_copy(src, dst, out_sem.at[i]) for i, (src, dst) in enumerate(outs)]
     mine = at_rows(h)
     moves = [
         (wq_in.at[i, :, pl.ds(hd * HEAD_DIM, HEAD_DIM)], W.at[0, z, y, mine, pl.ds((3 * hd + i) * HEAD_DIM, HEAD_DIM)])
@@ -495,6 +523,7 @@
     for s in (0, 1):
         ag_mid_start(s, 0, (2,))
         ag_mid_start(s, 0)
+    ag_mid_start(2, 0)
     gather_start(0, A1)
     ag_last_start(0, (2,))
     ag_mid_start(0, 1)
@@ -508,7 +537,6 @@
     gather_relay(0, A1)
     gather_start(1, DM)
     ag_relay_start(0)
-    ag_mid_start(2, 0)
     ag_mid_start(2, 1)
     ag_last_start(1)
     ag_final_start(1)
@@ -522,6 +550,8 @@
         at = pl.ds(pl.multiple_of(t * own, 128), own)
         w = W[0, :, :, :, at].reshape(width, own)
         QKV[:, at] = bf(dot(A1[...].reshape(seq, width), w))
+
+    ag_hop_start(2)
 
     def head(hd, i):
         return pl.ds(pl.multiple_of((3 * hd + i) * HEAD_DIM, 128), HEAD_DIM)
@@ -633,6 +663,7 @@
 
     qkv_back = back_product(lambda i: DQKV[pair_rows(i), :], 0, 0, 3 * own)
     fin[...] = bf(MID[...] + m[5] * scatter_result(2))
+    results[0].start()
     scatter_far(3, qkv_back)
     rs_hop_combine(0)
     rs_second(2)
@@ -660,10 +691,12 @@
     e1 = scatter_result(3) * (1.0 + m[1])
     n1, r1 = normalize(f32(tok[...]))
     dxin[...] = DX[...] + norm_back(n1, r1, e1)
+    results[1].start()
     rs_pair_start(1)
     rs_combine(5, (2,))
     rs_mid_start(5)
     rs_finish(0)
+    results[4].start()
     rs_pair_start(2)
     rs_mid_start(4, (2,))
     rs_pair_start(3)
@@ -671,29 +704,50 @@
     rs_pair_start(4)
     rs_pair_start(5)
     rs_finish(1)
+    results[3].start()
     for s in range(2, sections):
         rs_finish_third(s)
     for s in range(2, sections):
         rs_finish(s)
+    results[2].start()
     for s in range(sections):
         rs_sent(s)
     ag_sent(0)
     ag_sent(2)
     for i, buf in enumerate((A1, DM, A2, DA)):
         gather_sent(i, buf)
-
-
-def place(fin, dx, grads, o_fin, o_dx, o_qkv, o_out, o_in, o_back):
+    for result in results:
+        result.wait()
+
+
+def place(fin, dx, grads, o_fin, o_dx, o_qkv, o_out, o_in, o_back, v_fin, v_dx, v_grads, sem_in, sem_out):
     own = o_out.shape[1]
-    o_fin[0] = fin[...]
-    o_dx[0] = dx[...]
-    for i in range(3):
-        for hd in range(own // HEAD_DIM):
-            at = (3 * hd + i) * HEAD_DIM
-            o_qkv[i, :, hd * HEAD_DIM : (hd + 1) * HEAD_DIM] = grads[0, :, at : at + HEAD_DIM]
-    o_out[...] = grads[0, :, 3 * own :]
-    o_in[0] = grads[1]
-    o_back[...] = grads[2]
+    heads = own // HEAD_DIM
+    sources = (
+        (dx, v_dx), (grads.at[2], v_grads.at[2]), (grads.at[1], v_grads.at[1]),
+        (fin, v_fin), (grads.at[0], v_grads.at[0]),
+    )
+    pieces = [
+        (v_grads.at[0, :, pl.ds((3 * hd + i) * HEAD_DIM, HEAD_DIM)], o_qkv.at[i, :, pl.ds(hd * HEAD_DIM, HEAD_DIM)])
+        for i in range(3) for hd in range(heads)
+    ]
+    pieces.append((v_grads.at[0, :, pl.ds(3 * own, own)], o_out))
+    targets = (
+        [(v_dx, o_dx.at[0])], [(v_grads.at[2], o_back)], [(v_grads.at[1], o_in.at[0])],
+        [(v_fin, o_fin.at[0])], pieces,
+    )
+    loads = [pltpu.make_async_copy(a, b, sem_in.at[i]) for i, (a, b) in enumerate(sources)]
+    for load in loads:
+        load.start()
+    stores = []
+    for load, pairs in zip(loads, targets):
+        load.wait()
+        for a, b in pairs:
+            store = pltpu.make_async_copy(a, b, sem_out.at[len(stores)])
+            store.start()
+            stores.append(store)
+    for store in stores:
+        store.wait()
 
 
 def step(dims, tokens, modulation, w_qkv, w_out, w_in, w_back, out_grad):
@@ -735,21 +789,17 @@
         vmem((count, width), BF),
         vmem((6, 1, width), F32),
         vmem((count, width), BF),
+        vmem((count, width), BF),
+        vmem((count, width), F32),
+        vmem((3, rows, width), F32),
         dma((6 + 3 * heads,)),
-        dma((3, 2)), dma((3, 2)),
-        dma((3, 3, 3, 2)), dma((3, 3, 3, 2)),
-        dma((3, 3, 2, 2)), dma((3, 3, 2, 2)),
-        dma((3, 3, 2)), dma((3, 3, 2)),
-        dma((3, 2, 2)), dma((3, 2, 2)),
-        dma((3 + heads, 3, 2, 3)), dma((3 + heads, 3, 2, 3)),
-        dma((3 + heads, 3, 3)), dma((3 + heads, 3, 3)),
-        dma((3 + heads,)), dma((3 + heads,)),
-        dma((3 + heads,)), dma((3 + heads,)),
-        dma((2, 2, 2, 3)), dma((2, 2, 2, 3)),
-        dma((4, 3)), dma((4, 3)),
-        dma((4, 3)), dma((4, 3)),
+        dma((5,)),
+        dma((3, 5)), dma((3, 2)), dma((3, 3, 2)), dma((3, 3, 2)), dma((3, 2)), dma((3, 2)),
+        dma((3 + heads, 6)), dma((3 + heads, 3, 3)), dma((3 + heads, 3)), dma((3 + heads,)), dma((3 + heads,)),
+        dma((2, 2, 3)),
+        dma((4,)), dma((4, 3)), dma((4,)), dma((4, 3)),
     ]
-    spec = pl.BlockSpec(memory_space=pltpu.VMEM)
+    whole = pl.BlockSpec(memory_space=pl.ANY)
     final, dx, grads = pl.pallas_call(
         functools.partial(kernel, dims),
         out_shape=(
@@ -757,8 +807,8 @@
             jax.ShapeDtypeStruct((count, width), F32),
             jax.ShapeDtypeStruct((3, rows, width), F32),
         ),
-        in_specs=[pl.BlockSpec(memory_space=pl.ANY)] * 7,
-        out_specs=(spec, spec, spec),
+        in_specs=[whole] * 7,
+        out_specs=(whole,) * 3,
         scratch_shapes=scratch,
         compiler_params=pltpu.CompilerParams(
             collective_id=0, has_side_effects=True, vmem_limit_bytes=67043328
@@ -777,8 +827,12 @@
             jax.ShapeDtypeStruct((1, rows, width), F32),
             jax.ShapeDtypeStruct((rows, width), F32),
         ),
-        in_specs=[spec] * 3,
-        out_specs=(spec,) * 6,
+        in_specs=[whole] * 3,
+        out_specs=(whole,) * 6,
+        scratch_shapes=[
+            vmem((count, width), BF), vmem((count, width), F32), vmem((3, rows, width), F32),
+            dma((5,)), dma((5 + 3 * heads,)),
+        ],
     )(final, dx, grads)
     return final, dx, qkv.transpose(1, 0, 2)[None], out.T[None], inner, back.T[None]
 

time: 167 us -> 159 us (0.952); the launches traced: 165 us -> 159 us
  Pallas kernels: 164 us -> 158 us
    pallas_call x1, Pallas kernels: 161 us -> 156 us  [step(): pl.pallas_call(functools.partial(kernel, dims), out_shape=(jax.ShapeDtype...]
where the time goes in v9:
time: 159 us
  Pallas kernels  158 us (99%)
    pallas_call x1, Pallas kernels, step(): pl.pallas_call(functools.partial(kernel, dims), out_shape=(jax.ShapeDtype...  156 us

profile of v9, /device:TPU:0, one launch (start us, length us, event | category | flops | bytes accessed | tf_op | source)
XLA Modules:
  0.0 159.1 jit_solution(806508977960454953)
XLA Ops:
  0.6 155.8 %shard_map.118 = (bf16[128,1536]{1,0:T(8,128)(2,1)}, f32[128,1536]{1,0:T(8,128)}, f32[3,48,1536]{2,1,0:T(8,128)}) custom-call(bf16[128,1536]{1,0:T(8,128)(2,1)} %bitcast.22, f32[6,1,1536]{2,1,0:T(1,128)} %bitcast.27, bf16[3,48,384]{2,1,0:T(8,128)(2,1)} %bitcast.26, bf16[48,384]{1,0:T(8,128)(2,1)} %bitcast.28, bf16[48,1536]{1,0:T(8,128)(2,1)} %bitcast.24, ...), custom_call_target="tpu_custom_call" | custom-call | tf_op jit(solution)/shard_map/pallas_call | solution.py:803
  156.4 2.6 %shard_map.119 = (bf16[1,128,1536]{2,1,0:T(8,128)(2,1)}, f32[1,128,1536]{2,1,0:T(8,128)}, f32[3,48,384]{2,1,0:T(8,128)}, f32[48,384]{1,0:T(8,128)}, f32[1,48,1536]{2,1,0:T(8,128)}, /*index=5*/f32[48,1536]{1,0:T(8,128)}) custom-call(bf16[128,1536]{1,0:T(8,128)(2,1)} %get-tuple-element.15.fin, f32[128,1536]{1,0:T(8,128)} %get-tuple-element.16.dx, ...), custom_call_target="tpu_custom_call" | custom-call | tf_op jit(solution)/shard_map/pallas_call | solution.py:820

commit v10 on v9

--- a/solution.py
+++ b/solution.py
@@ -523,7 +523,6 @@
     for s in (0, 1):
         ag_mid_start(s, 0, (2,))
         ag_mid_start(s, 0)
-    ag_mid_start(2, 0)
     gather_start(0, A1)
     ag_last_start(0, (2,))
     ag_mid_start(0, 1)
@@ -537,6 +536,7 @@
     gather_relay(0, A1)
     gather_start(1, DM)
     ag_relay_start(0)
+    ag_mid_start(2, 0)
     ag_mid_start(2, 1)
     ag_last_start(1)
     ag_final_start(1)
@@ -582,12 +582,13 @@
     tile = 256
 
     def hidden(i):
-        @pl.loop(0, width // tile)
+        @pl.loop(0, width // (2 * tile))
         def _(t):
-            at = pl.ds(pl.multiple_of(t * tile, 128), tile)
-            g, d = gelu_pair(dot(two(A2, i), W[1, :, :, :, at].reshape(width, tile)))
-            GG[i, :, :, at] = bf(g).reshape(2, pair // 2, tile)
-            DU[i, :, :, at] = bf(d).reshape(2, pair // 2, tile)
+            for j in (0, 1):
+                at = pl.ds(pl.multiple_of((2 * t + j) * tile, 128), tile)
+                g, d = gelu_pair(dot(two(A2, i), W[1, :, :, :, at].reshape(width, tile)))
+                GG[i, :, :, at] = bf(g).reshape(2, pair // 2, tile)
+                DU[i, :, :, at] = bf(d).reshape(2, pair // 2, tile)
 
     gather_relay(1, DM)
     gather_wait(1, DM, 0)
@@ -664,44 +665,45 @@
     qkv_back = back_product(lambda i: DQKV[pair_rows(i), :], 0, 0, 3 * own)
     fin[...] = bf(MID[...] + m[5] * scatter_result(2))
     results[0].start()
-    scatter_far(3, qkv_back)
     rs_hop_combine(0)
-    rs_second(2)
     rs_combine(2)
     rs_mid_start(1)
+    rs_combine(3)
+    qkv_back = back_product(lambda i: DQKV[pair_rows(i), :], 0, 0, 3 * own)
+    scatter_far(3, qkv_back)
+    rs_second(2)
+    rs_combine(4)
     scatter_near(3, qkv_back)
-    rs_combine(3)
     rs_second(3)
     rs_mid_start(0, (2,))
-    rs_combine(4)
+    rs_pair_start(0)
+    rs_combine(5)
+    rs_mid_start(2)
     rs_combine(2, (2,))
     rs_second(4)
-    rs_combine(5)
-    rs_mid_start(2)
-    rs_pair_start(0)
+    rs_mid_start(3)
+    rs_combine(3, (2,))
+    rs_hop_combine(1)
+    rs_mid_start(4)
+    rs_mid_start(2, (2,))
     rs_second(5)
-    rs_hop_combine(1)
-    rs_combine(3, (2,))
-    rs_mid_start(3)
+    rs_combine(4, (2,))
+    rs_mid_start(3, (2,))
+    rs_mid_start(5)
+    rs_pair_start(2)
+    rs_pair_start(1)
     rs_finish_third(0)
-    rs_mid_start(2, (2,))
-    rs_combine(4, (2,))
-    rs_mid_start(4)
-    rs_mid_start(3, (2,))
+    rs_combine(5, (2,))
+    rs_mid_start(4, (2,))
+    rs_pair_start(3)
+    rs_finish(0)
+    results[4].start()
     e1 = scatter_result(3) * (1.0 + m[1])
     n1, r1 = normalize(f32(tok[...]))
     dxin[...] = DX[...] + norm_back(n1, r1, e1)
     results[1].start()
-    rs_pair_start(1)
-    rs_combine(5, (2,))
-    rs_mid_start(5)
-    rs_finish(0)
-    results[4].start()
-    rs_pair_start(2)
-    rs_mid_start(4, (2,))
-    rs_pair_start(3)
+    rs_pair_start(4)
     rs_mid_start(5, (2,))
-    rs_pair_start(4)
     rs_pair_start(5)
     rs_finish(1)
     results[3].start()

time: 159 us -> 158 us (level)
    pallas_call x1, Pallas kernels: 156 us -> 154 us  [step(): pl.pallas_call(functools.partial(kernel, dims), out_shape=(jax.ShapeDtype...]
where the time goes in v10:
time: 158 us; the launch traced here: 157 us
  Pallas kernels  157 us (99%)
    pallas_call x1, Pallas kernels, step(): pl.pallas_call(functools.partial(kernel, dims), out_shape=(jax.ShapeDtype...  154 us

profile of v10, /device:TPU:0, one launch (start us, length us, event | category | flops | bytes accessed | tf_op | source)
XLA Modules:
  0.0 157.5 jit_solution(13802708115636636929)
XLA Ops:
  0.6 154.1 %shard_map.118 = (bf16[128,1536]{1,0:T(8,128)(2,1)}, f32[128,1536]{1,0:T(8,128)}, f32[3,48,1536]{2,1,0:T(8,128)}) custom-call(bf16[128,1536]{1,0:T(8,128)(2,1)} %bitcast.22, f32[6,1,1536]{2,1,0:T(1,128)} %bitcast.27, bf16[3,48,384]{2,1,0:T(8,128)(2,1)} %bitcast.26, bf16[48,384]{1,0:T(8,128)(2,1)} %bitcast.28, bf16[48,1536]{1,0:T(8,128)(2,1)} %bitcast.24, ...), custom_call_target="tpu_custom_call" | custom-call | tf_op jit(solution)/shard_map/pallas_call | solution.py:805
  154.7 2.6 %shard_map.119 = (bf16[1,128,1536]{2,1,0:T(8,128)(2,1)}, f32[1,128,1536]{2,1,0:T(8,128)}, f32[3,48,384]{2,1,0:T(8,128)}, f32[48,384]{1,0:T(8,128)}, f32[1,48,1536]{2,1,0:T(8,128)}, /*index=5*/f32[48,1536]{1,0:T(8,128)}) custom-call(bf16[128,1536]{1,0:T(8,128)(2,1)} %get-tuple-element.15.fin, f32[128,1536]{1,0:T(8,128)} %get-tuple-element.16.dx, ...), custom_call_target="tpu_custom_call" | custom-call | tf_op jit(solution)/shard_map/pallas_call | solution.py:822

commit v11 on v10

--- a/solution.py
+++ b/solution.py
@@ -90,12 +90,12 @@
 
     def drain(sem, moves):
         units = sum(math.prod(move.src.shape) for move in moves) // (rows * 128)
-        for height in (rows, nh * rows):
+        for q, height in ((1, rows), (1, nh * rows), (3, nh * rows)):
             for i in range(1, nz + 1):
                 for j in range(1, ny + 1):
-                    n, rest = divmod(units * rows, height * i * j)
+                    n, rest = divmod(units * rows, q * height * i * j)
                     if rest == 0 and n <= width // 128:
-                        view = W.at[0, pl.ds(0, i), pl.ds(0, j), pl.ds(0, height), pl.ds(0, n * 128)]
+                        view = W.at[pl.ds(0, q), pl.ds(0, i), pl.ds(0, j), pl.ds(0, height), pl.ds(0, n * 128)]
                         pltpu.make_async_copy(view, view, sem).wait()
                         return
         raise ValueError(units)
@@ -166,7 +166,7 @@
         k, line = 1 - 2 * d, line_of(s, color)
         part = halves[d if j == 0 else 1 - d]
         piece = slab_at(W.at[s], line, -k if recv else 0, ag_cols[s][color], part, row_of(color))
-        arrived = a3r.at[s, color, d] if j == 0 else a4r.at[s, color // 2]
+        arrived = a3r.at[s, color] if j == 0 else a4r.at[s, color // 2]
         return copy(piece, piece, ags.at[s, 3 + color // 2], arrived, last(line, k))
 
     def ag_relay(s, color, d, recv):
@@ -201,8 +201,8 @@
 
     def ag_relay_start(s, colors=(0, 1)):
         for color in colors:
+            drain(a3r.at[s, color], [ag_last(s, color, d, 0, True) for d in (0, 1)])
             for d in (0, 1):
-                ag_last(s, color, d, 0, True).wait_recv()
                 ag_relay(s, color, d, False).start()
 
     def late(s, colors):
@@ -273,21 +273,21 @@
 
     def rs_first(s):
         src = parts[s].at[:, :, at_rows(1 - h), grad_cols[s][2]]
-        return copy(src, r4_at(s), rss.at[s, 5], r4r.at[s], pair_peer)
+        return copy(src, r4_at(s), rss.at[1], r4r.at[s], pair_peer)
 
     def rs_ring(s, color, d, kind):
         k, line = 1 - 2 * d, rs_line(s, color)
         part = halves[1 - d if kind == 1 else d]
         src = slab_at(parts[s], line, 2 if kind == 0 else k, grad_cols[s][color], part, row_of(color))
         dst = r1_at(s, color).at[2 if kind == 0 else d, part]
-        arrived = r1r.at[s, color, d if kind == 0 else 2]
-        return copy(src, dst, rss.at[s, color // 2], arrived, last(line, k))
+        arrived = r1r.at[s, color, min(kind, 1)]
+        return copy(src, dst, rss.at[0], arrived, last(line, k))
 
     def rs_mid(s, color, k):
         line = rs_line(s, color)
         return copy(
             line_at(parts[s], line, k, grad_cols[s][color], row_of(color)), r2_at(s, color).at[k - 1],
-            rss.at[s, 2 + color // 2], r2r.at[s, color], mid_dev(line, k),
+            rss.at[1], r2r.at[s, color], mid_dev(line, k),
         )
 
     def ringed(s, color):
@@ -299,7 +299,7 @@
         src = line_at(parts[s], color, 2 if kind == 0 else k, grad_cols[s][color], row)
         dst = r2_at(s, color).at[2 if kind == 0 else d, row]
         arrived = r5r.at[s, color, d if kind == 0 else 2]
-        return copy(src, dst, rss.at[s, 2], arrived, mid_dev(color, k))
+        return copy(src, dst, rss.at[1], arrived, mid_dev(color, k))
 
     def rs_hop_combine(s):
         for color in (0, 1):
@@ -314,7 +314,7 @@
     def rs_pair(s):
         return copy(
             parts[s].at[z, y, at_rows(1 - h), pair_cols[s]], R3.at[slots[s], :, pair_cols[s]],
-            rss.at[s, 4], r3r.at[s], pair_peer,
+            rss.at[1], r3r.at[s], pair_peer,
         )
 
     def rs_second(s):
@@ -336,8 +336,8 @@
     def rs_combine(s, colors=(0, 1)):
         for color in colors:
             line = rs_line(s, color)
+            drain(r1r.at[s, color, 0], [rs_ring(s, color, d, 0) for d in (0, 1)])
             for d in (0, 1):
-                rs_ring(s, color, d, 0).wait_recv()
                 k = 1 - 2 * d
 
                 @pl.loop(2 * d, 2 * d + 2)
@@ -351,7 +351,7 @@
     def rs_mid_start(s, colors=(0, 1)):
         for color in colors:
             line = rs_line(s, color)
-            drain(r1r.at[s, color, 2], [rs_ring(s, color, d, kind) for d in (0, 1) for kind in (1, 2)])
+            drain(r1r.at[s, color, 1], [rs_ring(s, color, d, kind) for d in (0, 1) for kind in (1, 2)])
 
             @pl.loop(0, 4)
             def _(i):
@@ -393,18 +393,18 @@
     def rs_finish_third(s):
         grads[slots[s], :, grad_cols[s][2]] = rs_total(s, 2)
 
-    def rs_sent(s):
-        for colors in ((0, 1),) if s == 1 else ((0, 1), (2,)):
-            rings = [rs_ring(s, color, d, kind) for color in colors for d in (0, 1) for kind in (0, 1, 2)]
-            drain(rss.at[s, colors[0] // 2], rings)
-            if ringed(s, colors[0]):
-                middle = [rs_hop(s, color, d, kind) for color in colors for d in (0, 1) for kind in (0, 1, 2)]
-            else:
-                middle = [rs_mid(s, color, k) for color in colors for k in (1, 2, 3)]
-            drain(rss.at[s, 2 + colors[0] // 2], middle)
-        if s != 1:
-            rs_first(s).wait_send()
-        rs_pair(s).wait_send()
+    def rs_sent():
+        rings, others = [], []
+        for s in range(sections):
+            for color in (0, 1) if s == 1 else (0, 1, 2):
+                rings += [rs_ring(s, color, d, kind) for d in (0, 1) for kind in (0, 1, 2)]
+                if ringed(s, color):
+                    others += [rs_hop(s, color, d, kind) for d in (0, 1) for kind in (0, 1, 2)]
+                else:
+                    others += [rs_mid(s, color, k) for k in (1, 2, 3)]
+            others += [rs_pair(s)] if s == 1 else [rs_pair(s), rs_first(s)]
+        drain(rss.at[0], rings)
+        drain(rss.at[1], others)
 
     def g_copy(i, buf, step, recv):
         if step == 0:
@@ -507,22 +507,24 @@
     moves += [(wo_in, W.at[0, z, y, mine, pl.ds(3 * own, own)])]
     moves += [(wi_in, W.at[1, z, y, mine]), (wb_in, W.at[2, z, y, mine])]
     moves += [(tok_in, tok), (og_in, og), (mod_in, mod)]
-    loads = [pltpu.make_async_copy(src, dst, in_sem.at[i]) for i, (src, dst) in enumerate(moves)]
+    count = len(moves) - 3
+    loads = [pltpu.make_async_copy(src, dst, in_sem.at[max(i - count + 1, 0)]) for i, (src, dst) in enumerate(moves)]
     for load in loads:
         load.start()
-    for load in loads:
+    drain(in_sem.at[0], [copy(src, dst, None, None, None) for src, dst in moves[:count]])
+    pl.semaphore_wait(barrier, len(peers))
+
+    for s in range(3):
+        ag_pair(s, False).start()
+    for s in (0, 1):
+        ag_mid_start(s, 0, (2,))
+        ag_mid_start(s, 0)
+    for load in loads[count:]:
         load.wait()
     m = [mod[i] for i in range(6)]
     n1, r1 = normalize(f32(tok[...]))
     A1[l, c] = bf(n1 * (1.0 + m[1]) + m[0])
     DM[l, c] = bf(m[5] * f32(og[...]))
-    pl.semaphore_wait(barrier, len(peers))
-
-    for s in range(3):
-        ag_pair(s, False).start()
-    for s in (0, 1):
-        ag_mid_start(s, 0, (2,))
-        ag_mid_start(s, 0)
     gather_start(0, A1)
     ag_last_start(0, (2,))
     ag_mid_start(0, 1)
@@ -618,9 +620,9 @@
 
     in_back = back_product(lambda i: two(DU, i), 1, 0, width)
     scatter_far(1, in_back)
+    rs_combine(0)
     turn(A2)
     grad_turned(1, lambda at: all_rows(DU, at), 0, half, tile)
-    rs_combine(0)
     rs_second(0)
     rs_start(1, (0,))
     grad_turned(1, lambda at: all_rows(DU, at), half, width, tile)
@@ -635,10 +637,10 @@
 
     ff_back = back_product(lambda i: two(GG, i), 2, 0, width)
     scatter_far(2, ff_back)
+    rs_combine(0, (2,))
+    rs_combine(1)
     scatter_near(2, ff_back)
     turn(A1)
-    rs_combine(0, (2,))
-    rs_combine(1)
     rs_mid_start(0)
     gather_relay(3, DA)
     gather_wait(3, DA, 0)
@@ -678,22 +680,22 @@
     rs_mid_start(0, (2,))
     rs_pair_start(0)
     rs_combine(5)
+    rs_second(4)
     rs_mid_start(2)
     rs_combine(2, (2,))
-    rs_second(4)
+    rs_hop_combine(1)
+    rs_second(5)
+    rs_combine(3, (2,))
     rs_mid_start(3)
-    rs_combine(3, (2,))
-    rs_hop_combine(1)
+    rs_combine(4, (2,))
     rs_mid_start(4)
     rs_mid_start(2, (2,))
-    rs_second(5)
-    rs_combine(4, (2,))
     rs_mid_start(3, (2,))
     rs_mid_start(5)
+    rs_combine(5, (2,))
     rs_pair_start(2)
     rs_pair_start(1)
     rs_finish_third(0)
-    rs_combine(5, (2,))
     rs_mid_start(4, (2,))
     rs_pair_start(3)
     rs_finish(0)
@@ -712,8 +714,7 @@
     for s in range(2, sections):
         rs_finish(s)
     results[2].start()
-    for s in range(sections):
-        rs_sent(s)
+    rs_sent()
     ag_sent(0)
     ag_sent(2)
     for i, buf in enumerate((A1, DM, A2, DA)):
@@ -794,10 +795,10 @@
         vmem((count, width), BF),
         vmem((count, width), F32),
         vmem((3, rows, width), F32),
-        dma((6 + 3 * heads,)),
+        dma((4,)),
         dma((5,)),
-        dma((3, 5)), dma((3, 2)), dma((3, 3, 2)), dma((3, 3, 2)), dma((3, 2)), dma((3, 2)),
-        dma((3 + heads, 6)), dma((3 + heads, 3, 3)), dma((3 + heads, 3)), dma((3 + heads,)), dma((3 + heads,)),
+        dma((3, 5)), dma((3, 2)), dma((3, 3, 2)), dma((3, 3)), dma((3, 2)), dma((3, 2)),
+        dma((2,)), dma((3 + heads, 3, 2)), dma((3 + heads, 3)), dma((3 + heads,)), dma((3 + heads,)),
         dma((2, 2, 3)),
         dma((4,)), dma((4, 3)), dma((4,)), dma((4, 3)),
     ]

time: 158 us -> 157 us (level)
  no operation moved by 1% of the time
where the time goes in v11:
time: 157 us
  Pallas kernels  156 us (99%)
    pallas_call x1, Pallas kernels, step(): pl.pallas_call(functools.partial(kernel, dims), out_shape=(jax.ShapeDtype...  153 us

profile of v11, /device:TPU:0, one launch (start us, length us, event | category | flops | bytes accessed | tf_op | source)
XLA Modules:
  0.0 156.8 jit_solution(6742758922381344696)
XLA Ops:
  0.6 153.4 %shard_map.118 = (bf16[128,1536]{1,0:T(8,128)(2,1)}, f32[128,1536]{1,0:T(8,128)}, f32[3,48,1536]{2,1,0:T(8,128)}) custom-call(bf16[128,1536]{1,0:T(8,128)(2,1)} %bitcast.22, f32[6,1,1536]{2,1,0:T(1,128)} %bitcast.27, bf16[3,48,384]{2,1,0:T(8,128)(2,1)} %bitcast.26, bf16[48,384]{1,0:T(8,128)(2,1)} %bitcast.28, bf16[48,1536]{1,0:T(8,128)(2,1)} %bitcast.24, ...), custom_call_target="tpu_custom_call" | custom-call | tf_op jit(solution)/shard_map/pallas_call | solution.py:806
  154.1 2.6 %shard_map.119 = (bf16[1,128,1536]{2,1,0:T(8,128)(2,1)}, f32[1,128,1536]{2,1,0:T(8,128)}, f32[3,48,384]{2,1,0:T(8,128)}, f32[48,384]{1,0:T(8,128)}, f32[1,48,1536]{2,1,0:T(8,128)}, /*index=5*/f32[48,1536]{1,0:T(8,128)}) custom-call(bf16[128,1536]{1,0:T(8,128)(2,1)} %get-tuple-element.15.fin, f32[128,1536]{1,0:T(8,128)} %get-tuple-element.16.dx, ...), custom_call_target="tpu_custom_call" | custom-call | tf_op jit(solution)/shard_map/pallas_call | solution.py:823

commit v12 on v11

--- a/solution.py
+++ b/solution.py
@@ -253,7 +253,7 @@
     spare = {2: (1, 4), 3: (1, 5), 4: (0, 4), 5: (0, 5)}
 
     def rs_line(s, color):
-        return color if color < 2 else (0, None, 1, 1, 0, 1)[s]
+        return color if color < 2 else (0, None, 0, 1, 0, 1)[s]
 
     def spare_at(s):
         return pl.ds(spare[s][1] * third, third)

time: 157 us -> 156 us (level)
  no operation moved by 1% of the time
where the time goes in v12:
time: 156 us; the launch traced here: 155 us
  Pallas kernels  155 us (99%)
    pallas_call x1, Pallas kernels, step(): pl.pallas_call(functools.partial(kernel, dims), out_shape=(jax.ShapeDtype...  152 us

profile of v12, /device:TPU:0, one launch (start us, length us, event | category | flops | bytes accessed | tf_op | source)
XLA Modules:
  0.0 155.5 jit_solution(17018100087290097715)
XLA Ops:
  0.6 152.1 %shard_map.118 = (bf16[128,1536]{1,0:T(8,128)(2,1)}, f32[128,1536]{1,0:T(8,128)}, f32[3,48,1536]{2,1,0:T(8,128)}) custom-call(bf16[128,1536]{1,0:T(8,128)(2,1)} %bitcast.22, f32[6,1,1536]{2,1,0:T(1,128)} %bitcast.27, bf16[3,48,384]{2,1,0:T(8,128)(2,1)} %bitcast.26, bf16[48,384]{1,0:T(8,128)(2,1)} %bitcast.28, bf16[48,1536]{1,0:T(8,128)(2,1)} %bitcast.24, ...), custom_call_target="tpu_custom_call" | custom-call | tf_op jit(solution)/shard_map/pallas_call | solution.py:806
  152.7 2.6 %shard_map.119 = (bf16[1,128,1536]{2,1,0:T(8,128)(2,1)}, f32[1,128,1536]{2,1,0:T(8,128)}, f32[3,48,384]{2,1,0:T(8,128)}, f32[48,384]{1,0:T(8,128)}, f32[1,48,1536]{2,1,0:T(8,128)}, /*index=5*/f32[48,1536]{1,0:T(8,128)}) custom-call(bf16[128,1536]{1,0:T(8,128)(2,1)} %get-tuple-element.15.fin, f32[128,1536]{1,0:T(8,128)} %get-tuple-element.16.dx, ...), custom_call_target="tpu_custom_call" | custom-call | tf_op jit(solution)/shard_map/pallas_call | solution.py:823

commit v13 on v12

--- a/solution.py
+++ b/solution.py
@@ -672,8 +672,8 @@
     rs_mid_start(1)
     rs_combine(3)
     qkv_back = back_product(lambda i: DQKV[pair_rows(i), :], 0, 0, 3 * own)
+    rs_second(2)
     scatter_far(3, qkv_back)
-    rs_second(2)
     rs_combine(4)
     scatter_near(3, qkv_back)
     rs_second(3)

time: 156 us -> 156 us (level)
  no operation moved by 1% of the time
where the time goes in v13:
time: 156 us; the launch traced here: 155 us
  Pallas kernels  155 us (99%)
    pallas_call x1, Pallas kernels, step(): pl.pallas_call(functools.partial(kernel, dims), out_shape=(jax.ShapeDtype...  152 us

profile of v13, /device:TPU:0, one launch (start us, length us, event | category | flops | bytes accessed | tf_op | source)
XLA Modules:
  0.0 155.5 jit_solution(9791120781148401593)
XLA Ops:
  0.6 152.1 %shard_map.118 = (bf16[128,1536]{1,0:T(8,128)(2,1)}, f32[128,1536]{1,0:T(8,128)}, f32[3,48,1536]{2,1,0:T(8,128)}) custom-call(bf16[128,1536]{1,0:T(8,128)(2,1)} %bitcast.22, f32[6,1,1536]{2,1,0:T(1,128)} %bitcast.27, bf16[3,48,384]{2,1,0:T(8,128)(2,1)} %bitcast.26, bf16[48,384]{1,0:T(8,128)(2,1)} %bitcast.28, bf16[48,1536]{1,0:T(8,128)(2,1)} %bitcast.24, ...), custom_call_target="tpu_custom_call" | custom-call | tf_op jit(solution)/shard_map/pallas_call | solution.py:806
  152.7 2.6 %shard_map.119 = (bf16[1,128,1536]{2,1,0:T(8,128)(2,1)}, f32[1,128,1536]{2,1,0:T(8,128)}, f32[3,48,384]{2,1,0:T(8,128)}, f32[48,384]{1,0:T(8,128)}, f32[1,48,1536]{2,1,0:T(8,128)}, /*index=5*/f32[48,1536]{1,0:T(8,128)}) custom-call(bf16[128,1536]{1,0:T(8,128)(2,1)} %get-tuple-element.15.fin, f32[128,1536]{1,0:T(8,128)} %get-tuple-element.16.dx, ...), custom_call_target="tpu_custom_call" | custom-call | tf_op jit(solution)/shard_map/pallas_call | solution.py:823

commit v14 on v13

--- a/solution.py
+++ b/solution.py
@@ -675,8 +675,8 @@
     rs_second(2)
     scatter_far(3, qkv_back)
     rs_combine(4)
+    rs_second(3)
     scatter_near(3, qkv_back)
-    rs_second(3)
     rs_mid_start(0, (2,))
     rs_pair_start(0)
     rs_combine(5)

time: 156 us -> 156 us (level)
  no operation moved by 1% of the time
where the time goes in v14:
time: 156 us; the launch traced here: 155 us
  Pallas kernels  155 us (99%)
    pallas_call x1, Pallas kernels, step(): pl.pallas_call(functools.partial(kernel, dims), out_shape=(jax.ShapeDtype...  152 us

profile of v14, /device:TPU:0, one launch (start us, length us, event | category | flops | bytes accessed | tf_op | source)
XLA Modules:
  0.0 155.5 jit_solution(5784728746365929658)
XLA Ops:
  0.6 152.1 %shard_map.118 = (bf16[128,1536]{1,0:T(8,128)(2,1)}, f32[128,1536]{1,0:T(8,128)}, f32[3,48,1536]{2,1,0:T(8,128)}) custom-call(bf16[128,1536]{1,0:T(8,128)(2,1)} %bitcast.22, f32[6,1,1536]{2,1,0:T(1,128)} %bitcast.27, bf16[3,48,384]{2,1,0:T(8,128)(2,1)} %bitcast.26, bf16[48,384]{1,0:T(8,128)(2,1)} %bitcast.28, bf16[48,1536]{1,0:T(8,128)(2,1)} %bitcast.24, ...), custom_call_target="tpu_custom_call" | custom-call | tf_op jit(solution)/shard_map/pallas_call | solution.py:806
  152.7 2.6 %shard_map.119 = (bf16[1,128,1536]{2,1,0:T(8,128)(2,1)}, f32[1,128,1536]{2,1,0:T(8,128)}, f32[3,48,384]{2,1,0:T(8,128)}, f32[48,384]{1,0:T(8,128)}, f32[1,48,1536]{2,1,0:T(8,128)}, /*index=5*/f32[48,1536]{1,0:T(8,128)}) custom-call(bf16[128,1536]{1,0:T(8,128)(2,1)} %get-tuple-element.15.fin, f32[128,1536]{1,0:T(8,128)} %get-tuple-element.16.dx, ...), custom_call_target="tpu_custom_call" | custom-call | tf_op jit(solution)/shard_map/pallas_call | solution.py:823
